TPU v7x, 128 devices: a whole 4x4x4 slice. The times are simulated.
128 devices in a mesh: span: 32 (over y, x, core), head: 4 (over z).
Axes of the slice: x: 4, y: 4, z: 4, core: 2. Of those that a mesh axis runs over, the one named last changes fastest.
Arguments:
- neighbour_query: bfloat16 [32768, 4096], P('span', 'head'), may hold values from -12 to 12
- neighbour_key: bfloat16 [32768, 4096], P('span', 'head'), may hold values from -6 to 6
- neighbour_value: bfloat16 [32768, 4096], P('span', 'head'), may hold values from -12.2 to 12.2
- segment_key: bfloat16 [8192, 4096], P('span', 'head'), may hold values from -30 to 30
- segment_value: bfloat16 [8192, 4096], P('span', 'head'), may hold values from -6 to 6
- decoder_query: bfloat16 [8192, 4096], P('span', 'head'), may hold values from -24 to 24
- sources: int32 [128, 2], P('span'), may hold values from 0 to 127, as said below
Outputs:
- blended: bfloat16 [8192, 4096], P('span', 'head')
Inputs may be any that keep to these rules, and one draw needn't show every extreme that they name: `sources`: the segments of index o of span are o * 4 to (o + 1) * 4 - 1. Among the 8 entries of the segments of one index of span, at most 2 name segments of one index of span, and in every such block some index is named exactly 2 times.
All inputs are finite; a program needn't handle non-finite values.
Results may differ from a plain program's by a relative error of at most 0.035.
Values may be sent and summed in bfloat16 or wider, within the bound.
No kernel may reach another device: no remote copies, remote signals or barrier semaphores. Data moves between devices by JAX's collectives and lax.ppermute only.
A program may use at most 192 MiB of HBM per device.

v0:
```python
import jax
import jax.numpy as jnp
from jax import lax
from jax.sharding import PartitionSpec as P

HEAD_DIM = 128
SEG_LEN = 64
NBR_LEN = 128
NEIGHBOURS = 2
SEG_DEV = 4


epsilon = 1e-06


def from_behind(x, axis, by):
    count = lax.axis_size(axis)
    pairs = [(i, i + by) for i in range(count) if 0 <= i + by < count]
    return lax.ppermute(x, axis, pairs)


def attend(query_rows, key_rows, value_rows):
    groups, length, columns = query_rows.shape
    head_count = columns // HEAD_DIM
    query_heads = query_rows.reshape(groups, length, head_count, HEAD_DIM)
    key_heads = key_rows.reshape(groups, key_rows.shape[1], head_count, HEAD_DIM)
    value_heads = value_rows.reshape(groups, value_rows.shape[1], head_count, HEAD_DIM)
    logit_scores = jnp.einsum(
        "bqhd,bkhd->bhqk", query_heads, key_heads, preferred_element_type=jnp.float32
    ) * HEAD_DIM ** (-0.5)
    logit_scores = logit_scores - jnp.max(logit_scores, axis=-1, keepdims=True)
    weights = jnp.exp(logit_scores)
    weights = (weights / jnp.sum(weights, axis=-1, keepdims=True)).astype(jnp.bfloat16)
    output = jnp.einsum("bhqk,bkhd->bqhd", weights, value_heads, preferred_element_type=jnp.float32)
    return output.reshape(groups, length, columns)


def squares(rows):
    wide = rows.astype(jnp.float32)
    return jnp.sum(wide * wide, axis=-1)


def normalize(rows, totals, full_width):
    scale = lax.rsqrt(totals / full_width + epsilon)
    return (rows.astype(jnp.float32) * scale[:, None]).astype(jnp.bfloat16)


def body(
    neighbour_query,
    neighbour_key,
    neighbour_value,
    segment_key,
    segment_value,
    decoder_query,
    sources,
):
    columns = neighbour_query.shape[1]
    full_width = columns * lax.axis_size("head")
    devices = lax.axis_size("span")
    per_device = SEG_DEV * NEIGHBOURS
    capacity = max(2, 2 * per_device // devices)
    panel_rows = NEIGHBOURS * NBR_LEN
    self_out = attend(
        neighbour_query.reshape(per_device, NBR_LEN, columns),
        neighbour_key.reshape(per_device, NBR_LEN, columns),
        neighbour_value.reshape(per_device, NBR_LEN, columns),
    ).astype(jnp.bfloat16)
    flat_self = self_out.reshape(per_device * NBR_LEN, columns)
    totals = lax.psum(squares(flat_self), "head")
    cross_query = normalize(flat_self, totals, full_width).reshape(per_device, NBR_LEN, columns)
    listed = sources.reshape(per_device)
    owners = listed // SEG_DEV
    within = listed % SEG_DEV
    position = jnp.arange(per_device)
    earlier = (owners[:, None] == owners[None, :]) & (position[:, None] > position[None, :])
    ranked = jnp.sum(earlier.astype(jnp.int32), axis=1)
    slots = owners * capacity + ranked
    picked = (slots[:, None] == jnp.arange(devices * capacity)[None, :]).astype(jnp.int32)
    request = jnp.sum(picked * (within + 1)[:, None], axis=0).reshape(devices, capacity)
    asked = lax.all_to_all(request, "span", split_axis=0, concat_axis=0, tiled=True)
    wanted = jnp.maximum(asked - 1, 0).reshape(devices * capacity)
    own_keys = segment_key.reshape(SEG_DEV, SEG_LEN, columns)[wanted]
    own_values = segment_value.reshape(SEG_DEV, SEG_LEN, columns)[wanted]
    got_keys, got_values = (
        lax.all_to_all(
            own_keys.reshape(devices, capacity, SEG_LEN, columns),
            "span",
            split_axis=0,
            concat_axis=0,
            tiled=True,
        ),
        lax.all_to_all(
            own_values.reshape(devices, capacity, SEG_LEN, columns),
            "span",
            split_axis=0,
            concat_axis=0,
            tiled=True,
        ),
    )
    source_keys = got_keys.reshape(devices * capacity, SEG_LEN, columns)[slots]
    source_values = got_values.reshape(devices * capacity, SEG_LEN, columns)[slots]
    crossed = attend(cross_query, source_keys, source_values).astype(jnp.bfloat16)
    encoded = (self_out.astype(jnp.float32) + crossed.astype(jnp.float32)).astype(jnp.bfloat16)
    encoded = encoded.reshape(per_device * NBR_LEN, columns)
    before_values = from_behind(encoded[-panel_rows:], "span", 1)
    used_values = jnp.concatenate([before_values, encoded[:-panel_rows]], axis=0)
    used_totals = lax.psum(squares(used_values), "head")
    used_keys = normalize(used_values, used_totals, full_width)
    blended = attend(
        decoder_query.reshape(SEG_DEV, SEG_LEN, columns),
        used_keys.reshape(SEG_DEV, panel_rows, columns),
        used_values.reshape(SEG_DEV, panel_rows, columns),
    ).astype(jnp.bfloat16)
    return blended.reshape(SEG_DEV * SEG_LEN, columns)


def solution(mesh):
    placed = (
        P("span", "head"),
        P("span", "head"),
        P("span", "head"),
        P("span", "head"),
        P("span", "head"),
        P("span", "head"),
        P("span", None),
    )
    return jax.shard_map(
        body, mesh=mesh, in_specs=placed, out_specs=P("span", "head"), check_vma=False
    )
```

profile of v0, /device:TPU:0, one launch (start us, length us, event | category | flops | bytes accessed | tf_op | source)
XLA Modules:
  0.0 285.2 jit_solution(6147242872137211904)
XLA Ops:
  0.0 0.8 copy.51
  0.8 0.1 reshape.253
  0.9 0.2 convert_reduce_fusion
  1.1 0.1 select_reduce_fusion
  1.2 0.1 all_to_all.12
  1.3 14.6 %all_to_all.19 = s32[32,1,2]{2,1,0:T(1,128)S(1)} all-to-all(s32[32,1,2]{2,1,0:T(1,128)S(1)} %bitcast.112), channel_id=1, replica_groups=mesh['span'=32,'head'=4] {'span'}, dimensions={0} | all-to-all | bytes 512 | tf_op jit(solution)/shard_map/all_to_all | solution.py:80
  15.9 0.1 maximum_reduce_fusion
  16.0 0.1 reshape.264
  16.1 5.2 %gather_fusion.2 = bf16[64,64,1024]{2,1,0:T(8,128)(2,1)} fusion(bf16[4,64,1024]{2,1,0:T(8,128)(2,1)S(1)} %bitcast.93, s32[1024]{0:T(1024)S(1)} %pad_clamp_fusion.1), kind=kCustom, calls=%fused_computation.2 | custom fusion | bytes 16777472 | tf_op jit(solution)/shard_map/gather | solution.py:82
  21.4 5.1 %all-to-all-start.2 = ((bf16[32,2,64,1024]{3,2,1,0:T(8,128)(2,1)}), bf16[32,2,64,1024]{3,2,1,0:T(8,128)(2,1)}, u32[]{:S(2)}, u32[]{:S(2)}) async-start(bf16[32,2,64,1024]{3,2,1,0:T(8,128)(2,1)} %bitcast.96), calls=%async_computation.2 | async-start | bytes 16777216 | tf_op jit(solution)/shard_map/all_to_all | solution.py:85
  26.5 5.2 %gather_fusion = bf16[64,64,1024]{2,1,0:T(8,128)(2,1)} fusion(bf16[4,64,1024]{2,1,0:T(8,128)(2,1)S(1)} %bitcast.94, s32[1024]{0:T(1024)S(1)} %pad_clamp_fusion.1), kind=kCustom, calls=%fused_computation | custom fusion | bytes 16777472 | tf_op jit(solution)/shard_map/gather | solution.py:83
  31.7 100.6 %all-to-all-done.2 = bf16[32,2,64,1024]{3,2,1,0:T(8,128)(2,1)} async-done(((bf16[32,2,64,1024]{3,2,1,0:T(8,128)(2,1)}), bf16[32,2,64,1024]{3,2,1,0:T(8,128)(2,1)}, u32[]{:S(2)}, u32[]{:S(2)}) %all-to-all-start.2) | async-done | bytes 8388640 | tf_op jit(solution)/shard_map/all_to_all | solution.py:85
  132.3 5.1 %all-to-all-start.1 = ((bf16[32,2,64,1024]{3,2,1,0:T(8,128)(2,1)}), bf16[32,2,64,1024]{3,2,1,0:T(8,128)(2,1)}, u32[]{:S(2)}, u32[]{:S(2)}) async-start(bf16[32,2,64,1024]{3,2,1,0:T(8,128)(2,1)} %bitcast.95), calls=%async_computation.1 | async-start | bytes 16777216 | tf_op jit(solution)/shard_map/all_to_all | solution.py:92
  137.4 0.1 reshape.256
  137.5 0.6 copy.68
  138.2 1.0 copy-done.4
  139.1 0.6 copy.69
  139.8 1.0 copy-done.5
  140.7 0.6 copy.67
  141.3 1.6 fusion.21
  142.9 4.0 %fusion.69 = (f32[8,8,128]{2,1,0:T(8,128)S(1)}, f32[8,8,128,128]{2,3,1,0:T(8,128)S(1)}) fusion(f32[8,8,128,128]{2,3,1,0:T(8,128)S(1)} %fusion.21), kind=kOutput, calls=%fused_computation.91 | output fusion | flops 4194431 | bytes 8421376 | tf_op jit(solution)/shard_map/sub | solution.py:31
  146.9 2.6 fusion.5
  149.5 11.7 %psum.14 = f32[1024]{0:T(1024)S(1)} all-reduce(f32[1024]{0:T(1024)S(1)} %bitcast.113), channel_id=1, replica_groups=mesh['span'=32,'head'=4] {'head'}, use_global_device_ids=true, to_apply=%region_5.6 | all-reduce | flops 1024 | bytes 8192 | tf_op jit(solution)/shard_map/psum | solution.py:69
  161.3 4.0 %gather_fusion.3 = bf16[8,64,1024]{2,1,0:T(8,128)(2,1)S(1)} fusion(bf16[64,64,1024]{2,1,0:T(8,128)(2,1)} %bitcast.12, s32[1024]{0:T(1024)S(1)} %pad_clamp_fusion), kind=kCustom, calls=%fused_computation.3 | custom fusion | bytes 2097184 | tf_op jit(solution)/shard_map/gather | solution.py:100
  165.3 2.3 fusion.12
  167.6 1.3 copy-done.6
  168.9 0.6 fusion.70
  169.5 73.8 %all-to-all-done.1 = bf16[32,2,64,1024]{3,2,1,0:T(8,128)(2,1)} async-done(((bf16[32,2,64,1024]{3,2,1,0:T(8,128)(2,1)}), bf16[32,2,64,1024]{3,2,1,0:T(8,128)(2,1)}, u32[]{:S(2)}, u32[]{:S(2)}) %all-to-all-start.1) | async-done | bytes 8388640 | tf_op jit(solution)/shard_map/all_to_all | solution.py:92
  243.3 5.0 %gather_fusion.1 = bf16[8,64,1024]{2,1,0:T(8,128)(2,1)} fusion(bf16[64,64,1024]{2,1,0:T(8,128)(2,1)} %bitcast.4, s32[1024]{0:T(1024)S(1)} %pad_clamp_fusion), kind=kCustom, calls=%fused_computation.1 | custom fusion | bytes 2097184 | tf_op jit(solution)/shard_map/gather | solution.py:101
  248.3 3.9 %fusion.4 = bf16[8,128,8,128]{1,3,2,0:T(8,128)(2,1)S(1)} fusion(bf16[8,8,128,128]{2,3,1,0:T(8,128)(2,1)} %get-tuple-element.10, f32[8,8,128]{2,1,0:T(8,128)S(1)} %fusion.70, f32[8,8,128,64]{2,3,1,0:T(8,128)} %copy-done.6, bf16[8,64,1024]{2,1,0:T(8,128)(2,1)} %gather_fusion.1), kind=kOutput, calls=%fused_computation.11 | convolution fusion | flops 141566016 | bytes 7372800 | tf_op jit(solution)/shard_map/bhqk,bkhd->bqhd/dot_general | solution.py:34
  252.3 0.3 copy.57
  252.6 0.1 copy.107
  252.7 2.1 collective-permute-start
  254.8 1.1 copy.73
  255.9 1.3 slice.27
  257.2 2.0 copy.58
  259.2 1.1 constant_dynamic-update-slice_fusion
  260.3 0.4 bitcast_dynamic-update-slice_fusion
  260.7 0.5 multiply_reduce_fusion
  261.1 0.6 copy.72
  261.8 11.8 %psum.15 = f32[1024]{0:T(1024)S(1)} all-reduce(f32[1024]{0:T(1024)S(1)} %multiply_reduce_fusion), channel_id=1, replica_groups=mesh['span'=32,'head'=4] {'head'}, use_global_device_ids=true, to_apply=%region_9.10 | all-reduce | flops 1024 | bytes 8192 | tf_op jit(solution)/shard_map/psum | solution.py:107
  273.6 1.3 multiply_convert_fusion
  274.9 0.8 fusion.18
  275.8 1.3 copy-done.7
  277.1 0.8 fusion.71
  278.0 5.9 %fusion.37 = bf16[4,64,8,128]{3,1,2,0:T(8,128)(2,1)S(1)} fusion(bf16[4,256,8,128]{3,2,1,0:T(8,128)(2,1)S(1)} %bitcast.99, f32[4,8,64]{2,1,0:T(8,128)S(1)} %fusion.71, f32[4,8,256,64]{2,3,1,0:T(8,128)} %copy-done.7), kind=kOutput, calls=%fused_computation.47 | convolution fusion | flops 137103616 | bytes 4726784 | tf_op jit(solution)/shard_map/bhqk,bkhd->bqhd/dot_general | solution.py:34
  283.9 0.3 copy.62
  284.3 0.9 copy.106
  (22 shorter events, 0.1 us)
Async XLA Ops:
  0.0 16.1 %copy-start = (bf16[256,1024]{1,0:T(8,128)(2,1)S(1)}, bf16[256,1024]{1,0:T(8,128)(2,1)}, u32[]{:S(2)}) copy-start(bf16[256,1024]{1,0:T(8,128)(2,1)} %param.10) | copy-start | bytes 1572868
  21.4 5.1 %copy-start.2 = (bf16[256,1024]{1,0:T(8,128)(2,1)S(1)}, bf16[256,1024]{1,0:T(8,128)(2,1)}, u32[]{:S(2)}) copy-start(bf16[256,1024]{1,0:T(8,128)(2,1)} %param.11) | copy-start | bytes 1572868
  21.4 111.0 %all-to-all-start.2 = ((bf16[32,2,64,1024]{3,2,1,0:T(8,128)(2,1)}), bf16[32,2,64,1024]{3,2,1,0:T(8,128)(2,1)}, u32[]{:S(2)}, u32[]{:S(2)}) async-start(bf16[32,2,64,1024]{3,2,1,0:T(8,128)(2,1)} %bitcast.96), calls=%async_computation.2 | async-start | bytes 16777216 | tf_op jit(solution)/shard_map/all_to_all | solution.py:85
  132.3 5.2 %copy-start.3 = (bf16[1024,1024]{1,0:T(8,128)(2,1)S(1)}, bf16[1024,1024]{1,0:T(8,128)(2,1)}, u32[]{:S(2)}) copy-start(bf16[1024,1024]{1,0:T(8,128)(2,1)} %param.7) | copy-start | bytes 6291460
  132.3 111.0 %all-to-all-start.1 = ((bf16[32,2,64,1024]{3,2,1,0:T(8,128)(2,1)}), bf16[32,2,64,1024]{3,2,1,0:T(8,128)(2,1)}, u32[]{:S(2)}, u32[]{:S(2)}) async-start(bf16[32,2,64,1024]{3,2,1,0:T(8,128)(2,1)} %bitcast.95), calls=%async_computation.1 | async-start | bytes 16777216 | tf_op jit(solution)/shard_map/all_to_all | solution.py:92
  137.5 1.6 copy-start.4
  139.1 1.6 copy-start.5
  167.6 1.4 copy-start.6
  252.7 6.5 %collective-permute-start = (bf16[256,1024]{1,0:T(8,128)(2,1)S(1)}, bf16[256,1024]{1,0:T(8,128)(2,1)}, u32[]{:S(2)}, u32[]{:S(2)}) collective-permute-start(bf16[256,1024]{1,0:T(8,128)(2,1)S(1)} %bitcast.111), channel_id=1, source_target_pairs={{0,4},{4,8},{8,12},{12,16},{16,20},{20,24},{24,28},{28,32},{32,36}... | collective-permute-start | bytes 1572872 | tf_op jit(solution)/shard_map/ppermute | solution.py:19
  275.8 1.4 copy-start.7
  278.0 7.2 %copy-start.1 = (bf16[256,1024]{1,0:T(8,128)(2,1)S(1)}, bf16[256,1024]{1,0:T(8,128)(2,1)}, u32[]{:S(2)}) copy-start(bf16[256,1024]{1,0:T(8,128)(2,1)} %param.10) | copy-start | bytes 1572868
where the time goes:
time: 290 us; the launch traced here: 285 us
  waiting for transfers between devices  174 us (60%)
  blocking collectives  38.1 us (13%)
  local copies, waits for them, and re-layouts  35.3 us (12%)
  matrix products  17.1 us (6%)
  starting transfers between devices  12.3 us (4%)
  other arithmetic  7.62 us (3%)
    all_to_all x1, waiting for transfers between devices, body(): lax.all_to_all(own_keys.reshape(devices, capacity, SEG_LEN, columns), 'sp...  101 us
    all_to_all x1, waiting for transfers between devices, body(): lax.all_to_all(own_values.reshape(devices, capacity, SEG_LEN, columns), '...  73.8 us
    all_to_all x1, blocking collectives, body(): lax.all_to_all(request, 'span', split_axis=0, concat_axis=0, tiled=True)  14.6 us
    dot_general x3, matrix products, attend(): jnp.einsum('bhqk,bkhd->bqhd', weights, value_heads, preferred_element_typ...  12.4 us
    psum x1, blocking collectives, body(): used_totals = lax.psum(squares(used_values), 'head')  11.8 us
    psum x1, blocking collectives, body(): totals = lax.psum(squares(flat_self), 'head')  11.7 us
    unnamed x25, local copies, waits for them, and re-layouts  11.1 us
  transfers between devices with their start and end apart: 3, of which 2 were waited for; matrix products, arithmetic and copies ran while one was open for 9% of the time, Pallas kernels for 0%

commit v1 on v0

v1 whole, which is shorter than its diff:
```python
import functools

import jax
import jax.numpy as jnp
from jax import lax
from jax.experimental import pallas as pl
from jax.experimental.pallas import tpu as pltpu
from jax.sharding import PartitionSpec as P

HEAD_DIM = 128
SEG_LEN = 64
NBR_LEN = 128
NEIGHBOURS = 2
SEG_DEV = 4

EPSILON = 1e-06
LOG2E = 1.4426950408889634
SCALE2 = HEAD_DIM ** (-0.5) * LOG2E
HALF = SEG_LEN // 2
TAIL = 8

F32 = jnp.float32
BF16 = jnp.bfloat16


def dot(a, b, contract):
    return lax.dot_general(a, b, ((contract[:1], contract[1:]), ((), ())), preferred_element_type=F32)


def cost(flops, moved, exps=0):
    return pl.CostEstimate(flops=flops, bytes_accessed=moved, transcendentals=exps)


def params(**more):
    return pltpu.CompilerParams(vmem_limit_bytes=40 * 1024 * 1024, **more)


def pack_kernel(sources_ref, key_ref, value_ref, out_ref):
    heads = key_ref.shape[1] // HEAD_DIM
    listed = SEG_DEV * NEIGHBOURS
    lane = lax.broadcasted_iota(jnp.int32, (TAIL, HEAD_DIM), 1)
    tail = jnp.zeros((TAIL, HEAD_DIM), F32)
    for i in range(listed):
        named = sources_ref[i // NEIGHBOURS, i % NEIGHBOURS].astype(F32)
        tail = jnp.where(lane == i, named, tail)
    tail = tail.astype(BF16)
    for kv, ref in enumerate((key_ref, value_ref)):
        for half in range(2):
            for head in range(heads):
                stripe = (kv * 2 + half) * heads + head
                for seg in range(SEG_DEV):
                    row = seg * SEG_LEN + half * HALF
                    out_ref[stripe, seg * HALF:(seg + 1) * HALF, :] = ref[
                        row:row + HALF, head * HEAD_DIM:(head + 1) * HEAD_DIM
                    ]
                out_ref[stripe, SEG_DEV * HALF:SEG_DEV * HALF + TAIL, :] = tail


def pack(sources, segment_key, segment_value):
    columns = segment_key.shape[1]
    stripes = 4 * columns // HEAD_DIM
    shape = (stripes, SEG_DEV * HALF + TAIL, HEAD_DIM)
    return pl.pallas_call(
        pack_kernel,
        out_shape=jax.ShapeDtypeStruct(shape, BF16),
        in_specs=[
            pl.BlockSpec(memory_space=pltpu.SMEM),
            pl.BlockSpec(memory_space=pltpu.VMEM),
            pl.BlockSpec(memory_space=pltpu.VMEM),
        ],
        out_specs=pl.BlockSpec(memory_space=pltpu.VMEM),
        compiler_params=params(),
        cost_estimate=cost(1000000, 2 * 2 * segment_key.size * 2),
        name="pack_stripes",
    )(sources, segment_key, segment_value)


def pick_kernel(first, count, table_sources_ref, table_ref, out_ref):
    devices = out_ref.shape[0]

    def one(device, carry):
        for i in range(count):
            named = table_sources_ref[device, first + i]
            owner = lax.shift_right_logical(named, 2)
            within = lax.bitwise_and(named, SEG_DEV - 1)
            start = pl.multiple_of(within * HALF, HALF)
            out_ref[device, i * HALF:(i + 1) * HALF, :] = table_ref[owner, pl.ds(start, HALF), :]
        return carry

    lax.fori_loop(0, devices, one, 0)


def pick(named, table, first, count):
    devices = table.shape[0]
    return pl.pallas_call(
        functools.partial(pick_kernel, first, count),
        out_shape=jax.ShapeDtypeStruct((devices, count * HALF, HEAD_DIM), BF16),
        in_specs=[pl.BlockSpec(memory_space=pltpu.SMEM), pl.BlockSpec(memory_space=pltpu.VMEM)],
        out_specs=pl.BlockSpec(memory_space=pltpu.VMEM),
        compiler_params=params(),
        cost_estimate=cost(1000000, 2 * table.size + 2 * devices * count * HALF * HEAD_DIM),
        name="pick_stripes",
    )(named, table)


def lanes_of(square):
    return jnp.sum(square.T, axis=0, keepdims=True)


def self_kernel(query_ref, key_ref, value_ref, out_ref, squares_ref):
    n = pl.program_id(0)
    total = jnp.zeros((NBR_LEN, HEAD_DIM), F32)
    for head in range(query_ref.shape[1] // HEAD_DIM):
        at = slice(head * HEAD_DIM, (head + 1) * HEAD_DIM)
        scores = dot(key_ref[:, at], query_ref[:, at], (1, 1))
        top = jnp.max(scores, axis=0, keepdims=True)
        weights = jnp.exp2((scores - top) * SCALE2)
        weights = weights * (1.0 / jnp.sum(weights, axis=0, keepdims=True))
        rows = dot(weights.astype(BF16), value_ref[:, at], (0, 0)).astype(BF16)
        out_ref[:, at] = rows
        wide = rows.astype(F32)
        total = total + wide * wide
    squares_ref[pl.ds(n, 1), :] = lanes_of(total)


def self_attention(query, key, value):
    rows, columns = query.shape
    count = rows // NBR_LEN
    block = pl.BlockSpec((NBR_LEN, columns), lambda n: (n, 0))
    return pl.pallas_call(
        self_kernel,
        grid=(count,),
        out_shape=(
            jax.ShapeDtypeStruct((rows, columns), BF16),
            jax.ShapeDtypeStruct((count, NBR_LEN), F32),
        ),
        in_specs=[block, block, block],
        out_specs=(block, pl.BlockSpec((count, NBR_LEN), lambda n: (0, 0))),
        compiler_params=params(),
        cost_estimate=cost(4 * rows * NBR_LEN * columns, 8 * rows * columns, rows * columns),
        name="self_attention",
    )(query, key, value)


def cross_kernel(first, full_width, self_ref, got_ref, totals_ref, out_ref, squares_ref):
    n = pl.program_id(0)
    heads = self_ref.shape[1] // HEAD_DIM
    scale = lax.rsqrt(totals_ref[pl.ds(first + n, 1), :] / full_width + EPSILON) * SCALE2
    total = jnp.zeros((NBR_LEN, HEAD_DIM), F32)
    for head in range(heads):
        at = slice(head * HEAD_DIM, (head + 1) * HEAD_DIM)
        own = self_ref[:, at]
        key = jnp.concatenate([got_ref[head], got_ref[heads + head]], axis=0)
        value = jnp.concatenate([got_ref[2 * heads + head], got_ref[3 * heads + head]], axis=0)
        scores = dot(key, own, (1, 1))
        top = jnp.max(scores, axis=0, keepdims=True)
        weights = jnp.exp2((scores - top) * scale)
        weights = weights * (1.0 / jnp.sum(weights, axis=0, keepdims=True))
        crossed = dot(weights.astype(BF16), value, (0, 0)).astype(BF16)
        rows = (own.astype(F32) + crossed.astype(F32)).astype(BF16)
        out_ref[:, at] = rows
        wide = rows.astype(F32)
        total = total + wide * wide
    squares_ref[pl.ds(n, 1), :] = lanes_of(total)


def cross_attention(self_out, got, totals, first, count, got_first, full_width):
    columns = self_out.shape[1]
    rows = count * NBR_LEN
    return pl.pallas_call(
        functools.partial(cross_kernel, first, full_width),
        grid=(count,),
        out_shape=(
            jax.ShapeDtypeStruct((rows, columns), BF16),
            jax.ShapeDtypeStruct((count, NBR_LEN), F32),
        ),
        in_specs=[
            pl.BlockSpec((NBR_LEN, columns), lambda n: (first + n, 0)),
            pl.BlockSpec((got.shape[0], HALF, HEAD_DIM), lambda n: (0, got_first + n, 0)),
            pl.BlockSpec(totals.shape, lambda n: (0, 0)),
        ],
        out_specs=(
            pl.BlockSpec((NBR_LEN, columns), lambda n: (n, 0)),
            pl.BlockSpec((count, NBR_LEN), lambda n: (0, 0)),
        ),
        compiler_params=params(),
        cost_estimate=cost(4 * rows * SEG_LEN * columns, 6 * rows * columns, rows * columns // 2),
        name="cross_attention",
    )(self_out, got, totals)


def decode_kernel(full_width, *refs):
    query_ref, prior_ref, totals_ref, out_ref = refs[-4:]
    u = pl.program_id(0)
    scale = lax.rsqrt(totals_ref[u] / full_width + EPSILON) * SCALE2
    for head in range(query_ref.shape[1] // HEAD_DIM):
        at = slice(head * HEAD_DIM, (head + 1) * HEAD_DIM)
        prior = prior_ref[:, at]
        scores = dot(query_ref[:, at], prior, (1, 1)) * scale
        top = jnp.max(scores, axis=1, keepdims=True)
        weights = jnp.exp2(scores - top)
        weights = weights * (1.0 / jnp.sum(weights, axis=1, keepdims=True))
        out_ref[:, at] = dot(weights.astype(BF16), prior, (1, 0)).astype(BF16)


def decode(query, prior, totals, first, held, full_width):
    columns = query.shape[1]
    panel = NEIGHBOURS * NBR_LEN
    count = prior.shape[0] // panel
    query_block = pl.BlockSpec((SEG_LEN, columns), lambda u: (first + u, 0))
    in_specs = [
        query_block,
        pl.BlockSpec((panel, columns), lambda u: (u, 0)),
        pl.BlockSpec((count, 1, panel), lambda u: (0, 0, 0)),
    ]
    operands = (query, prior, totals.reshape(count, 1, panel))
    aliases = {}
    if held is not None:
        in_specs = [pl.BlockSpec(memory_space=pl.ANY)] + in_specs
        operands = (held,) + operands
        aliases = {0: 0}
    rows = count * SEG_LEN
    return pl.pallas_call(
        functools.partial(decode_kernel, full_width),
        grid=(count,),
        out_shape=jax.ShapeDtypeStruct(query.shape, BF16),
        in_specs=in_specs,
        out_specs=query_block,
        input_output_aliases=aliases,
        compiler_params=params(),
        cost_estimate=cost(4 * rows * panel * columns, 4 * rows * columns + 2 * prior.size, rows * 2 * columns),
        name="decode",
    )(*operands)


def over_heads(part):
    heads = lax.axis_size("head")
    total = part
    for step in range(1, heads):
        total = total + lax.ppermute(part, "head", [(i, (i + step) % heads) for i in range(heads)])
    return total


def from_behind(part):
    devices = lax.axis_size("span")
    return lax.ppermute(part, "span", [(i, i + 1) for i in range(devices - 1)])


def total_from_behind(part):
    devices, heads = lax.axis_size("span"), lax.axis_size("head")
    total = None
    for step in range(heads):
        pairs = [
            (s * heads + h, (s + 1) * heads + (h + step) % heads)
            for s in range(devices - 1)
            for h in range(heads)
        ]
        came = lax.ppermute(part, ("span", "head"), pairs)
        total = came if total is None else total + came
    return total


def exchange(x):
    return lax.all_to_all(x, "span", split_axis=0, concat_axis=0, tiled=True)


def body(
    neighbour_query,
    neighbour_key,
    neighbour_value,
    segment_key,
    segment_value,
    decoder_query,
    sources,
):
    columns = neighbour_query.shape[1]
    full_width = columns * lax.axis_size("head")
    per_device = SEG_DEV * NEIGHBOURS
    table = exchange(pack(sources, segment_key, segment_value))
    self_out, squares = self_attention(neighbour_query, neighbour_key, neighbour_value)
    totals = over_heads(squares)
    named = table[:, SEG_DEV * HALF, :per_device].astype(jnp.int32)
    got = exchange(pick(named, table, 0, per_device))
    last = per_device - NEIGHBOURS
    panel, panel_squares = cross_attention(self_out, got, totals, last, NEIGHBOURS, last, full_width)
    came = from_behind(panel)
    came_totals = total_from_behind(panel_squares)
    rest, rest_squares = cross_attention(self_out, got, totals, 0, last, 0, full_width)
    rest_totals = over_heads(rest_squares)
    blended = decode(decoder_query, rest, rest_totals, 1, None, full_width)
    return decode(decoder_query, came, came_totals, 0, blended, full_width)


def solution(mesh):
    placed = (
        P("span", "head"),
        P("span", "head"),
        P("span", "head"),
        P("span", "head"),
        P("span", "head"),
        P("span", "head"),
        P("span", None),
    )
    return jax.shard_map(
        body, mesh=mesh, in_specs=placed, out_specs=P("span", "head"), check_vma=False
    )
```

time: 290 us -> 130 us (0.45); the launches traced: 285 us -> 128 us
  waiting for transfers between devices: 174 us -> 7.33 us
  Pallas kernels: 0 us -> 52.1 us
  local copies, waits for them, and re-layouts: 35.3 us -> 14.4 us
  matrix products: 17.1 us -> 0 us
  starting transfers between devices: 12.3 us -> 28.4 us
  blocking collectives: 38.1 us -> 25.7 us
  other arithmetic: 7.62 us -> 0.03 us
    all_to_all x2 -> x1, waiting for transfers between devices: 174 us -> 0.01 us  [exchange(): return lax.all_to_all(x, 'span', split_axis=0, concat_axis=0, tiled=True)]
    pallas_call x0 -> x7, Pallas kernels: none -> 52.1 us  [the longest x1 18.9 us: self_attention(): pl.pallas_call(self_kernel, grid=(count,), out_shape=(jax.ShapeDtypeStruc...]
    psum x2 -> x0, blocking collectives: 23.5 us -> none  [the longest x1 11.8 us: body(): used_totals = lax.psum(squares(used_values), 'head')]
    ppermute x1 -> x11, starting transfers between devices: 2.11 us -> 24.4 us  [the longest x4 13.7 us: total_from_behind(): came = lax.ppermute(part, ('span', 'head'), pairs)]
    gather x4 -> x0, local copies, waits for them, and re-layouts: 19.4 us -> none  [the longest x1 5.24 us: body(): own_keys = segment_key.reshape(SEG_DEV, SEG_LEN, columns)[wanted]]
    dot_general x6 -> x0, matrix products: 17.1 us -> none  [the longest x3 12.4 us: attend(): jnp.einsum('bhqk,bkhd->bqhd', weights, value_heads, preferred_element_typ...]
    all_to_all x1, blocking collectives: 14.6 us -> 25.7 us  [exchange(): return lax.all_to_all(x, 'span', split_axis=0, concat_axis=0, tiled=True)]
    ppermute x1 -> x11, waiting for transfers between devices: 0.01 us -> 7.33 us  [the longest x6 7.32 us: over_heads(): lax.ppermute(part, 'head', [(i, (i + step) % heads) for i in range(heads)])]
  transfers between devices with their start and end apart: 3 -> 12, of which waited for: 2 -> 4; matrix products, arithmetic and copies ran while one was open for 9% -> 0% of each run, Pallas kernels for 0% -> 32%
where the time goes in v1:
time: 130 us; the launch traced here: 128 us
  Pallas kernels  52.1 us (40%)
  starting transfers between devices  28.4 us (22%)
  blocking collectives  25.7 us (20%)
  local copies, waits for them, and re-layouts  14.4 us (11%)
  waiting for transfers between devices  7.33 us (6%)
    all_to_all x1, blocking collectives, exchange(): return lax.all_to_all(x, 'span', split_axis=0, concat_axis=0, tiled=True)  25.7 us
    pallas_call x1, Pallas kernels, self_attention(): pl.pallas_call(self_kernel, grid=(count,), out_shape=(jax.ShapeDtypeStruc...  18.9 us
    pallas_call x2, Pallas kernels, cross_attention(): pl.pallas_call(functools.partial(cross_kernel, first, full_width), grid=(...  18.7 us
    unnamed x23, local copies, waits for them, and re-layouts  14.4 us
    ppermute x4, starting transfers between devices, total_from_behind(): came = lax.ppermute(part, ('span', 'head'), pairs)  13.7 us
    pallas_call x2, Pallas kernels, decode(): pl.pallas_call(functools.partial(decode_kernel, full_width), grid=(count,...  12.1 us
    ppermute x6, starting transfers between devices, over_heads(): lax.ppermute(part, 'head', [(i, (i + step) % heads) for i in range(heads)])  9.44 us
    ppermute x6, waiting for transfers between devices, over_heads(): lax.ppermute(part, 'head', [(i, (i + step) % heads) for i in range(heads)])  7.32 us
  transfers between devices with their start and end apart: 12, of which 4 were waited for; matrix products, arithmetic and copies ran while one was open for 0% of the time, Pallas kernels for 32%

profile of v1, /device:TPU:0, one launch (start us, length us, event | category | flops | bytes accessed | tf_op | source)
XLA Modules:
  0.0 128.2 jit_solution(6824824379697614499)
XLA Ops:
  0.0 0.8 copy.9.sources_ref
  0.8 1.0 copy-done.9
  1.8 1.0 copy-done.10
  2.8 0.8 pack_stripes.1
  3.6 25.7 %all_to_all.10.table_ref = bf16[32,136,128]{2,1,0:T(8,128)(2,1)S(1)} all-to-all(bf16[32,136,128]{2,1,0:T(8,128)(2,1)S(1)} %pack_stripes.1), channel_id=1, replica_groups=mesh['span'=32,'head'=4] {'span'}, dimensions={0} | all-to-all | bytes 2228224 | tf_op jit(solution)/shard_map/all_to_all | solution.py:264
  29.4 1.6 %pick_stripes.1 = bf16[32,256,128]{2,1,0:T(8,128)(2,1)S(1)} custom-call(s32[32,8]{1,0:T(8,128)S(1)} %bitcast.2, bf16[32,136,128]{2,1,0:T(8,128)(2,1)S(1)} %all_to_all.10.table_ref), custom_call_target="tpu_custom_call" | custom-call | flops 1000000 | bytes 3211264 | tf_op jit(solution)/shard_map/pick_stripes/pallas_call | solution.py:95
  31.0 0.0 copy-start.2
  31.0 1.3 %copy-done.2 = bf16[32,256,128]{2,1,0:T(8,128)(2,1)} copy-done((bf16[32,256,128]{2,1,0:T(8,128)(2,1)}, bf16[32,256,128]{2,1,0:T(8,128)(2,1)S(1)}, u32[]{:S(2)}) %copy-start.2) | copy-done | bytes 2097176
  32.3 4.0 %all-to-all-start.1 = ((bf16[32,256,128]{2,1,0:T(8,128)(2,1)}), bf16[32,256,128]{2,1,0:T(8,128)(2,1)S(1)}, u32[]{:S(2)}, u32[]{:S(2)}) async-start(bf16[32,256,128]{2,1,0:T(8,128)(2,1)} %copy-done.2), calls=%async_computation.1 | async-start | bytes 4194304 | tf_op jit(solution)/shard_map/all_to_all | solution.py:264
  36.3 0.0 copy-start.3
  36.3 1.6 %copy-done.3 = bf16[1024,1024]{1,0:T(8,128)(2,1)S(1)} copy-done((bf16[1024,1024]{1,0:T(8,128)(2,1)S(1)}, bf16[1024,1024]{1,0:T(8,128)(2,1)}, u32[]{:S(2)}) %copy-start.3) | copy-done | bytes 2097176
  37.9 1.6 %copy-done.4 = bf16[1024,1024]{1,0:T(8,128)(2,1)S(1)} copy-done((bf16[1024,1024]{1,0:T(8,128)(2,1)S(1)}, bf16[1024,1024]{1,0:T(8,128)(2,1)}, u32[]{:S(2)}) %copy-start.4) | copy-done | bytes 2097176
  39.5 1.6 %copy-done.5 = bf16[1024,1024]{1,0:T(8,128)(2,1)S(1)} copy-done((bf16[1024,1024]{1,0:T(8,128)(2,1)S(1)}, bf16[1024,1024]{1,0:T(8,128)(2,1)}, u32[]{:S(2)}) %copy-start.5) | copy-done | bytes 2097176
  41.1 18.9 %self_attention.1 = (bf16[1024,1024]{1,0:T(8,128)(2,1)S(1)}, f32[8,128]{1,0:T(8,128)S(1)}) custom-call(bf16[1024,1024]{1,0:T(8,128)(2,1)S(1)} %copy-done.3, bf16[1024,1024]{1,0:T(8,128)(2,1)S(1)} %copy-done.4, bf16[1024,1024]{1,0:T(8,128)(2,1)S(1)} %copy-done.5), custom_call_target="tpu_custom_call" | custom-call | flops 536870912 | bytes 8388608 | tf_op jit(solution)/shard_map/self_attention/pallas_call | solution.py:130
  60.0 0.0 copy-start
  60.1 1.3 %copy-done = bf16[1024,1024]{1,0:T(8,128)(2,1)} copy-done((bf16[1024,1024]{1,0:T(8,128)(2,1)}, bf16[1024,1024]{1,0:T(8,128)(2,1)S(1)}, u32[]{:S(2)}) %copy-start) | copy-done | bytes 2097176
  61.4 4.0 %collective-permute-start.2 = (f32[8,128]{1,0:T(8,128)S(1)}, f32[8,128]{1,0:T(8,128)S(1)}, u32[]{:S(2)}, u32[]{:S(2)}) collective-permute-start(f32[8,128]{1,0:T(8,128)S(1)} %get-tuple-element.12), channel_id=1, source_target_pairs={{0,3},{1,0},{2,1},{3,2},{4,7},{5,4},{6,5},{7,6},{8,11},{9,8},{10,9... | collective-permute-start | bytes 12296 | tf_op jit(solution)/shard_map/ppermute | solution.py:240
  65.4 0.0 collective-permute-start.1
  65.4 1.3 collective-permute-start
  66.7 0.1 collective-permute-done.2
  66.7 3.8 %collective-permute-done.1 = f32[8,128]{1,0:T(8,128)S(1)} collective-permute-done((f32[8,128]{1,0:T(8,128)S(1)}, f32[8,128]{1,0:T(8,128)S(1)}, u32[]{:S(2)}, u32[]{:S(2)}) %collective-permute-start.1) | collective-permute-done | bytes 4128 | tf_op jit(solution)/shard_map/ppermute | solution.py:240
  70.5 0.0 collective-permute-done
  70.5 0.0 all-to-all-done.1.got_ref
  70.5 0.0 copy-start.1
  70.6 1.6 %copy-done.1 = bf16[1024,1024]{1,0:T(8,128)(2,1)S(1)} copy-done((bf16[1024,1024]{1,0:T(8,128)(2,1)S(1)}, bf16[1024,1024]{1,0:T(8,128)(2,1)}, u32[]{:S(2)}) %copy-start.1) | copy-done | bytes 2097176
  72.1 5.1 %cross_attention.3 = (bf16[256,1024]{1,0:T(8,128)(2,1)}, f32[2,128]{1,0:T(2,128)S(1)}) custom-call(bf16[1024,1024]{1,0:T(8,128)(2,1)S(1)} %copy-done.1, bf16[32,256,128]{2,1,0:T(8,128)(2,1)S(1)} %all-to-all-done.1.got_ref, f32[8,128]{1,0:T(8,128)S(1)} %add_add_fusion.1.totals_ref), custom_call_target="tpu_custom_call" | custom-call | flops 67108864 | bytes 1572864 | tf_op jit(solution)/shard_map/cross_attention/pallas_call | solution.py:170
  77.3 1.3 %collective-permute-start.6 = (bf16[256,1024]{1,0:T(8,128)(2,1)}, bf16[256,1024]{1,0:T(8,128)(2,1)S(1)}, u32[]{:S(2)}, u32[]{:S(2)}) collective-permute-start(bf16[256,1024]{1,0:T(8,128)(2,1)} %get-tuple-element.15), channel_id=1, source_target_pairs={{0,4},{4,8},{8,12},{12,16},{16,20},{20,24},{24,28},{28,32},{32,36}... | collective-permute-start | bytes 1572872 | tf_op jit(solution)/shard_map/ppermute | solution.py:246
  78.6 0.0 copy-start.6
  78.6 4.6 %collective-permute-start.10 = (f32[2,128]{1,0:T(2,128)S(1)}, f32[2,128]{1,0:T(2,128)S(1)}, u32[]{:S(2)}, u32[]{:S(2)}) collective-permute-start(f32[2,128]{1,0:T(2,128)S(1)} %get-tuple-element.16), channel_id=1, source_target_pairs={{0,7},{1,4},{2,5},{3,6},{4,11},{5,8},{6,9},{7,10},{8,15},{9,12},{1... | collective-permute-start | bytes 3080 | tf_op jit(solution)/shard_map/ppermute | solution.py:258
  83.2 3.3 %collective-permute-start.9 = (f32[2,128]{1,0:T(2,128)S(1)}, f32[2,128]{1,0:T(2,128)S(1)}, u32[]{:S(2)}, u32[]{:S(2)}) collective-permute-start(f32[2,128]{1,0:T(2,128)S(1)} %get-tuple-element.16), channel_id=1, source_target_pairs={{0,6},{1,7},{2,4},{3,5},{4,10},{5,11},{6,8},{7,9},{8,14},{9,15},{1... | collective-permute-start | bytes 3080 | tf_op jit(solution)/shard_map/ppermute | solution.py:258
  86.6 4.0 %collective-permute-start.8 = (f32[2,128]{1,0:T(2,128)S(1)}, f32[2,128]{1,0:T(2,128)S(1)}, u32[]{:S(2)}, u32[]{:S(2)}) collective-permute-start(f32[2,128]{1,0:T(2,128)S(1)} %get-tuple-element.16), channel_id=1, source_target_pairs={{0,5},{1,6},{2,7},{3,4},{4,9},{5,10},{6,11},{7,8},{8,13},{9,14},{1... | collective-permute-start | bytes 3080 | tf_op jit(solution)/shard_map/ppermute | solution.py:258
  90.5 1.8 %collective-permute-start.7 = (f32[2,128]{1,0:T(2,128)S(1)}, f32[2,128]{1,0:T(2,128)S(1)}, u32[]{:S(2)}, u32[]{:S(2)}) collective-permute-start(f32[2,128]{1,0:T(2,128)S(1)} %get-tuple-element.16), channel_id=1, source_target_pairs={{0,4},{1,5},{2,6},{3,7},{4,8},{5,9},{6,10},{7,11},{8,12},{9,13},{1... | collective-permute-start | bytes 3080 | tf_op jit(solution)/shard_map/ppermute | solution.py:258
  92.3 13.6 %cross_attention.2 = (bf16[768,1024]{1,0:T(8,128)(2,1)S(1)}, f32[6,128]{1,0:T(8,128)S(1)}) custom-call(bf16[1024,1024]{1,0:T(8,128)(2,1)S(1)} %copy-done.1, bf16[32,256,128]{2,1,0:T(8,128)(2,1)S(1)} %all-to-all-done.1.got_ref, f32[8,128]{1,0:T(8,128)S(1)} %add_add_fusion.1.totals_ref), custom_call_target="tpu_custom_call" | custom-call | flops 201326592 | bytes 4718592 | tf_op jit(solution)/shard_map/cross_attention/pallas_call | solution.py:170
  105.9 1.2 copy-done.7
  107.0 0.0 collective-permute-done.10
  107.0 2.4 %collective-permute-start.5 = (f32[6,128]{1,0:T(8,128)S(1)}, f32[6,128]{1,0:T(8,128)S(1)}, u32[]{:S(2)}, u32[]{:S(2)}) collective-permute-start(f32[6,128]{1,0:T(8,128)S(1)} %get-tuple-element.14), channel_id=1, source_target_pairs={{0,3},{1,0},{2,1},{3,2},{4,7},{5,4},{6,5},{7,6},{8,11},{9,8},{10,9... | collective-permute-start | bytes 9224 | tf_op jit(solution)/shard_map/ppermute | solution.py:240
  109.4 0.0 collective-permute-done.9
  109.4 0.4 collective-permute-start.4
  109.9 0.0 collective-permute-done.8
  109.9 1.3 %collective-permute-start.3 = (f32[6,128]{1,0:T(8,128)S(1)}, f32[6,128]{1,0:T(8,128)S(1)}, u32[]{:S(2)}, u32[]{:S(2)}) collective-permute-start(f32[6,128]{1,0:T(8,128)S(1)} %get-tuple-element.14), channel_id=1, source_target_pairs={{0,1},{1,2},{2,3},{3,0},{4,5},{5,6},{6,7},{7,4},{8,9},{9,10},{10,1... | collective-permute-start | bytes 9224 | tf_op jit(solution)/shard_map/ppermute | solution.py:240
  111.2 0.0 collective-permute-done.7
  111.2 0.0 collective-permute-done.5
  111.2 3.3 %collective-permute-done.4 = f32[6,128]{1,0:T(8,128)S(1)} collective-permute-done((f32[6,128]{1,0:T(8,128)S(1)}, f32[6,128]{1,0:T(8,128)S(1)}, u32[]{:S(2)}, u32[]{:S(2)}) %collective-permute-start.4) | collective-permute-done | bytes 3104 | tf_op jit(solution)/shard_map/ppermute | solution.py:240
  114.5 0.1 collective-permute-done.3
  114.7 1.4 %copy-done.8 = bf16[768,1024]{1,0:T(8,128)(2,1)S(1)} copy-done((bf16[768,1024]{1,0:T(8,128)(2,1)S(1)}, bf16[768,1024]{1,0:T(8,128)(2,1)}, u32[]{:S(2)}) %copy-start.8) | copy-done | bytes 1572888
  116.1 8.7 %decode.2.refs_0_ = bf16[256,1024]{1,0:T(8,128)(2,1)} custom-call(bf16[256,1024]{1,0:T(8,128)(2,1)S(1)} %copy-done.6, bf16[768,1024]{1,0:T(8,128)(2,1)S(1)} %copy-done.8, f32[3,1,256]{2,1,0:T(1,128)S(1)} %reshape.8.refs_2_), custom_call_target="tpu_custom_call" | custom-call | flops 201326592 | bytes 2359296 | tf_op jit(solution)/shard_map/decode/pallas_call | solution.py:223
  124.8 0.0 collective-permute-done.6.refs_2_
  124.8 3.3 %decode.3 = bf16[256,1024]{1,0:T(8,128)(2,1)} custom-call(bf16[256,1024]{1,0:T(8,128)(2,1)} %decode.2.refs_0_, bf16[256,1024]{1,0:T(8,128)(2,1)S(1)} %copy-done.6, bf16[256,1024]{1,0:T(8,128)(2,1)S(1)} %collective-permute-done.6.refs_2_, f32[1,1,256]{2,1,0:T(1,128)S(1)} %bitcast.3), custom_call_target="tpu_custom_call", output_to_operand_aliasing={{}: (0, {})} | custom-call | flops 67108864 | bytes 786432 | tf_op jit(solution)/shard_map/decode/pallas_call | solution.py:223
  (12 shorter events, 0.1 us)
Async XLA Ops:
  0.8 1.0 copy-start.9
  1.8 1.0 copy-start.10
  31.0 1.3 %copy-start.2 = (bf16[32,256,128]{2,1,0:T(8,128)(2,1)}, bf16[32,256,128]{2,1,0:T(8,128)(2,1)S(1)}, u32[]{:S(2)}) copy-start(bf16[32,256,128]{2,1,0:T(8,128)(2,1)S(1)} %pick_stripes.1) | copy-start | bytes 6291460
  32.3 38.2 %all-to-all-start.1 = ((bf16[32,256,128]{2,1,0:T(8,128)(2,1)}), bf16[32,256,128]{2,1,0:T(8,128)(2,1)S(1)}, u32[]{:S(2)}, u32[]{:S(2)}) async-start(bf16[32,256,128]{2,1,0:T(8,128)(2,1)} %copy-done.2), calls=%async_computation.1 | async-start | bytes 4194304 | tf_op jit(solution)/shard_map/all_to_all | solution.py:264
  36.3 1.6 %copy-start.3 = (bf16[1024,1024]{1,0:T(8,128)(2,1)S(1)}, bf16[1024,1024]{1,0:T(8,128)(2,1)}, u32[]{:S(2)}) copy-start(bf16[1024,1024]{1,0:T(8,128)(2,1)} %query_ref.1) | copy-start | bytes 6291460
  37.9 1.6 %copy-start.4 = (bf16[1024,1024]{1,0:T(8,128)(2,1)S(1)}, bf16[1024,1024]{1,0:T(8,128)(2,1)}, u32[]{:S(2)}) copy-start(bf16[1024,1024]{1,0:T(8,128)(2,1)} %key_ref.2) | copy-start | bytes 6291460
  39.5 1.6 %copy-start.5 = (bf16[1024,1024]{1,0:T(8,128)(2,1)S(1)}, bf16[1024,1024]{1,0:T(8,128)(2,1)}, u32[]{:S(2)}) copy-start(bf16[1024,1024]{1,0:T(8,128)(2,1)} %value_ref.2) | copy-start | bytes 6291460
  60.0 1.3 %copy-start = (bf16[1024,1024]{1,0:T(8,128)(2,1)}, bf16[1024,1024]{1,0:T(8,128)(2,1)S(1)}, u32[]{:S(2)}) copy-start(bf16[1024,1024]{1,0:T(8,128)(2,1)S(1)} %get-tuple-element.11.self_ref) | copy-start | bytes 6291460
  61.4 5.4 %collective-permute-start.2 = (f32[8,128]{1,0:T(8,128)S(1)}, f32[8,128]{1,0:T(8,128)S(1)}, u32[]{:S(2)}, u32[]{:S(2)}) collective-permute-start(f32[8,128]{1,0:T(8,128)S(1)} %get-tuple-element.12), channel_id=1, source_target_pairs={{0,3},{1,0},{2,1},{3,2},{4,7},{5,4},{6,5},{7,6},{8,11},{9,8},{10,9... | collective-permute-start | bytes 12296 | tf_op jit(solution)/shard_map/ppermute | solution.py:240
  65.4 5.1 %collective-permute-start.1 = (f32[8,128]{1,0:T(8,128)S(1)}, f32[8,128]{1,0:T(8,128)S(1)}, u32[]{:S(2)}, u32[]{:S(2)}) collective-permute-start(f32[8,128]{1,0:T(8,128)S(1)} %get-tuple-element.12), channel_id=1, source_target_pairs={{0,2},{1,3},{2,0},{3,1},{4,6},{5,7},{6,4},{7,5},{8,10},{9,11},{10,... | collective-permute-start | bytes 12296 | tf_op jit(solution)/shard_map/ppermute | solution.py:240
  65.4 5.1 %collective-permute-start = (f32[8,128]{1,0:T(8,128)S(1)}, f32[8,128]{1,0:T(8,128)S(1)}, u32[]{:S(2)}, u32[]{:S(2)}) collective-permute-start(f32[8,128]{1,0:T(8,128)S(1)} %get-tuple-element.12), channel_id=1, source_target_pairs={{0,1},{1,2},{2,3},{3,0},{4,5},{5,6},{6,7},{7,4},{8,9},{9,10},{10,1... | collective-permute-start | bytes 12296 | tf_op jit(solution)/shard_map/ppermute | solution.py:240
  70.5 1.6 %copy-start.1 = (bf16[1024,1024]{1,0:T(8,128)(2,1)S(1)}, bf16[1024,1024]{1,0:T(8,128)(2,1)}, u32[]{:S(2)}) copy-start(bf16[1024,1024]{1,0:T(8,128)(2,1)} %copy-done) | copy-start | bytes 6291460
  77.3 47.6 %collective-permute-start.6 = (bf16[256,1024]{1,0:T(8,128)(2,1)}, bf16[256,1024]{1,0:T(8,128)(2,1)S(1)}, u32[]{:S(2)}, u32[]{:S(2)}) collective-permute-start(bf16[256,1024]{1,0:T(8,128)(2,1)} %get-tuple-element.15), channel_id=1, source_target_pairs={{0,4},{4,8},{8,12},{12,16},{16,20},{20,24},{24,28},{28,32},{32,36}... | collective-permute-start | bytes 1572872 | tf_op jit(solution)/shard_map/ppermute | solution.py:246
  78.6 36.1 %copy-start.6 = (bf16[256,1024]{1,0:T(8,128)(2,1)S(1)}, bf16[256,1024]{1,0:T(8,128)(2,1)}, u32[]{:S(2)}) copy-start(bf16[256,1024]{1,0:T(8,128)(2,1)} %refs_1_.1) | copy-start | bytes 1572868
  78.6 28.4 %collective-permute-start.10 = (f32[2,128]{1,0:T(2,128)S(1)}, f32[2,128]{1,0:T(2,128)S(1)}, u32[]{:S(2)}, u32[]{:S(2)}) collective-permute-start(f32[2,128]{1,0:T(2,128)S(1)} %get-tuple-element.16), channel_id=1, source_target_pairs={{0,7},{1,4},{2,5},{3,6},{4,11},{5,8},{6,9},{7,10},{8,15},{9,12},{1... | collective-permute-start | bytes 3080 | tf_op jit(solution)/shard_map/ppermute | solution.py:258
  83.2 26.2 %collective-permute-start.9 = (f32[2,128]{1,0:T(2,128)S(1)}, f32[2,128]{1,0:T(2,128)S(1)}, u32[]{:S(2)}, u32[]{:S(2)}) collective-permute-start(f32[2,128]{1,0:T(2,128)S(1)} %get-tuple-element.16), channel_id=1, source_target_pairs={{0,6},{1,7},{2,4},{3,5},{4,10},{5,11},{6,8},{7,9},{8,14},{9,15},{1... | collective-permute-start | bytes 3080 | tf_op jit(solution)/shard_map/ppermute | solution.py:258
  86.6 23.3 %collective-permute-start.8 = (f32[2,128]{1,0:T(2,128)S(1)}, f32[2,128]{1,0:T(2,128)S(1)}, u32[]{:S(2)}, u32[]{:S(2)}) collective-permute-start(f32[2,128]{1,0:T(2,128)S(1)} %get-tuple-element.16), channel_id=1, source_target_pairs={{0,5},{1,6},{2,7},{3,4},{4,9},{5,10},{6,11},{7,8},{8,13},{9,14},{1... | collective-permute-start | bytes 3080 | tf_op jit(solution)/shard_map/ppermute | solution.py:258
  90.5 20.7 %collective-permute-start.7 = (f32[2,128]{1,0:T(2,128)S(1)}, f32[2,128]{1,0:T(2,128)S(1)}, u32[]{:S(2)}, u32[]{:S(2)}) collective-permute-start(f32[2,128]{1,0:T(2,128)S(1)} %get-tuple-element.16), channel_id=1, source_target_pairs={{0,4},{1,5},{2,6},{3,7},{4,8},{5,9},{6,10},{7,11},{8,12},{9,13},{1... | collective-permute-start | bytes 3080 | tf_op jit(solution)/shard_map/ppermute | solution.py:258
  105.9 1.2 copy-start.7
  107.0 4.2 %collective-permute-start.5 = (f32[6,128]{1,0:T(8,128)S(1)}, f32[6,128]{1,0:T(8,128)S(1)}, u32[]{:S(2)}, u32[]{:S(2)}) collective-permute-start(f32[6,128]{1,0:T(8,128)S(1)} %get-tuple-element.14), channel_id=1, source_target_pairs={{0,3},{1,0},{2,1},{3,2},{4,7},{5,4},{6,5},{7,6},{8,11},{9,8},{10,9... | collective-permute-start | bytes 9224 | tf_op jit(solution)/shard_map/ppermute | solution.py:240
  109.4 5.1 %collective-permute-start.4 = (f32[6,128]{1,0:T(8,128)S(1)}, f32[6,128]{1,0:T(8,128)S(1)}, u32[]{:S(2)}, u32[]{:S(2)}) collective-permute-start(f32[6,128]{1,0:T(8,128)S(1)} %get-tuple-element.14), channel_id=1, source_target_pairs={{0,2},{1,3},{2,0},{3,1},{4,6},{5,7},{6,4},{7,5},{8,10},{9,11},{10,... | collective-permute-start | bytes 9224 | tf_op jit(solution)/shard_map/ppermute | solution.py:240
  109.9 4.8 %collective-permute-start.3 = (f32[6,128]{1,0:T(8,128)S(1)}, f32[6,128]{1,0:T(8,128)S(1)}, u32[]{:S(2)}, u32[]{:S(2)}) collective-permute-start(f32[6,128]{1,0:T(8,128)S(1)} %get-tuple-element.14), channel_id=1, source_target_pairs={{0,1},{1,2},{2,3},{3,0},{4,5},{5,6},{6,7},{7,4},{8,9},{9,10},{10,1... | collective-permute-start | bytes 9224 | tf_op jit(solution)/shard_map/ppermute | solution.py:240
  114.7 1.4 %copy-start.8 = (bf16[768,1024]{1,0:T(8,128)(2,1)S(1)}, bf16[768,1024]{1,0:T(8,128)(2,1)}, u32[]{:S(2)}) copy-start(bf16[768,1024]{1,0:T(8,128)(2,1)} %copy-done.7) | copy-start | bytes 4718596

commit v2 on v1

v2 whole, which is shorter than its diff:
```python
import functools

import jax
import jax.numpy as jnp
from jax import lax
from jax.experimental import pallas as pl
from jax.experimental.pallas import tpu as pltpu
from jax.sharding import PartitionSpec as P

HEAD_DIM = 128
SEG_LEN = 64
NBR_LEN = 128
NEIGHBOURS = 2
SEG_DEV = 4

EPSILON = 1e-06
LOG2E = 1.4426950408889634
SCALE2 = HEAD_DIM ** (-0.5) * LOG2E
HALF = SEG_LEN // 2
TAIL = 8
PACK_MIB = 60
SELF_MIB = 60
SMALL_MIB = 24

F32 = jnp.float32
BF16 = jnp.bfloat16


def dot(a, b, contract):
    return lax.dot_general(a, b, ((contract[:1], contract[1:]), ((), ())), preferred_element_type=F32)


def cost(flops, moved, exps=0):
    return pl.CostEstimate(flops=flops, bytes_accessed=moved, transcendentals=exps)


def params(mib):
    return pltpu.CompilerParams(vmem_limit_bytes=mib * 1024 * 1024)


def pack_kernel(sources_ref, key_ref, value_ref, out_ref):
    heads = key_ref.shape[1] // HEAD_DIM
    lane = lax.broadcasted_iota(jnp.int32, (TAIL, HEAD_DIM), 1)
    tail = jnp.zeros((TAIL, HEAD_DIM), F32)
    for i in range(SEG_DEV * NEIGHBOURS):
        named = sources_ref[i % NEIGHBOURS, i // NEIGHBOURS].astype(F32)
        tail = jnp.where(lane == i, named, tail)
    tail = tail.astype(BF16)
    for kv, ref in enumerate((key_ref, value_ref)):
        for half in range(2):
            for head in range(heads):
                for seg in range(SEG_DEV):
                    row = seg * SEG_LEN + half * HALF
                    out_ref[kv * 2 + half, head, seg * HALF:(seg + 1) * HALF, :] = ref[
                        row:row + HALF, head * HEAD_DIM:(head + 1) * HEAD_DIM
                    ]
                out_ref[kv * 2 + half, head, SEG_DEV * HALF:SEG_DEV * HALF + TAIL, :] = tail


def pack(sources, segment_key, segment_value):
    rows, columns = segment_key.shape
    heads = columns // HEAD_DIM
    long = SEG_DEV * HALF + TAIL
    steps = 4
    block = pl.BlockSpec((rows, columns // steps), lambda i: (0, i))
    out = pl.pallas_call(
        pack_kernel,
        grid=(steps,),
        out_shape=jax.ShapeDtypeStruct((4, heads, long, HEAD_DIM), BF16),
        in_specs=[pl.BlockSpec(memory_space=pltpu.SMEM), block, block],
        out_specs=pl.BlockSpec((4, heads // steps, long, HEAD_DIM), lambda i: (0, i, 0, 0)),
        compiler_params=params(PACK_MIB),
        cost_estimate=cost(1000000, 2 * 2 * segment_key.size * 2),
        name="pack_stripes",
    )(sources.T, segment_key, segment_value)
    return out.reshape(4 * heads, long, HEAD_DIM)


def pick_kernel(named_ref, table_ref, out_ref):
    devices = out_ref.shape[0]
    count = SEG_DEV * NEIGHBOURS

    def one(device, carry):
        for i in range(count):
            named = named_ref[device, i]
            owner = lax.shift_right_logical(named, 2)
            within = lax.bitwise_and(named, SEG_DEV - 1)
            start = pl.multiple_of(within * HALF, HALF)
            out_ref[device, i * HALF:(i + 1) * HALF, :] = table_ref[owner, pl.ds(start, HALF), :]
        return carry

    lax.fori_loop(0, devices, one, 0, unroll=2)


def pick(named, table):
    devices = table.shape[0]
    count = SEG_DEV * NEIGHBOURS
    return pl.pallas_call(
        pick_kernel,
        out_shape=jax.ShapeDtypeStruct((devices, count * HALF, HEAD_DIM), BF16),
        in_specs=[pl.BlockSpec(memory_space=pltpu.SMEM), pl.BlockSpec(memory_space=pltpu.VMEM)],
        out_specs=pl.BlockSpec(memory_space=pltpu.VMEM),
        compiler_params=params(SMALL_MIB),
        cost_estimate=cost(1000000, 2 * table.size + 2 * devices * count * HALF * HEAD_DIM),
        name="pick_stripes",
    )(named, table)


def lanes_of(square):
    return jnp.sum(square.T, axis=0, keepdims=True)


def columns_of(head):
    return slice(head * HEAD_DIM, (head + 1) * HEAD_DIM)


def softmax_down(scores, scale):
    weights = jnp.exp2((scores - jnp.max(scores, axis=0, keepdims=True)) * scale)
    return (weights * (1.0 / jnp.sum(weights, axis=0, keepdims=True))).astype(BF16)


def softmax_across(scores):
    weights = jnp.exp2(scores - jnp.max(scores, axis=1, keepdims=True))
    return (weights * (1.0 / jnp.sum(weights, axis=1, keepdims=True))).astype(BF16)


def self_kernel(query_ref, key_ref, value_ref, out_ref, squares_ref):
    n = pl.program_id(0)
    heads = range(query_ref.shape[1] // HEAD_DIM)
    at = [columns_of(head) for head in heads]
    scores = [dot(key_ref[:, at[h]], query_ref[:, at[h]], (1, 1)) for h in heads]
    weights = [softmax_down(scores[h], SCALE2) for h in heads]
    sums = [dot(weights[h], value_ref[:, at[h]], (0, 0)) for h in heads]
    total = jnp.zeros((NBR_LEN, HEAD_DIM), F32)
    for h in heads:
        rows = sums[h].astype(BF16)
        out_ref[:, at[h]] = rows
        wide = rows.astype(F32)
        total = total + wide * wide
    squares_ref[pl.ds(n, 1), :] = lanes_of(total)


def self_attention(query, key, value):
    rows, columns = query.shape
    count = rows // NBR_LEN
    block = pl.BlockSpec((NBR_LEN, columns), lambda n: (n, 0))
    return pl.pallas_call(
        self_kernel,
        grid=(count,),
        out_shape=(
            jax.ShapeDtypeStruct((rows, columns), BF16),
            jax.ShapeDtypeStruct((count, NBR_LEN), F32),
        ),
        in_specs=[block, block, block],
        out_specs=(block, pl.BlockSpec((count, NBR_LEN), lambda n: (0, 0))),
        compiler_params=params(SELF_MIB),
        cost_estimate=cost(8000000000, 8 * rows * columns, rows * columns),
        name="self_attention",
    )(query, key, value)


def cross_kernel(first, full_width, self_ref, got_ref, totals_ref, out_ref, squares_ref):
    n = pl.program_id(0)
    count = self_ref.shape[1] // HEAD_DIM
    heads = range(count)
    at = [columns_of(head) for head in heads]
    scale = lax.rsqrt(totals_ref[pl.ds(first + n, 1), :] / full_width + EPSILON) * SCALE2
    keys = [jnp.concatenate([got_ref[h], got_ref[count + h]], axis=0) for h in heads]
    scores = [dot(keys[h], self_ref[:, at[h]], (1, 1)) for h in heads]
    weights = [softmax_down(scores[h], scale) for h in heads]
    values = [jnp.concatenate([got_ref[2 * count + h], got_ref[3 * count + h]], axis=0) for h in heads]
    sums = [dot(weights[h], values[h], (0, 0)) for h in heads]
    total = jnp.zeros((NBR_LEN, HEAD_DIM), F32)
    for h in heads:
        crossed = sums[h].astype(BF16)
        rows = (self_ref[:, at[h]].astype(F32) + crossed.astype(F32)).astype(BF16)
        out_ref[:, at[h]] = rows
        wide = rows.astype(F32)
        total = total + wide * wide
    squares_ref[pl.ds(n, 1), :] = lanes_of(total)


def cross_attention(self_out, got, totals, first, count, full_width):
    columns = self_out.shape[1]
    rows = count * NBR_LEN
    return pl.pallas_call(
        functools.partial(cross_kernel, first, full_width),
        grid=(count,),
        out_shape=(
            jax.ShapeDtypeStruct((rows, columns), BF16),
            jax.ShapeDtypeStruct((count, NBR_LEN), F32),
        ),
        in_specs=[
            pl.BlockSpec((NBR_LEN, columns), lambda n: (first + n, 0)),
            pl.BlockSpec((got.shape[0], HALF, HEAD_DIM), lambda n: (0, first + n, 0)),
            pl.BlockSpec(totals.shape, lambda n: (0, 0)),
        ],
        out_specs=(
            pl.BlockSpec((NBR_LEN, columns), lambda n: (n, 0)),
            pl.BlockSpec((count, NBR_LEN), lambda n: (0, 0)),
        ),
        compiler_params=params(SMALL_MIB),
        cost_estimate=cost(1000000000 * count, 6 * rows * columns, rows * columns // 2),
        name="cross_attention",
    )(self_out, got, totals)


def decode_kernel(full_width, query_ref, came_ref, rest_ref, totals_ref, out_ref, prior_ref):
    u = pl.program_id(0)

    @pl.when(u == 0)
    def _():
        prior_ref[...] = came_ref[...]

    @pl.when(u > 0)
    def _():
        prior_ref[...] = rest_ref[...]

    heads = range(query_ref.shape[1] // HEAD_DIM)
    at = [columns_of(head) for head in heads]
    scale = lax.rsqrt(totals_ref[u] / full_width + EPSILON) * SCALE2
    scores = [dot(query_ref[:, at[h]], prior_ref[:, at[h]], (1, 1)) for h in heads]
    weights = [softmax_across(scores[h] * scale) for h in heads]
    for h in heads:
        out_ref[:, at[h]] = dot(weights[h], prior_ref[:, at[h]], (1, 0)).astype(BF16)


def decode(query, came, rest, totals, full_width):
    columns = query.shape[1]
    panel = NEIGHBOURS * NBR_LEN
    query_block = pl.BlockSpec((SEG_LEN, columns), lambda u: (u, 0))
    return pl.pallas_call(
        functools.partial(decode_kernel, full_width),
        grid=(SEG_DEV,),
        out_shape=jax.ShapeDtypeStruct(query.shape, BF16),
        in_specs=[
            query_block,
            pl.BlockSpec((panel, columns), lambda u: (0, 0)),
            pl.BlockSpec((panel, columns), lambda u: (jnp.maximum(u - 1, 0), 0)),
            pl.BlockSpec((SEG_DEV, 1, panel), lambda u: (0, 0, 0)),
        ],
        out_specs=query_block,
        scratch_shapes=[pltpu.VMEM((panel, columns), BF16)],
        compiler_params=params(SMALL_MIB),
        cost_estimate=cost(4000000000, 4 * query.size + 2 * (came.size + rest.size), query.size * 2),
        name="decode",
    )(query, came, rest, totals.reshape(SEG_DEV, 1, panel))


def over_heads(part):
    heads = lax.axis_size("head")
    total = part
    for step in range(1, heads):
        total = total + lax.ppermute(part, "head", [(i, (i + step) % heads) for i in range(heads)])
    return total


def from_behind(part):
    devices = lax.axis_size("span")
    return lax.ppermute(part, "span", [(i, i + 1) for i in range(devices - 1)])


def exchange(x):
    return lax.all_to_all(x, "span", split_axis=0, concat_axis=0, tiled=True)


def body(
    neighbour_query,
    neighbour_key,
    neighbour_value,
    segment_key,
    segment_value,
    decoder_query,
    sources,
):
    columns = neighbour_query.shape[1]
    full_width = columns * lax.axis_size("head")
    per_device = SEG_DEV * NEIGHBOURS
    table = exchange(pack(sources, segment_key, segment_value))
    self_out, squares = self_attention(neighbour_query, neighbour_key, neighbour_value)
    totals = over_heads(squares)
    table, totals = lax.optimization_barrier((table, totals))
    named = table[:, SEG_DEV * HALF, :per_device].astype(jnp.int32)
    got = exchange(pick(named, table))
    last = per_device - NEIGHBOURS
    panel, panel_squares = cross_attention(self_out, got, totals, last, NEIGHBOURS, full_width)
    came_squares = from_behind(panel_squares)
    came = from_behind(panel)
    rest, rest_squares = cross_attention(self_out, got, totals, 0, last, full_width)
    used = over_heads(jnp.concatenate([came_squares, rest_squares], axis=0))
    return decode(decoder_query, came, rest, used, full_width)


def solution(mesh):
    placed = (
        P("span", "head"),
        P("span", "head"),
        P("span", "head"),
        P("span", "head"),
        P("span", "head"),
        P("span", "head"),
        P("span", None),
    )
    return jax.shard_map(
        body, mesh=mesh, in_specs=placed, out_specs=P("span", "head"), check_vma=False
    )
```

time: 130 us -> 88.1 us (0.68)
  Pallas kernels: 52.1 us -> 22.5 us
  local copies, waits for them, and re-layouts: 14.4 us -> 0.01 us
  blocking collectives: 25.7 us -> 35.8 us
  starting transfers between devices: 28.4 us -> 20.9 us
    unnamed x23 -> x4, local copies, waits for them, and re-layouts: 14.4 us -> 0.01 us
    ppermute x4 -> x0, starting transfers between devices: 13.7 us -> none  [total_from_behind(): came = lax.ppermute(part, ('span', 'head'), pairs)]
    pallas_call x2, Pallas kernels: 18.7 us -> 5.32 us  [cross_attention(): pl.pallas_call(functools.partial(cross_kernel, first, full_width), grid=(...]
    pallas_call x1, Pallas kernels: 18.9 us -> 8.69 us  [self_attention(): pl.pallas_call(self_kernel, grid=(count,), out_shape=(jax.ShapeDtypeStruc...]
    all_to_all x1, blocking collectives: 25.7 us -> 35.8 us  [exchange(): return lax.all_to_all(x, 'span', split_axis=0, concat_axis=0, tiled=True)]
    pallas_call x4 -> x3, Pallas kernels: 14.4 us -> 8.47 us  [the longest x1 3.54 us: pack(): pl.pallas_call(pack_kernel, grid=(steps,), out_shape=jax.ShapeDtypeStruct...]
    all_to_all x1, starting transfers between devices: 4.02 us -> 7.43 us  [exchange(): return lax.all_to_all(x, 'span', split_axis=0, concat_axis=0, tiled=True)]
    ppermute x1 -> x2, starting transfers between devices: 1.31 us -> 4.66 us  [from_behind(): return lax.ppermute(part, 'span', [(i, i + 1) for i in range(devices - 1)])]
  transfers between devices with their start and end apart: 12 -> 9, of which waited for: 4 -> 5; matrix products, arithmetic and copies ran while one was open for 0% -> 1% of each run, Pallas kernels for 32% -> 14%
where the time goes in v2:
time: 88.1 us; the launch traced here: 87.5 us
  blocking collectives  35.8 us (41%)
  Pallas kernels  22.5 us (26%)
  starting transfers between devices  20.9 us (24%)
  waiting for transfers between devices  7.56 us (9%)
    all_to_all x1, blocking collectives, exchange(): return lax.all_to_all(x, 'span', split_axis=0, concat_axis=0, tiled=True)  35.8 us
    ppermute x6, starting transfers between devices, over_heads(): lax.ppermute(part, 'head', [(i, (i + step) % heads) for i in range(heads)])  8.8 us
    pallas_call x1, Pallas kernels, self_attention(): pl.pallas_call(self_kernel, grid=(count,), out_shape=(jax.ShapeDtypeStruc...  8.69 us
    ppermute x6, waiting for transfers between devices, over_heads(): lax.ppermute(part, 'head', [(i, (i + step) % heads) for i in range(heads)])  7.55 us
    all_to_all x1, starting transfers between devices, exchange(): return lax.all_to_all(x, 'span', split_axis=0, concat_axis=0, tiled=True)  7.43 us
    pallas_call x2, Pallas kernels, cross_attention(): pl.pallas_call(functools.partial(cross_kernel, first, full_width), grid=(...  5.32 us
    ppermute x2, starting transfers between devices, from_behind(): return lax.ppermute(part, 'span', [(i, i + 1) for i in range(devices - 1)])  4.66 us
    pallas_call x1, Pallas kernels, pack(): pl.pallas_call(pack_kernel, grid=(steps,), out_shape=jax.ShapeDtypeStruct...  3.54 us
  transfers between devices with their start and end apart: 9, of which 5 were waited for; matrix products, arithmetic and copies ran while one was open for 1% of the time, Pallas kernels for 14%

profile of v2, /device:TPU:0, one launch (start us, length us, event | category | flops | bytes accessed | tf_op | source)
XLA Modules:
  0.0 87.5 jit_solution(4251660011953419431)
XLA Ops:
  0.0 3.5 %pack_stripes.1 = bf16[4,8,136,128]{3,2,1,0:T(8,128)(2,1)} custom-call(s32[2,4]{1,0:T(2,128)} %bitcast.7, bf16[256,1024]{1,0:T(8,128)(2,1)} %key_ref.3, bf16[256,1024]{1,0:T(8,128)(2,1)} %value_ref.3), custom_call_target="tpu_custom_call" | custom-call | flops 1000000 | bytes 2097152 | tf_op jit(solution)/shard_map/pack_stripes/pallas_call | solution.py:66
  3.5 7.4 %all-to-all-start = ((bf16[32,136,128]{2,1,0:T(8,128)(2,1)}), bf16[32,136,128]{2,1,0:T(8,128)(2,1)S(1)}, u32[]{:S(2)}, u32[]{:S(2)}) async-start(bf16[32,136,128]{2,1,0:T(8,128)(2,1)} %bitcast.6), calls=%async_computation | async-start | bytes 2228224 | tf_op jit(solution)/shard_map/all_to_all | solution.py:264
  11.0 8.7 %self_attention.1 = (bf16[1024,1024]{1,0:T(8,128)(2,1)}, f32[8,128]{1,0:T(8,128)}) custom-call(bf16[1024,1024]{1,0:T(8,128)(2,1)} %query_ref.2, bf16[1024,1024]{1,0:T(8,128)(2,1)} %key_ref.2, bf16[1024,1024]{1,0:T(8,128)(2,1)} %value_ref.2), custom_call_target="tpu_custom_call" | custom-call | flops 8000000000 | bytes 8388608 | tf_op jit(solution)/shard_map/self_attention/pallas_call | solution.py:147
  19.7 4.0 %collective-permute-start.2 = (f32[8,128]{1,0:T(8,128)}, f32[8,128]{1,0:T(8,128)S(1)}, u32[]{:S(2)}, u32[]{:S(2)}) collective-permute-start(f32[8,128]{1,0:T(8,128)} %get-tuple-element.14), channel_id=1, source_target_pairs={{0,3},{1,0},{2,1},{3,2},{4,7},{5,4},{6,5},{7,6},{8,11},{9,8},{10,9... | collective-permute-start | bytes 12296 | tf_op jit(solution)/shard_map/ppermute | solution.py:254
  23.7 0.0 collective-permute-start.1
  23.7 1.3 %collective-permute-start = (f32[8,128]{1,0:T(8,128)}, f32[8,128]{1,0:T(8,128)S(1)}, u32[]{:S(2)}, u32[]{:S(2)}) collective-permute-start(f32[8,128]{1,0:T(8,128)} %get-tuple-element.14), channel_id=1, source_target_pairs={{0,1},{1,2},{2,3},{3,0},{4,5},{5,6},{6,7},{7,4},{8,9},{9,10},{10,1... | collective-permute-start | bytes 12296 | tf_op jit(solution)/shard_map/ppermute | solution.py:254
  25.0 0.3 collective-permute-done.2
  25.2 3.8 %collective-permute-done.1 = f32[8,128]{1,0:T(8,128)S(1)} collective-permute-done((f32[8,128]{1,0:T(8,128)}, f32[8,128]{1,0:T(8,128)S(1)}, u32[]{:S(2)}, u32[]{:S(2)}) %collective-permute-start.1) | collective-permute-done | bytes 4128 | tf_op jit(solution)/shard_map/ppermute | solution.py:254
  29.0 0.0 collective-permute-done
  29.0 0.7 add_add_fusion.1.totals_ref
  29.7 0.0 all-to-all-done.table_ref
  29.7 1.6 %pick_stripes.1 = bf16[32,256,128]{2,1,0:T(8,128)(2,1)S(1)} custom-call(s32[32,8]{1,0:T(8,128)S(1)} %bitcast.4, bf16[32,136,128]{2,1,0:T(8,128)(2,1)S(1)} %all-to-all-done.table_ref), custom_call_target="tpu_custom_call" | custom-call | flops 1000000 | bytes 3211264 | tf_op jit(solution)/shard_map/pick_stripes/pallas_call | solution.py:98
  31.3 0.0 copy-start.1
  31.3 35.8 %all_to_all.10.got_ref = bf16[32,256,128]{2,1,0:T(8,128)(2,1)S(1)} all-to-all(bf16[32,256,128]{2,1,0:T(8,128)(2,1)S(1)} %pick_stripes.1), channel_id=1, replica_groups=mesh['span'=32,'head'=4] {'span'}, dimensions={0} | all-to-all | bytes 4194304 | tf_op jit(solution)/shard_map/all_to_all | solution.py:264
  67.1 0.0 copy-done.1
  67.1 1.3 %cross_attention.2 = (bf16[256,1024]{1,0:T(8,128)(2,1)S(1)}, f32[2,128]{1,0:T(2,128)S(1)}) custom-call(bf16[1024,1024]{1,0:T(8,128)(2,1)S(1)} %copy-done.1, bf16[32,256,128]{2,1,0:T(8,128)(2,1)S(1)} %all_to_all.10.got_ref, f32[8,128]{1,0:T(8,128)S(1)} %add_add_fusion.1.totals_ref), custom_call_target="tpu_custom_call" | custom-call | flops 2000000000 | bytes 1572864 | tf_op jit(solution)/shard_map/cross_attention/pallas_call | solution.py:186
  68.4 2.0 %collective-permute-start.4 = (f32[2,128]{1,0:T(2,128)S(1)}, f32[2,128]{1,0:T(2,128)S(1)}, u32[]{:S(2)}, u32[]{:S(2)}) collective-permute-start(f32[2,128]{1,0:T(2,128)S(1)} %get-tuple-element.19), channel_id=1, source_target_pairs={{0,4},{4,8},{8,12},{12,16},{16,20},{20,24},{24,28},{28,32},{32,36}... | collective-permute-start | bytes 3080 | tf_op jit(solution)/shard_map/ppermute | solution.py:260
  70.5 0.0 copy-start
  70.5 2.6 %collective-permute-start.3 = (bf16[256,1024]{1,0:T(8,128)(2,1)S(1)}, bf16[256,1024]{1,0:T(8,128)(2,1)S(1)}, u32[]{:S(2)}, u32[]{:S(2)}) collective-permute-start(bf16[256,1024]{1,0:T(8,128)(2,1)S(1)} %get-tuple-element.17), channel_id=1, source_target_pairs={{0,4},{4,8},{8,12},{12,16},{16,20},{20,24},{24,28},{28,32},{32,36}... | collective-permute-start | bytes 1572872 | tf_op jit(solution)/shard_map/ppermute | solution.py:260
  73.1 4.0 %cross_attention.3 = (bf16[768,1024]{1,0:T(8,128)(2,1)S(1)}, f32[6,128]{1,0:T(8,128)S(1)}) custom-call(bf16[1024,1024]{1,0:T(8,128)(2,1)S(1)} %copy-done.1, bf16[32,256,128]{2,1,0:T(8,128)(2,1)S(1)} %all_to_all.10.got_ref, f32[8,128]{1,0:T(8,128)S(1)} %add_add_fusion.1.totals_ref), custom_call_target="tpu_custom_call" | custom-call | flops 6000000000 | bytes 4718592 | tf_op jit(solution)/shard_map/cross_attention/pallas_call | solution.py:186
  77.1 0.0 collective-permute-done.4
  77.1 0.7 collective-permute-start.7
  77.8 1.5 %collective-permute-start.6 = (f32[8,128]{1,0:T(8,128)S(1)}, f32[8,128]{1,0:T(8,128)S(1)}, u32[]{:S(2)}, u32[]{:S(2)}) collective-permute-start(f32[8,128]{1,0:T(8,128)S(1)} %pad_maximum_fusion), channel_id=1, source_target_pairs={{0,2},{1,3},{2,0},{3,1},{4,6},{5,7},{6,4},{7,5},{8,10},{9,11},{10,... | collective-permute-start | bytes 12296 | tf_op jit(solution)/shard_map/ppermute | solution.py:254
  79.3 1.3 %collective-permute-start.5 = (f32[8,128]{1,0:T(8,128)S(1)}, f32[8,128]{1,0:T(8,128)S(1)}, u32[]{:S(2)}, u32[]{:S(2)}) collective-permute-start(f32[8,128]{1,0:T(8,128)S(1)} %pad_maximum_fusion), channel_id=1, source_target_pairs={{0,1},{1,2},{2,3},{3,0},{4,5},{5,6},{6,7},{7,4},{8,9},{9,10},{10,1... | collective-permute-start | bytes 12296 | tf_op jit(solution)/shard_map/ppermute | solution.py:254
  80.7 0.2 collective-permute-done.7
  80.8 2.1 %collective-permute-done.6 = f32[8,128]{1,0:T(8,128)S(1)} collective-permute-done((f32[8,128]{1,0:T(8,128)S(1)}, f32[8,128]{1,0:T(8,128)S(1)}, u32[]{:S(2)}, u32[]{:S(2)}) %collective-permute-start.6) | collective-permute-done | bytes 4128 | tf_op jit(solution)/shard_map/ppermute | solution.py:254
  82.9 1.2 %collective-permute-done.5 = f32[8,128]{1,0:T(8,128)S(1)} collective-permute-done((f32[8,128]{1,0:T(8,128)S(1)}, f32[8,128]{1,0:T(8,128)S(1)}, u32[]{:S(2)}, u32[]{:S(2)}) %collective-permute-start.5) | collective-permute-done | bytes 4128 | tf_op jit(solution)/shard_map/ppermute | solution.py:254
  84.1 0.0 collective-permute-done.3.came_ref
  84.2 0.0 copy-done
  84.2 3.4 %decode.1 = bf16[256,1024]{1,0:T(8,128)(2,1)} custom-call(bf16[256,1024]{1,0:T(8,128)(2,1)S(1)} %copy-done, bf16[256,1024]{1,0:T(8,128)(2,1)S(1)} %collective-permute-done.3.came_ref, bf16[768,1024]{1,0:T(8,128)(2,1)S(1)} %get-tuple-element.18.rest_ref, f32[4,1,256]{2,1,0:T(1,128)S(1)} %bitcast.5), custom_call_target="tpu_custom_call" | custom-call | flops 4000000000 | bytes 3145728 | tf_op jit(solution)/shard_map/decode/pallas_call | solution.py:232
  (3 shorter events, 0.0 us)
Async XLA Ops:
  3.5 26.2 %all-to-all-start = ((bf16[32,136,128]{2,1,0:T(8,128)(2,1)}), bf16[32,136,128]{2,1,0:T(8,128)(2,1)S(1)}, u32[]{:S(2)}, u32[]{:S(2)}) async-start(bf16[32,136,128]{2,1,0:T(8,128)(2,1)} %bitcast.6), calls=%async_computation | async-start | bytes 2228224 | tf_op jit(solution)/shard_map/all_to_all | solution.py:264
  19.7 5.6 %collective-permute-start.2 = (f32[8,128]{1,0:T(8,128)}, f32[8,128]{1,0:T(8,128)S(1)}, u32[]{:S(2)}, u32[]{:S(2)}) collective-permute-start(f32[8,128]{1,0:T(8,128)} %get-tuple-element.14), channel_id=1, source_target_pairs={{0,3},{1,0},{2,1},{3,2},{4,7},{5,4},{6,5},{7,6},{8,11},{9,8},{10,9... | collective-permute-start | bytes 12296 | tf_op jit(solution)/shard_map/ppermute | solution.py:254
  23.7 5.3 %collective-permute-start.1 = (f32[8,128]{1,0:T(8,128)}, f32[8,128]{1,0:T(8,128)S(1)}, u32[]{:S(2)}, u32[]{:S(2)}) collective-permute-start(f32[8,128]{1,0:T(8,128)} %get-tuple-element.14), channel_id=1, source_target_pairs={{0,2},{1,3},{2,0},{3,1},{4,6},{5,7},{6,4},{7,5},{8,10},{9,11},{10,... | collective-permute-start | bytes 12296 | tf_op jit(solution)/shard_map/ppermute | solution.py:254
  23.7 5.3 %collective-permute-start = (f32[8,128]{1,0:T(8,128)}, f32[8,128]{1,0:T(8,128)S(1)}, u32[]{:S(2)}, u32[]{:S(2)}) collective-permute-start(f32[8,128]{1,0:T(8,128)} %get-tuple-element.14), channel_id=1, source_target_pairs={{0,1},{1,2},{2,3},{3,0},{4,5},{5,6},{6,7},{7,4},{8,9},{9,10},{10,1... | collective-permute-start | bytes 12296 | tf_op jit(solution)/shard_map/ppermute | solution.py:254
  31.3 35.8 %copy-start.1 = (bf16[1024,1024]{1,0:T(8,128)(2,1)S(1)}, bf16[1024,1024]{1,0:T(8,128)(2,1)}, u32[]{:S(2)}) copy-start(bf16[1024,1024]{1,0:T(8,128)(2,1)} %get-tuple-element.13.self_ref) | copy-start | bytes 6291460
  68.4 8.7 %collective-permute-start.4 = (f32[2,128]{1,0:T(2,128)S(1)}, f32[2,128]{1,0:T(2,128)S(1)}, u32[]{:S(2)}, u32[]{:S(2)}) collective-permute-start(f32[2,128]{1,0:T(2,128)S(1)} %get-tuple-element.19), channel_id=1, source_target_pairs={{0,4},{4,8},{8,12},{12,16},{16,20},{20,24},{24,28},{28,32},{32,36}... | collective-permute-start | bytes 3080 | tf_op jit(solution)/shard_map/ppermute | solution.py:260
  70.5 13.7 %copy-start = (bf16[256,1024]{1,0:T(8,128)(2,1)S(1)}, bf16[256,1024]{1,0:T(8,128)(2,1)}, u32[]{:S(2)}) copy-start(bf16[256,1024]{1,0:T(8,128)(2,1)} %query_ref.3) | copy-start | bytes 1572868
  70.5 13.7 %collective-permute-start.3 = (bf16[256,1024]{1,0:T(8,128)(2,1)S(1)}, bf16[256,1024]{1,0:T(8,128)(2,1)S(1)}, u32[]{:S(2)}, u32[]{:S(2)}) collective-permute-start(bf16[256,1024]{1,0:T(8,128)(2,1)S(1)} %get-tuple-element.17), channel_id=1, source_target_pairs={{0,4},{4,8},{8,12},{12,16},{16,20},{20,24},{24,28},{28,32},{32,36}... | collective-permute-start | bytes 1572872 | tf_op jit(solution)/shard_map/ppermute | solution.py:260
  77.1 3.7 %collective-permute-start.7 = (f32[8,128]{1,0:T(8,128)S(1)}, f32[8,128]{1,0:T(8,128)S(1)}, u32[]{:S(2)}, u32[]{:S(2)}) collective-permute-start(f32[8,128]{1,0:T(8,128)S(1)} %pad_maximum_fusion), channel_id=1, source_target_pairs={{0,3},{1,0},{2,1},{3,2},{4,7},{5,4},{6,5},{7,6},{8,11},{9,8},{10,9... | collective-permute-start | bytes 12296 | tf_op jit(solution)/shard_map/ppermute | solution.py:254
  77.8 5.1 %collective-permute-start.6 = (f32[8,128]{1,0:T(8,128)S(1)}, f32[8,128]{1,0:T(8,128)S(1)}, u32[]{:S(2)}, u32[]{:S(2)}) collective-permute-start(f32[8,128]{1,0:T(8,128)S(1)} %pad_maximum_fusion), channel_id=1, source_target_pairs={{0,2},{1,3},{2,0},{3,1},{4,6},{5,7},{6,4},{7,5},{8,10},{9,11},{10,... | collective-permute-start | bytes 12296 | tf_op jit(solution)/shard_map/ppermute | solution.py:254
  79.3 4.8 %collective-permute-start.5 = (f32[8,128]{1,0:T(8,128)S(1)}, f32[8,128]{1,0:T(8,128)S(1)}, u32[]{:S(2)}, u32[]{:S(2)}) collective-permute-start(f32[8,128]{1,0:T(8,128)S(1)} %pad_maximum_fusion), channel_id=1, source_target_pairs={{0,1},{1,2},{2,3},{3,0},{4,5},{5,6},{6,7},{7,4},{8,9},{9,10},{10,1... | collective-permute-start | bytes 12296 | tf_op jit(solution)/shard_map/ppermute | solution.py:254

commit v3 on v2

--- a/solution.py
+++ b/solution.py
@@ -20,6 +20,7 @@
 TAIL = 8
 PACK_MIB = 60
 SELF_MIB = 60
+PICK_MIB = 24
 SMALL_MIB = 24
 
 F32 = jnp.float32
@@ -38,69 +39,105 @@
     return pltpu.CompilerParams(vmem_limit_bytes=mib * 1024 * 1024)
 
 
-def pack_kernel(sources_ref, key_ref, value_ref, out_ref):
+def in_hbm(x):
+    return pltpu.with_memory_space_constraint(x, pltpu.HBM)
+
+
+def pack_kernel(sources_ref, key_ref, value_ref, out_ref, rows_ref, packed_ref, in_sems, out_sems):
     heads = key_ref.shape[1] // HEAD_DIM
+
+    def into(kv, seg):
+        at = pl.ds(seg * SEG_LEN, SEG_LEN)
+        ref = (key_ref, value_ref)[kv]
+        return pltpu.make_async_copy(ref.at[at, :], rows_ref.at[kv, at, :], in_sems.at[kv, seg])
+
+    def out_of(seg):
+        at = pl.ds(seg * HALF, HALF + TAIL if seg == SEG_DEV - 1 else HALF)
+        return pltpu.make_async_copy(packed_ref.at[:, at, :], out_ref.at[:, at, :], out_sems.at[seg])
+
+    for seg in range(SEG_DEV):
+        for kv in range(2):
+            into(kv, seg).start()
     lane = lax.broadcasted_iota(jnp.int32, (TAIL, HEAD_DIM), 1)
     tail = jnp.zeros((TAIL, HEAD_DIM), F32)
     for i in range(SEG_DEV * NEIGHBOURS):
         named = sources_ref[i % NEIGHBOURS, i // NEIGHBOURS].astype(F32)
         tail = jnp.where(lane == i, named, tail)
     tail = tail.astype(BF16)
-    for kv, ref in enumerate((key_ref, value_ref)):
-        for half in range(2):
-            for head in range(heads):
-                for seg in range(SEG_DEV):
-                    row = seg * SEG_LEN + half * HALF
-                    out_ref[kv * 2 + half, head, seg * HALF:(seg + 1) * HALF, :] = ref[
-                        row:row + HALF, head * HEAD_DIM:(head + 1) * HEAD_DIM
+    for stripe in range(4 * heads):
+        packed_ref[stripe, SEG_DEV * HALF:SEG_DEV * HALF + TAIL, :] = tail
+    for seg in range(SEG_DEV):
+        for kv in range(2):
+            into(kv, seg).wait()
+            for half in range(2):
+                row = seg * SEG_LEN + half * HALF
+                for head in range(heads):
+                    packed_ref[(kv * 2 + half) * heads + head, seg * HALF:(seg + 1) * HALF, :] = rows_ref[
+                        kv, row:row + HALF, head * HEAD_DIM:(head + 1) * HEAD_DIM
                     ]
-                out_ref[kv * 2 + half, head, SEG_DEV * HALF:SEG_DEV * HALF + TAIL, :] = tail
+        out_of(seg).start()
+    for seg in range(SEG_DEV):
+        out_of(seg).wait()
 
 
 def pack(sources, segment_key, segment_value):
     rows, columns = segment_key.shape
-    heads = columns // HEAD_DIM
-    long = SEG_DEV * HALF + TAIL
-    steps = 4
-    block = pl.BlockSpec((rows, columns // steps), lambda i: (0, i))
-    out = pl.pallas_call(
+    shape = (4 * columns // HEAD_DIM, SEG_DEV * HALF + TAIL, HEAD_DIM)
+    hbm = pl.BlockSpec(memory_space=pl.ANY)
+    return pl.pallas_call(
         pack_kernel,
-        grid=(steps,),
-        out_shape=jax.ShapeDtypeStruct((4, heads, long, HEAD_DIM), BF16),
-        in_specs=[pl.BlockSpec(memory_space=pltpu.SMEM), block, block],
-        out_specs=pl.BlockSpec((4, heads // steps, long, HEAD_DIM), lambda i: (0, i, 0, 0)),
+        out_shape=jax.ShapeDtypeStruct(shape, BF16),
+        in_specs=[pl.BlockSpec(memory_space=pltpu.SMEM), hbm, hbm],
+        out_specs=hbm,
+        scratch_shapes=[
+            pltpu.VMEM((2, rows, columns), BF16),
+            pltpu.VMEM(shape, BF16),
+            pltpu.SemaphoreType.DMA((2, SEG_DEV)),
+            pltpu.SemaphoreType.DMA((SEG_DEV,)),
+        ],
         compiler_params=params(PACK_MIB),
         cost_estimate=cost(1000000, 2 * 2 * segment_key.size * 2),
         name="pack_stripes",
     )(sources.T, segment_key, segment_value)
-    return out.reshape(4 * heads, long, HEAD_DIM)
 
 
 def pick_kernel(named_ref, table_ref, out_ref):
-    devices = out_ref.shape[0]
+    here = out_ref.shape[0]
+    devices = table_ref.shape[0]
+    first = pl.program_id(0) * here
     count = SEG_DEV * NEIGHBOURS
 
-    def one(device, carry):
+    def one(step, carry):
+        device = first + step
+        behind = lax.rem(device + devices - 1, devices)
         for i in range(count):
-            named = named_ref[device, i]
+            if i < NEIGHBOURS:
+                named = named_ref[behind, count - NEIGHBOURS + i]
+            else:
+                named = named_ref[device, i - NEIGHBOURS]
             owner = lax.shift_right_logical(named, 2)
             within = lax.bitwise_and(named, SEG_DEV - 1)
             start = pl.multiple_of(within * HALF, HALF)
-            out_ref[device, i * HALF:(i + 1) * HALF, :] = table_ref[owner, pl.ds(start, HALF), :]
+            out_ref[step, i * HALF:(i + 1) * HALF, :] = table_ref[owner, pl.ds(start, HALF), :]
         return carry
 
-    lax.fori_loop(0, devices, one, 0, unroll=2)
+    lax.fori_loop(0, here, one, 0, unroll=2)
 
 
 def pick(named, table):
     devices = table.shape[0]
     count = SEG_DEV * NEIGHBOURS
+    steps = 4
     return pl.pallas_call(
         pick_kernel,
+        grid=(steps,),
         out_shape=jax.ShapeDtypeStruct((devices, count * HALF, HEAD_DIM), BF16),
-        in_specs=[pl.BlockSpec(memory_space=pltpu.SMEM), pl.BlockSpec(memory_space=pltpu.VMEM)],
-        out_specs=pl.BlockSpec(memory_space=pltpu.VMEM),
-        compiler_params=params(SMALL_MIB),
+        in_specs=[
+            pl.BlockSpec(memory_space=pltpu.SMEM),
+            pl.BlockSpec(table.shape, lambda i: (0, 0, 0)),
+        ],
+        out_specs=pl.BlockSpec((devices // steps, count * HALF, HEAD_DIM), lambda i: (i, 0, 0)),
+        compiler_params=params(PICK_MIB),
         cost_estimate=cost(1000000, 2 * table.size + 2 * devices * count * HALF * HEAD_DIM),
         name="pick_stripes",
     )(named, table)
@@ -140,10 +177,10 @@
     squares_ref[pl.ds(n, 1), :] = lanes_of(total)
 
 
-def self_attention(query, key, value):
-    rows, columns = query.shape
-    count = rows // NBR_LEN
-    block = pl.BlockSpec((NBR_LEN, columns), lambda n: (n, 0))
+def self_attention(query, key, value, first, count):
+    columns = query.shape[1]
+    rows = count * NBR_LEN
+    block = pl.BlockSpec((NBR_LEN, columns), lambda n: (first + n, 0))
     return pl.pallas_call(
         self_kernel,
         grid=(count,),
@@ -152,9 +189,12 @@
             jax.ShapeDtypeStruct((count, NBR_LEN), F32),
         ),
         in_specs=[block, block, block],
-        out_specs=(block, pl.BlockSpec((count, NBR_LEN), lambda n: (0, 0))),
+        out_specs=(
+            pl.BlockSpec((NBR_LEN, columns), lambda n: (n, 0)),
+            pl.BlockSpec((count, NBR_LEN), lambda n: (0, 0)),
+        ),
         compiler_params=params(SELF_MIB),
-        cost_estimate=cost(8000000000, 8 * rows * columns, rows * columns),
+        cost_estimate=cost(1000000000 * count, 8 * rows * columns, rows * columns),
         name="self_attention",
     )(query, key, value)
 
@@ -180,32 +220,30 @@
     squares_ref[pl.ds(n, 1), :] = lanes_of(total)
 
 
-def cross_attention(self_out, got, totals, first, count, full_width):
-    columns = self_out.shape[1]
-    rows = count * NBR_LEN
+def cross_attention(self_rows, got, totals, first, full_width):
+    rows, columns = self_rows.shape
+    count = rows // NBR_LEN
+    block = pl.BlockSpec((NBR_LEN, columns), lambda n: (n, 0))
     return pl.pallas_call(
         functools.partial(cross_kernel, first, full_width),
         grid=(count,),
         out_shape=(
-            jax.ShapeDtypeStruct((rows, columns), BF16),
+            pltpu.HBM((rows, columns), BF16),
             jax.ShapeDtypeStruct((count, NBR_LEN), F32),
         ),
         in_specs=[
-            pl.BlockSpec((NBR_LEN, columns), lambda n: (first + n, 0)),
+            block,
             pl.BlockSpec((got.shape[0], HALF, HEAD_DIM), lambda n: (0, first + n, 0)),
             pl.BlockSpec(totals.shape, lambda n: (0, 0)),
         ],
-        out_specs=(
-            pl.BlockSpec((NBR_LEN, columns), lambda n: (n, 0)),
-            pl.BlockSpec((count, NBR_LEN), lambda n: (0, 0)),
-        ),
+        out_specs=(block, pl.BlockSpec((count, NBR_LEN), lambda n: (0, 0))),
         compiler_params=params(SMALL_MIB),
         cost_estimate=cost(1000000000 * count, 6 * rows * columns, rows * columns // 2),
         name="cross_attention",
-    )(self_out, got, totals)
-
-
-def decode_kernel(full_width, query_ref, came_ref, rest_ref, totals_ref, out_ref, prior_ref):
+    )(in_hbm(self_rows), got, totals)
+
+
+def decode_kernel(full_width, place_ref, query_ref, came_ref, rest_ref, totals_ref, out_ref, prior_ref):
     u = pl.program_id(0)
 
     @pl.when(u == 0)
@@ -216,16 +254,18 @@
     def _():
         prior_ref[...] = rest_ref[...]
 
+    empty = (u == 0) & (place_ref[0] == 0)
     heads = range(query_ref.shape[1] // HEAD_DIM)
     at = [columns_of(head) for head in heads]
     scale = lax.rsqrt(totals_ref[u] / full_width + EPSILON) * SCALE2
     scores = [dot(query_ref[:, at[h]], prior_ref[:, at[h]], (1, 1)) for h in heads]
     weights = [softmax_across(scores[h] * scale) for h in heads]
     for h in heads:
-        out_ref[:, at[h]] = dot(weights[h], prior_ref[:, at[h]], (1, 0)).astype(BF16)
-
-
-def decode(query, came, rest, totals, full_width):
+        rows = dot(weights[h], prior_ref[:, at[h]], (1, 0))
+        out_ref[:, at[h]] = jnp.where(empty, 0.0, rows).astype(BF16)
+
+
+def decode(place, query, came, rest, totals, full_width):
     columns = query.shape[1]
     panel = NEIGHBOURS * NBR_LEN
     query_block = pl.BlockSpec((SEG_LEN, columns), lambda u: (u, 0))
@@ -234,6 +274,7 @@
         grid=(SEG_DEV,),
         out_shape=jax.ShapeDtypeStruct(query.shape, BF16),
         in_specs=[
+            pl.BlockSpec(memory_space=pltpu.SMEM),
             query_block,
             pl.BlockSpec((panel, columns), lambda u: (0, 0)),
             pl.BlockSpec((panel, columns), lambda u: (jnp.maximum(u - 1, 0), 0)),
@@ -244,7 +285,7 @@
         compiler_params=params(SMALL_MIB),
         cost_estimate=cost(4000000000, 4 * query.size + 2 * (came.size + rest.size), query.size * 2),
         name="decode",
-    )(query, came, rest, totals.reshape(SEG_DEV, 1, panel))
+    )(place, in_hbm(query), in_hbm(came), in_hbm(rest), totals.reshape(SEG_DEV, 1, panel))
 
 
 def over_heads(part):
@@ -276,19 +317,21 @@
     columns = neighbour_query.shape[1]
     full_width = columns * lax.axis_size("head")
     per_device = SEG_DEV * NEIGHBOURS
+    last = per_device - NEIGHBOURS
+    triple = (neighbour_query, neighbour_key, neighbour_value)
     table = exchange(pack(sources, segment_key, segment_value))
-    self_out, squares = self_attention(neighbour_query, neighbour_key, neighbour_value)
-    totals = over_heads(squares)
-    table, totals = lax.optimization_barrier((table, totals))
+    panel, panel_squares = self_attention(*triple, last, NEIGHBOURS)
+    came = from_behind(panel)
+    rest, rest_squares = self_attention(*triple, 0, last)
+    table, came, panel_squares, rest_squares = lax.optimization_barrier((table, came, panel_squares, rest_squares))
     named = table[:, SEG_DEV * HALF, :per_device].astype(jnp.int32)
     got = exchange(pick(named, table))
-    last = per_device - NEIGHBOURS
-    panel, panel_squares = cross_attention(self_out, got, totals, last, NEIGHBOURS, full_width)
-    came_squares = from_behind(panel_squares)
-    came = from_behind(panel)
-    rest, rest_squares = cross_attention(self_out, got, totals, 0, last, full_width)
+    totals = over_heads(jnp.concatenate([from_behind(panel_squares), rest_squares], axis=0))
+    came, came_squares = cross_attention(came, got, totals, 0, full_width)
+    rest, rest_squares = cross_attention(rest, got, totals, NEIGHBOURS, full_width)
     used = over_heads(jnp.concatenate([came_squares, rest_squares], axis=0))
-    return decode(decoder_query, came, rest, used, full_width)
+    place = lax.axis_index("span").astype(jnp.int32).reshape(1)
+    return decode(place, decoder_query, came, rest, used, full_width)
 
 
 def solution(mesh):

time: 88.1 us -> 97.3 us (1.10)
  the two profiles are of different devices: /device:TPU:0 before, /device:TPU:14 now
where the time goes in v3:
time: 97.3 us; the launch traced here: 96.5 us
  waiting for transfers between devices  36.9 us (38%)
  Pallas kernels  30.1 us (31%)
  starting transfers between devices  29.4 us (30%)
    ppermute x2, waiting for transfers between devices, from_behind(): return lax.ppermute(part, 'span', [(i, i + 1) for i in range(devices - 1)])  31.2 us
    all_to_all x2, starting transfers between devices, exchange(): return lax.all_to_all(x, 'span', split_axis=0, concat_axis=0, tiled=True)  14.6 us
    ppermute x6, starting transfers between devices, over_heads(): lax.ppermute(part, 'head', [(i, (i + step) % heads) for i in range(heads)])  10.8 us
    pallas_call x2, Pallas kernels, self_attention(): pl.pallas_call(self_kernel, grid=(count,), out_shape=(jax.ShapeDtypeStruc...  9.92 us
    pallas_call x2, Pallas kernels, cross_attention(): pl.pallas_call(functools.partial(cross_kernel, first, full_width), grid=(...  9 us
    ppermute x6, waiting for transfers between devices, over_heads(): lax.ppermute(part, 'head', [(i, (i + step) % heads) for i in range(heads)])  5.71 us
    pallas_call x1, Pallas kernels, decode(): pl.pallas_call(functools.partial(decode_kernel, full_width), grid=(SEG_DE...  5.15 us
    ppermute x2, starting transfers between devices, from_behind(): return lax.ppermute(part, 'span', [(i, i + 1) for i in range(devices - 1)])  4.04 us
  transfers between devices with their start and end apart: 10, of which 7 were waited for; matrix products, arithmetic and copies ran while one was open for 0% of the time, Pallas kernels for 10%

profile of v3, /device:TPU:14, one launch (start us, length us, event | category | flops | bytes accessed | tf_op | source)
XLA Modules:
  0.0 96.5 jit_solution(15642685795415426471)
XLA Ops:
  0.0 2.9 %pack_stripes.1 = bf16[32,136,128]{2,1,0:T(8,128)(2,1)} custom-call(s32[2,4]{1,0:T(2,128)} %bitcast.6, bf16[256,1024]{1,0:T(8,128)(2,1)} %key_ref.3, bf16[256,1024]{1,0:T(8,128)(2,1)} %value_ref.3), custom_call_target="tpu_custom_call" | custom-call | flops 1000000 | bytes 2097152 | tf_op jit(solution)/shard_map/pack_stripes/pallas_call | solution.py:87
  2.9 7.5 %all-to-all-start = ((bf16[32,136,128]{2,1,0:T(8,128)(2,1)}), bf16[32,136,128]{2,1,0:T(8,128)(2,1)S(1)}, u32[]{:S(2)}, u32[]{:S(2)}) async-start(bf16[32,136,128]{2,1,0:T(8,128)(2,1)} %pack_stripes.1), calls=%async_computation | async-start | bytes 2228224 | tf_op jit(solution)/shard_map/all_to_all | solution.py:305
  10.4 3.1 %self_attention.2 = (bf16[256,1024]{1,0:T(8,128)(2,1)}, f32[2,128]{1,0:T(2,128)}) custom-call(bf16[1024,1024]{1,0:T(8,128)(2,1)} %query_ref.4, bf16[1024,1024]{1,0:T(8,128)(2,1)} %key_ref.5, bf16[1024,1024]{1,0:T(8,128)(2,1)} %value_ref.5), custom_call_target="tpu_custom_call" | custom-call | flops 2000000000 | bytes 2097152 | tf_op jit(solution)/shard_map/self_attention/pallas_call | solution.py:184
  13.5 2.0 %collective-permute-start = (bf16[256,1024]{1,0:T(8,128)(2,1)}, bf16[256,1024]{1,0:T(8,128)(2,1)S(1)}, u32[]{:S(2)}, u32[]{:S(2)}) collective-permute-start(bf16[256,1024]{1,0:T(8,128)(2,1)} %get-tuple-element.17), channel_id=1, source_target_pairs={{0,4},{4,8},{8,12},{12,16},{16,20},{20,24},{24,28},{28,32},{32,36}... | collective-permute-start | bytes 1572872 | tf_op jit(solution)/shard_map/ppermute | solution.py:301
  15.5 6.8 %self_attention.3 = (bf16[768,1024]{1,0:T(8,128)(2,1)}, f32[6,128]{1,0:T(8,128)}) custom-call(bf16[1024,1024]{1,0:T(8,128)(2,1)} %query_ref.4, bf16[1024,1024]{1,0:T(8,128)(2,1)} %key_ref.5, bf16[1024,1024]{1,0:T(8,128)(2,1)} %value_ref.5), custom_call_target="tpu_custom_call" | custom-call | flops 6000000000 | bytes 6291456 | tf_op jit(solution)/shard_map/self_attention/pallas_call | solution.py:184
  22.3 7.5 %collective-permute-done.self_ref = bf16[256,1024]{1,0:T(8,128)(2,1)S(1)} collective-permute-done((bf16[256,1024]{1,0:T(8,128)(2,1)}, bf16[256,1024]{1,0:T(8,128)(2,1)S(1)}, u32[]{:S(2)}, u32[]{:S(2)}) %collective-permute-start) | collective-permute-done | bytes 524320 | tf_op jit(solution)/shard_map/ppermute | solution.py:301
  29.8 0.0 copy-start.1
  29.8 0.0 all-to-all-done.table_ref
  29.9 3.1 %pick_stripes.1 = bf16[32,256,128]{2,1,0:T(8,128)(2,1)} custom-call(s32[32,8]{1,0:T(8,128)S(1)} %bitcast.4, bf16[32,136,128]{2,1,0:T(8,128)(2,1)S(1)} %all-to-all-done.table_ref), custom_call_target="tpu_custom_call" | custom-call | flops 1000000 | bytes 3211264 | tf_op jit(solution)/shard_map/pick_stripes/pallas_call | solution.py:131
  33.0 0.0 copy-start.2
  33.0 0.0 copy-start
  33.0 0.0 copy-done.1
  33.0 7.1 %all-to-all-start.1 = ((bf16[32,256,128]{2,1,0:T(8,128)(2,1)}), bf16[32,256,128]{2,1,0:T(8,128)(2,1)S(1)}, u32[]{:S(2)}, u32[]{:S(2)}) async-start(bf16[32,256,128]{2,1,0:T(8,128)(2,1)} %pick_stripes.1), calls=%async_computation.1 | async-start | bytes 4194304 | tf_op jit(solution)/shard_map/all_to_all | solution.py:305
  40.2 0.0 copy-done.2
  40.2 2.0 %collective-permute-start.1 = (f32[2,128]{1,0:T(2,128)S(1)}, f32[2,128]{1,0:T(2,128)S(1)}, u32[]{:S(2)}, u32[]{:S(2)}) collective-permute-start(f32[2,128]{1,0:T(2,128)S(1)} %copy-done.2), channel_id=1, source_target_pairs={{0,4},{4,8},{8,12},{12,16},{16,20},{20,24},{24,28},{28,32},{32,36}... | collective-permute-start | bytes 3080 | tf_op jit(solution)/shard_map/ppermute | solution.py:301
  42.2 23.6 %collective-permute-done.1 = f32[2,128]{1,0:T(2,128)S(1)} collective-permute-done((f32[2,128]{1,0:T(2,128)S(1)}, f32[2,128]{1,0:T(2,128)S(1)}, u32[]{:S(2)}, u32[]{:S(2)}) %collective-permute-start.1) | collective-permute-done | bytes 1056 | tf_op jit(solution)/shard_map/ppermute | solution.py:301
  65.8 0.0 copy-done
  65.8 2.0 %collective-permute-start.2 = (f32[8,128]{1,0:T(8,128)S(1)}, f32[8,128]{1,0:T(8,128)S(1)}, u32[]{:S(2)}, u32[]{:S(2)}) collective-permute-start(f32[8,128]{1,0:T(8,128)S(1)} %pad_maximum_fusion), channel_id=1, source_target_pairs={{0,1},{1,2},{2,3},{3,0},{4,5},{5,6},{6,7},{7,4},{8,9},{9,10},{10,1... | collective-permute-start | bytes 12296 | tf_op jit(solution)/shard_map/ppermute | solution.py:295
  67.8 3.6 %collective-permute-start.3 = (f32[8,128]{1,0:T(8,128)S(1)}, f32[8,128]{1,0:T(8,128)S(1)}, u32[]{:S(2)}, u32[]{:S(2)}) collective-permute-start(f32[8,128]{1,0:T(8,128)S(1)} %pad_maximum_fusion), channel_id=1, source_target_pairs={{0,2},{1,3},{2,0},{3,1},{4,6},{5,7},{6,4},{7,5},{8,10},{9,11},{10,... | collective-permute-start | bytes 12296 | tf_op jit(solution)/shard_map/ppermute | solution.py:295
  71.4 1.0 %collective-permute-start.4 = (f32[8,128]{1,0:T(8,128)S(1)}, f32[8,128]{1,0:T(8,128)S(1)}, u32[]{:S(2)}, u32[]{:S(2)}) collective-permute-start(f32[8,128]{1,0:T(8,128)S(1)} %pad_maximum_fusion), channel_id=1, source_target_pairs={{0,3},{1,0},{2,1},{3,2},{4,7},{5,4},{6,5},{7,6},{8,11},{9,8},{10,9... | collective-permute-start | bytes 12296 | tf_op jit(solution)/shard_map/ppermute | solution.py:295
  72.4 0.0 collective-permute-done.2
  72.4 0.6 collective-permute-done.3
  73.0 2.0 %collective-permute-done.4 = f32[8,128]{1,0:T(8,128)S(1)} collective-permute-done((f32[8,128]{1,0:T(8,128)S(1)}, f32[8,128]{1,0:T(8,128)S(1)}, u32[]{:S(2)}, u32[]{:S(2)}) %collective-permute-start.4) | collective-permute-done | bytes 4128 | tf_op jit(solution)/shard_map/ppermute | solution.py:295
  75.0 0.0 all-to-all-done.1.got_ref
  75.0 6.1 %cross_attention.3 = (bf16[768,1024]{1,0:T(8,128)(2,1)}, f32[6,128]{1,0:T(8,128)S(1)}) custom-call(bf16[768,1024]{1,0:T(8,128)(2,1)} %get-tuple-element.25.self_ref, bf16[32,256,128]{2,1,0:T(8,128)(2,1)S(1)} %all-to-all-done.1.got_ref, f32[8,128]{1,0:T(8,128)S(1)} %add_add_fusion.1.totals_ref), custom_call_target="tpu_custom_call" | custom-call | flops 6000000000 | bytes 4718592 | tf_op jit(solution)/shard_map/cross_attention/pallas_call | solution.py:227
  81.2 2.9 %cross_attention.2 = (bf16[256,1024]{1,0:T(8,128)(2,1)}, f32[2,128]{1,0:T(2,128)S(1)}) custom-call(bf16[256,1024]{1,0:T(8,128)(2,1)} %copy-done.1, bf16[32,256,128]{2,1,0:T(8,128)(2,1)S(1)} %all-to-all-done.1.got_ref, f32[8,128]{1,0:T(8,128)S(1)} %add_add_fusion.1.totals_ref), custom_call_target="tpu_custom_call" | custom-call | flops 2000000000 | bytes 1572864 | tf_op jit(solution)/shard_map/cross_attention/pallas_call | solution.py:227
  84.1 0.1 collective-permute-start.5
  84.1 3.6 %collective-permute-start.6 = (f32[8,128]{1,0:T(8,128)S(1)}, f32[8,128]{1,0:T(8,128)S(1)}, u32[]{:S(2)}, u32[]{:S(2)}) collective-permute-start(f32[8,128]{1,0:T(8,128)S(1)} %pad_maximum_fusion.1), channel_id=1, source_target_pairs={{0,2},{1,3},{2,0},{3,1},{4,6},{5,7},{6,4},{7,5},{8,10},{9,11},{10,... | collective-permute-start | bytes 12296 | tf_op jit(solution)/shard_map/ppermute | solution.py:295
  87.8 0.5 collective-permute-start.7
  88.3 0.7 collective-permute-done.5
  88.9 0.5 collective-permute-done.6
  89.4 2.0 %collective-permute-done.7 = f32[8,128]{1,0:T(8,128)S(1)} collective-permute-done((f32[8,128]{1,0:T(8,128)S(1)}, f32[8,128]{1,0:T(8,128)S(1)}, u32[]{:S(2)}, u32[]{:S(2)}) %collective-permute-start.7) | collective-permute-done | bytes 4128 | tf_op jit(solution)/shard_map/ppermute | solution.py:295
  91.4 5.1 %decode.1 = bf16[256,1024]{1,0:T(8,128)(2,1)} custom-call(s32[1]{0:T(128)} %bitcast.place_ref, bf16[256,1024]{1,0:T(8,128)(2,1)} %query_ref.5, bf16[256,1024]{1,0:T(8,128)(2,1)} %get-tuple-element.24.came_ref, bf16[768,1024]{1,0:T(8,128)(2,1)} %get-tuple-element.26.rest_ref, f32[4,1,256]{2,1,0:T(1,128)S(1)} %bitcast.5), custom_call_target="tpu_custom_call" | custom-call | flops 4000000000 | bytes 3145728 | tf_op jit(solution)/shard_map/decode/pallas_call | solution.py:272
  (5 shorter events, 0.0 us)
Async XLA Ops:
  2.9 27.0 %all-to-all-start = ((bf16[32,136,128]{2,1,0:T(8,128)(2,1)}), bf16[32,136,128]{2,1,0:T(8,128)(2,1)S(1)}, u32[]{:S(2)}, u32[]{:S(2)}) async-start(bf16[32,136,128]{2,1,0:T(8,128)(2,1)} %pack_stripes.1), calls=%async_computation | async-start | bytes 2228224 | tf_op jit(solution)/shard_map/all_to_all | solution.py:305
  13.5 16.4 %collective-permute-start = (bf16[256,1024]{1,0:T(8,128)(2,1)}, bf16[256,1024]{1,0:T(8,128)(2,1)S(1)}, u32[]{:S(2)}, u32[]{:S(2)}) collective-permute-start(bf16[256,1024]{1,0:T(8,128)(2,1)} %get-tuple-element.17), channel_id=1, source_target_pairs={{0,4},{4,8},{8,12},{12,16},{16,20},{20,24},{24,28},{28,32},{32,36}... | collective-permute-start | bytes 1572872 | tf_op jit(solution)/shard_map/ppermute | solution.py:301
  29.8 3.2 %copy-start.1 = (bf16[256,1024]{1,0:T(8,128)(2,1)}, bf16[256,1024]{1,0:T(8,128)(2,1)S(1)}, u32[]{:S(2)}) copy-start(bf16[256,1024]{1,0:T(8,128)(2,1)S(1)} %collective-permute-done.self_ref) | copy-start | bytes 1572868
  33.0 7.2 %copy-start.2 = (f32[2,128]{1,0:T(2,128)S(1)}, f32[2,128]{1,0:T(2,128)}, u32[]{:S(2)}) copy-start(f32[2,128]{1,0:T(2,128)} %get-tuple-element.22) | copy-start | bytes 3076
  33.0 32.8 %copy-start = (f32[6,128]{1,0:T(8,128)S(1)}, f32[6,128]{1,0:T(8,128)}, u32[]{:S(2)}) copy-start(f32[6,128]{1,0:T(8,128)} %get-tuple-element.23) | copy-start | bytes 9220
  33.0 42.0 %all-to-all-start.1 = ((bf16[32,256,128]{2,1,0:T(8,128)(2,1)}), bf16[32,256,128]{2,1,0:T(8,128)(2,1)S(1)}, u32[]{:S(2)}, u32[]{:S(2)}) async-start(bf16[32,256,128]{2,1,0:T(8,128)(2,1)} %pick_stripes.1), calls=%async_computation.1 | async-start | bytes 4194304 | tf_op jit(solution)/shard_map/all_to_all | solution.py:305
  40.2 25.7 %collective-permute-start.1 = (f32[2,128]{1,0:T(2,128)S(1)}, f32[2,128]{1,0:T(2,128)S(1)}, u32[]{:S(2)}, u32[]{:S(2)}) collective-permute-start(f32[2,128]{1,0:T(2,128)S(1)} %copy-done.2), channel_id=1, source_target_pairs={{0,4},{4,8},{8,12},{12,16},{16,20},{20,24},{24,28},{28,32},{32,36}... | collective-permute-start | bytes 3080 | tf_op jit(solution)/shard_map/ppermute | solution.py:301
  65.8 6.6 %collective-permute-start.2 = (f32[8,128]{1,0:T(8,128)S(1)}, f32[8,128]{1,0:T(8,128)S(1)}, u32[]{:S(2)}, u32[]{:S(2)}) collective-permute-start(f32[8,128]{1,0:T(8,128)S(1)} %pad_maximum_fusion), channel_id=1, source_target_pairs={{0,1},{1,2},{2,3},{3,0},{4,5},{5,6},{6,7},{7,4},{8,9},{9,10},{10,1... | collective-permute-start | bytes 12296 | tf_op jit(solution)/shard_map/ppermute | solution.py:295
  67.8 5.2 %collective-permute-start.3 = (f32[8,128]{1,0:T(8,128)S(1)}, f32[8,128]{1,0:T(8,128)S(1)}, u32[]{:S(2)}, u32[]{:S(2)}) collective-permute-start(f32[8,128]{1,0:T(8,128)S(1)} %pad_maximum_fusion), channel_id=1, source_target_pairs={{0,2},{1,3},{2,0},{3,1},{4,6},{5,7},{6,4},{7,5},{8,10},{9,11},{10,... | collective-permute-start | bytes 12296 | tf_op jit(solution)/shard_map/ppermute | solution.py:295
  71.4 3.6 %collective-permute-start.4 = (f32[8,128]{1,0:T(8,128)S(1)}, f32[8,128]{1,0:T(8,128)S(1)}, u32[]{:S(2)}, u32[]{:S(2)}) collective-permute-start(f32[8,128]{1,0:T(8,128)S(1)} %pad_maximum_fusion), channel_id=1, source_target_pairs={{0,3},{1,0},{2,1},{3,2},{4,7},{5,4},{6,5},{7,6},{8,11},{9,8},{10,9... | collective-permute-start | bytes 12296 | tf_op jit(solution)/shard_map/ppermute | solution.py:295
  84.1 4.9 %collective-permute-start.5 = (f32[8,128]{1,0:T(8,128)S(1)}, f32[8,128]{1,0:T(8,128)S(1)}, u32[]{:S(2)}, u32[]{:S(2)}) collective-permute-start(f32[8,128]{1,0:T(8,128)S(1)} %pad_maximum_fusion.1), channel_id=1, source_target_pairs={{0,1},{1,2},{2,3},{3,0},{4,5},{5,6},{6,7},{7,4},{8,9},{9,10},{10,1... | collective-permute-start | bytes 12296 | tf_op jit(solution)/shard_map/ppermute | solution.py:295
  84.1 5.3 %collective-permute-start.6 = (f32[8,128]{1,0:T(8,128)S(1)}, f32[8,128]{1,0:T(8,128)S(1)}, u32[]{:S(2)}, u32[]{:S(2)}) collective-permute-start(f32[8,128]{1,0:T(8,128)S(1)} %pad_maximum_fusion.1), channel_id=1, source_target_pairs={{0,2},{1,3},{2,0},{3,1},{4,6},{5,7},{6,4},{7,5},{8,10},{9,11},{10,... | collective-permute-start | bytes 12296 | tf_op jit(solution)/shard_map/ppermute | solution.py:295
  87.8 3.6 %collective-permute-start.7 = (f32[8,128]{1,0:T(8,128)S(1)}, f32[8,128]{1,0:T(8,128)S(1)}, u32[]{:S(2)}, u32[]{:S(2)}) collective-permute-start(f32[8,128]{1,0:T(8,128)S(1)} %pad_maximum_fusion.1), channel_id=1, source_target_pairs={{0,3},{1,0},{2,1},{3,2},{4,7},{5,4},{6,5},{7,6},{8,11},{9,8},{10,9... | collective-permute-start | bytes 12296 | tf_op jit(solution)/shard_map/ppermute | solution.py:295

commit v4 on v3

--- a/solution.py
+++ b/solution.py
@@ -7,6 +7,7 @@
 from jax.experimental.pallas import tpu as pltpu
 from jax.sharding import PartitionSpec as P
 
+
 HEAD_DIM = 128
 SEG_LEN = 64
 NBR_LEN = 128
@@ -19,7 +20,7 @@
 HALF = SEG_LEN // 2
 TAIL = 8
 PACK_MIB = 60
-SELF_MIB = 60
+SELF_MIB = 24
 PICK_MIB = 24
 SMALL_MIB = 24
 
@@ -177,7 +178,7 @@
     squares_ref[pl.ds(n, 1), :] = lanes_of(total)
 
 
-def self_attention(query, key, value, first, count):
+def self_attention(query, key, value, first, count, held=jax.ShapeDtypeStruct):
     columns = query.shape[1]
     rows = count * NBR_LEN
     block = pl.BlockSpec((NBR_LEN, columns), lambda n: (first + n, 0))
@@ -185,7 +186,7 @@
         self_kernel,
         grid=(count,),
         out_shape=(
-            jax.ShapeDtypeStruct((rows, columns), BF16),
+            held((rows, columns), BF16),
             jax.ShapeDtypeStruct((count, NBR_LEN), F32),
         ),
         in_specs=[block, block, block],
@@ -196,15 +197,52 @@
         compiler_params=params(SELF_MIB),
         cost_estimate=cost(1000000000 * count, 8 * rows * columns, rows * columns),
         name="self_attention",
-    )(query, key, value)
-
-
-def cross_kernel(first, full_width, self_ref, got_ref, totals_ref, out_ref, squares_ref):
+    )(in_hbm(query), in_hbm(key), in_hbm(value))
+
+
+def squares_kernel(rows_ref, own_ref, squares_ref):
+    for n in range(NEIGHBOURS):
+        total = jnp.zeros((NBR_LEN, HEAD_DIM), F32)
+        for head in range(rows_ref.shape[1] // HEAD_DIM):
+            wide = rows_ref[n * NBR_LEN:(n + 1) * NBR_LEN, columns_of(head)].astype(F32)
+            total = total + wide * wide
+        squares_ref[n:n + 1, :] = lanes_of(total)
+    squares_ref[NEIGHBOURS:, :] = own_ref[...]
+
+
+def squares_above(rows, own):
+    vmem = pl.BlockSpec(memory_space=pltpu.VMEM)
+    return pl.pallas_call(
+        squares_kernel,
+        out_shape=jax.ShapeDtypeStruct((NEIGHBOURS + own.shape[0], NBR_LEN), F32),
+        in_specs=[vmem, vmem],
+        out_specs=vmem,
+        compiler_params=params(SMALL_MIB),
+        cost_estimate=cost(1000000000, 2 * rows.size),
+        name="row_squares",
+    )(rows, own)
+
+
+def summed(refs, at):
+    return functools.reduce(lambda a, b: a + b, [ref[at, :] for ref in refs])
+
+
+def cross_kernel(full_width, came_ref, rest_ref, got_ref, *refs):
+    parts, (out_ref, squares_ref, self_ref) = refs[:-3], refs[-3:]
     n = pl.program_id(0)
+
+    @pl.when(n < NEIGHBOURS)
+    def _():
+        self_ref[...] = came_ref[...]
+
+    @pl.when(n >= NEIGHBOURS)
+    def _():
+        self_ref[...] = rest_ref[...]
+
     count = self_ref.shape[1] // HEAD_DIM
     heads = range(count)
     at = [columns_of(head) for head in heads]
-    scale = lax.rsqrt(totals_ref[pl.ds(first + n, 1), :] / full_width + EPSILON) * SCALE2
+    scale = lax.rsqrt(summed(parts, pl.ds(n, 1)) / full_width + EPSILON) * SCALE2
     keys = [jnp.concatenate([got_ref[h], got_ref[count + h]], axis=0) for h in heads]
     scores = [dot(keys[h], self_ref[:, at[h]], (1, 1)) for h in heads]
     weights = [softmax_down(scores[h], scale) for h in heads]
@@ -220,44 +258,40 @@
     squares_ref[pl.ds(n, 1), :] = lanes_of(total)
 
 
-def cross_attention(self_rows, got, totals, first, full_width):
-    rows, columns = self_rows.shape
-    count = rows // NBR_LEN
-    block = pl.BlockSpec((NBR_LEN, columns), lambda n: (n, 0))
-    return pl.pallas_call(
-        functools.partial(cross_kernel, first, full_width),
+def cross_attention(came, rest, got, parts, full_width):
+    columns = came.shape[1]
+    count = SEG_DEV * NEIGHBOURS
+    rows = count * NBR_LEN
+    sums = pl.BlockSpec((count, NBR_LEN), lambda n: (0, 0))
+    return pl.pallas_call(
+        functools.partial(cross_kernel, full_width),
         grid=(count,),
         out_shape=(
-            pltpu.HBM((rows, columns), BF16),
+            jax.ShapeDtypeStruct((rows, columns), BF16),
             jax.ShapeDtypeStruct((count, NBR_LEN), F32),
         ),
         in_specs=[
-            block,
-            pl.BlockSpec((got.shape[0], HALF, HEAD_DIM), lambda n: (0, first + n, 0)),
-            pl.BlockSpec(totals.shape, lambda n: (0, 0)),
-        ],
-        out_specs=(block, pl.BlockSpec((count, NBR_LEN), lambda n: (0, 0))),
+            pl.BlockSpec((NBR_LEN, columns), lambda n: (jnp.minimum(n, NEIGHBOURS - 1), 0)),
+            pl.BlockSpec((NBR_LEN, columns), lambda n: (jnp.maximum(n - NEIGHBOURS, 0), 0)),
+            pl.BlockSpec((got.shape[0], HALF, HEAD_DIM), lambda n: (0, n, 0)),
+        ]
+        + [sums] * len(parts),
+        out_specs=(pl.BlockSpec((NBR_LEN, columns), lambda n: (n, 0)), sums),
+        scratch_shapes=[pltpu.VMEM((NBR_LEN, columns), BF16)],
         compiler_params=params(SMALL_MIB),
         cost_estimate=cost(1000000000 * count, 6 * rows * columns, rows * columns // 2),
         name="cross_attention",
-    )(in_hbm(self_rows), got, totals)
-
-
-def decode_kernel(full_width, place_ref, query_ref, came_ref, rest_ref, totals_ref, out_ref, prior_ref):
+    )(came, rest, got, *parts)
+
+
+def decode_kernel(full_width, place_ref, query_ref, prior_ref, *refs):
+    parts, out_ref = refs[:-1], refs[-1]
     u = pl.program_id(0)
-
-    @pl.when(u == 0)
-    def _():
-        prior_ref[...] = came_ref[...]
-
-    @pl.when(u > 0)
-    def _():
-        prior_ref[...] = rest_ref[...]
-
     empty = (u == 0) & (place_ref[0] == 0)
     heads = range(query_ref.shape[1] // HEAD_DIM)
     at = [columns_of(head) for head in heads]
-    scale = lax.rsqrt(totals_ref[u] / full_width + EPSILON) * SCALE2
+    totals = [summed(parts, pl.ds(u * NEIGHBOURS + n, 1)) for n in range(NEIGHBOURS)]
+    scale = lax.rsqrt(jnp.concatenate(totals, axis=1) / full_width + EPSILON) * SCALE2
     scores = [dot(query_ref[:, at[h]], prior_ref[:, at[h]], (1, 1)) for h in heads]
     weights = [softmax_across(scores[h] * scale) for h in heads]
     for h in heads:
@@ -265,10 +299,11 @@
         out_ref[:, at[h]] = jnp.where(empty, 0.0, rows).astype(BF16)
 
 
-def decode(place, query, came, rest, totals, full_width):
+def decode(place, query, prior, parts, full_width):
     columns = query.shape[1]
     panel = NEIGHBOURS * NBR_LEN
     query_block = pl.BlockSpec((SEG_LEN, columns), lambda u: (u, 0))
+    sums = pl.BlockSpec(parts[0].shape, lambda u: (0, 0))
     return pl.pallas_call(
         functools.partial(decode_kernel, full_width),
         grid=(SEG_DEV,),
@@ -276,24 +311,22 @@
         in_specs=[
             pl.BlockSpec(memory_space=pltpu.SMEM),
             query_block,
-            pl.BlockSpec((panel, columns), lambda u: (0, 0)),
-            pl.BlockSpec((panel, columns), lambda u: (jnp.maximum(u - 1, 0), 0)),
-            pl.BlockSpec((SEG_DEV, 1, panel), lambda u: (0, 0, 0)),
-        ],
+            pl.BlockSpec((panel, columns), lambda u: (u, 0)),
+        ]
+        + [sums] * len(parts),
         out_specs=query_block,
-        scratch_shapes=[pltpu.VMEM((panel, columns), BF16)],
         compiler_params=params(SMALL_MIB),
-        cost_estimate=cost(4000000000, 4 * query.size + 2 * (came.size + rest.size), query.size * 2),
+        cost_estimate=cost(4000000000, 4 * query.size + 2 * prior.size, query.size * 2),
         name="decode",
-    )(place, in_hbm(query), in_hbm(came), in_hbm(rest), totals.reshape(SEG_DEV, 1, panel))
+    )(place, query, prior, *parts)
 
 
 def over_heads(part):
     heads = lax.axis_size("head")
-    total = part
-    for step in range(1, heads):
-        total = total + lax.ppermute(part, "head", [(i, (i + step) % heads) for i in range(heads)])
-    return total
+    return [part] + [
+        lax.ppermute(part, "head", [(i, (i + step) % heads) for i in range(heads)])
+        for step in range(1, heads)
+    ]
 
 
 def from_behind(part):
@@ -318,20 +351,19 @@
     full_width = columns * lax.axis_size("head")
     per_device = SEG_DEV * NEIGHBOURS
     last = per_device - NEIGHBOURS
+    place = lax.axis_index("span").astype(jnp.int32).reshape(1)
+    sources, place = lax.optimization_barrier((sources, place))
     triple = (neighbour_query, neighbour_key, neighbour_value)
     table = exchange(pack(sources, segment_key, segment_value))
-    panel, panel_squares = self_attention(*triple, last, NEIGHBOURS)
+    panel, _ = self_attention(*triple, last, NEIGHBOURS, pltpu.HBM)
     came = from_behind(panel)
     rest, rest_squares = self_attention(*triple, 0, last)
-    table, came, panel_squares, rest_squares = lax.optimization_barrier((table, came, panel_squares, rest_squares))
+    table, rest_squares = lax.optimization_barrier((table, rest_squares))
     named = table[:, SEG_DEV * HALF, :per_device].astype(jnp.int32)
     got = exchange(pick(named, table))
-    totals = over_heads(jnp.concatenate([from_behind(panel_squares), rest_squares], axis=0))
-    came, came_squares = cross_attention(came, got, totals, 0, full_width)
-    rest, rest_squares = cross_attention(rest, got, totals, NEIGHBOURS, full_width)
-    used = over_heads(jnp.concatenate([came_squares, rest_squares], axis=0))
-    place = lax.axis_index("span").astype(jnp.int32).reshape(1)
-    return decode(place, decoder_query, came, rest, used, full_width)
+    parts = over_heads(squares_above(came, rest_squares))
+    encoded, squares = cross_attention(came, rest, got, parts, full_width)
+    return decode(place, decoder_query, encoded, over_heads(squares), full_width)
 
 
 def solution(mesh):

time: 97.3 us -> 94.7 us (0.973)
  the two profiles are of different devices: /device:TPU:14 before, /device:TPU:24 now
where the time goes in v4:
time: 94.7 us; the launch traced here: 94.3 us
  waiting for transfers between devices  41.1 us (43%)
  starting transfers between devices  26.4 us (28%)
  Pallas kernels  24.1 us (25%)
  local copies, waits for them, and re-layouts  2.56 us (3%)
    ppermute x1, waiting for transfers between devices, from_behind(): return lax.ppermute(part, 'span', [(i, i + 1) for i in range(devices - 1)])  27 us
    all_to_all x2, starting transfers between devices, exchange(): return lax.all_to_all(x, 'span', split_axis=0, concat_axis=0, tiled=True)  13.6 us
    ppermute x6, starting transfers between devices, over_heads(): lax.ppermute(part, 'head', [(i, (i + step) % heads) for i in range(heads)])  10.8 us
    pallas_call x2, Pallas kernels, self_attention(): pl.pallas_call(self_kernel, grid=(count,), out_shape=(held((rows, columns...  9.3 us
    all_to_all x2, waiting for transfers between devices, exchange(): return lax.all_to_all(x, 'span', split_axis=0, concat_axis=0, tiled=True)  8.36 us
    ppermute x6, waiting for transfers between devices, over_heads(): lax.ppermute(part, 'head', [(i, (i + step) % heads) for i in range(heads)])  5.74 us
    pallas_call x1, Pallas kernels, cross_attention(): pl.pallas_call(functools.partial(cross_kernel, full_width), grid=(count,)...  5.48 us
    pallas_call x1, Pallas kernels, decode(): pl.pallas_call(functools.partial(decode_kernel, full_width), grid=(SEG_DE...  3.19 us
  transfers between devices with their start and end apart: 9, of which 7 were waited for; matrix products, arithmetic and copies ran while one was open for 0% of the time, Pallas kernels for 10%

profile of v4, /device:TPU:24, one launch (start us, length us, event | category | flops | bytes accessed | tf_op | source)
XLA Modules:
  0.0 94.3 jit_solution(13902328656883540594)
XLA Ops:
  0.0 2.9 %pack_stripes.1 = bf16[32,136,128]{2,1,0:T(8,128)(2,1)} custom-call(s32[2,4]{1,0:T(2,128)} %bitcast.4, bf16[256,1024]{1,0:T(8,128)(2,1)} %key_ref.5, bf16[256,1024]{1,0:T(8,128)(2,1)} %value_ref.5), custom_call_target="tpu_custom_call" | custom-call | flops 1000000 | bytes 2097152 | tf_op jit(solution)/shard_map/pack_stripes/pallas_call | solution.py:88
  2.9 7.4 %all-to-all-start = ((bf16[32,136,128]{2,1,0:T(8,128)(2,1)}), bf16[32,136,128]{2,1,0:T(8,128)(2,1)S(1)}, u32[]{:S(2)}, u32[]{:S(2)}) async-start(bf16[32,136,128]{2,1,0:T(8,128)(2,1)} %pack_stripes.1), calls=%async_computation | async-start | bytes 2228224 | tf_op jit(solution)/shard_map/all_to_all | solution.py:338
  10.2 6.2 %self_attention.3 = (bf16[768,1024]{1,0:T(8,128)(2,1)S(1)}, f32[6,128]{1,0:T(8,128)S(1)}) custom-call(bf16[1024,1024]{1,0:T(8,128)(2,1)} %query_ref.4, bf16[1024,1024]{1,0:T(8,128)(2,1)} %key_ref.4, bf16[1024,1024]{1,0:T(8,128)(2,1)} %value_ref.4), custom_call_target="tpu_custom_call" | custom-call | flops 6000000000 | bytes 6291456 | tf_op jit(solution)/shard_map/self_attention/pallas_call | solution.py:185
  16.4 0.0 copy-start.1
  16.4 1.1 %copy-done.1 = bf16[768,1024]{1,0:T(8,128)(2,1)} copy-done((bf16[768,1024]{1,0:T(8,128)(2,1)}, bf16[768,1024]{1,0:T(8,128)(2,1)S(1)}, u32[]{:S(2)}) %copy-start.1) | copy-done | bytes 1572888
  17.6 8.4 %all-to-all-done.table_ref = bf16[32,136,128]{2,1,0:T(8,128)(2,1)S(1)} async-done(((bf16[32,136,128]{2,1,0:T(8,128)(2,1)}), bf16[32,136,128]{2,1,0:T(8,128)(2,1)S(1)}, u32[]{:S(2)}, u32[]{:S(2)}) %all-to-all-start) | async-done | bytes 1114144 | tf_op jit(solution)/shard_map/all_to_all | solution.py:338
  26.0 3.1 %pick_stripes.1 = bf16[32,256,128]{2,1,0:T(8,128)(2,1)} custom-call(s32[32,8]{1,0:T(8,128)S(1)} %bitcast.3, bf16[32,136,128]{2,1,0:T(8,128)(2,1)S(1)} %all-to-all-done.table_ref), custom_call_target="tpu_custom_call" | custom-call | flops 1000000 | bytes 3211264 | tf_op jit(solution)/shard_map/pick_stripes/pallas_call | solution.py:132
  29.1 6.2 %all-to-all-start.1 = ((bf16[32,256,128]{2,1,0:T(8,128)(2,1)}), bf16[32,256,128]{2,1,0:T(8,128)(2,1)S(1)}, u32[]{:S(2)}, u32[]{:S(2)}) async-start(bf16[32,256,128]{2,1,0:T(8,128)(2,1)} %pick_stripes.1), calls=%async_computation.1 | async-start | bytes 4194304 | tf_op jit(solution)/shard_map/all_to_all | solution.py:338
  35.3 3.1 %self_attention.2 = (bf16[256,1024]{1,0:T(8,128)(2,1)}, f32[2,128]{1,0:T(2,128)}) custom-call(bf16[1024,1024]{1,0:T(8,128)(2,1)} %query_ref.4, bf16[1024,1024]{1,0:T(8,128)(2,1)} %key_ref.4, bf16[1024,1024]{1,0:T(8,128)(2,1)} %value_ref.4), custom_call_target="tpu_custom_call" | custom-call | flops 2000000000 | bytes 2097152 | tf_op jit(solution)/shard_map/self_attention/pallas_call | solution.py:185
  38.5 2.0 %collective-permute-start = (bf16[256,1024]{1,0:T(8,128)(2,1)}, bf16[256,1024]{1,0:T(8,128)(2,1)S(1)}, u32[]{:S(2)}, u32[]{:S(2)}) collective-permute-start(bf16[256,1024]{1,0:T(8,128)(2,1)} %get-tuple-element.15), channel_id=1, source_target_pairs={{0,4},{4,8},{8,12},{12,16},{16,20},{20,24},{24,28},{28,32},{32,36}... | collective-permute-start | bytes 1572872 | tf_op jit(solution)/shard_map/ppermute | solution.py:334
  40.5 27.0 %collective-permute-done.rows_ref.came_ref = bf16[256,1024]{1,0:T(8,128)(2,1)S(1)} collective-permute-done((bf16[256,1024]{1,0:T(8,128)(2,1)}, bf16[256,1024]{1,0:T(8,128)(2,1)S(1)}, u32[]{:S(2)}, u32[]{:S(2)}) %collective-permute-start) | collective-permute-done | bytes 524320 | tf_op jit(solution)/shard_map/ppermute | solution.py:334
  67.4 0.2 row_squares.1.refs_0_
  67.6 2.0 %collective-permute-start.1 = (f32[8,128]{1,0:T(8,128)S(1)}, f32[8,128]{1,0:T(8,128)S(1)}, u32[]{:S(2)}, u32[]{:S(2)}) collective-permute-start(f32[8,128]{1,0:T(8,128)S(1)} %row_squares.1.refs_0_), channel_id=1, source_target_pairs={{0,1},{1,2},{2,3},{3,0},{4,5},{5,6},{6,7},{7,4},{8,9},{9,10},{10,1... | collective-permute-start | bytes 12296 | tf_op jit(solution)/shard_map/ppermute | solution.py:327
  69.6 3.6 %collective-permute-start.2 = (f32[8,128]{1,0:T(8,128)S(1)}, f32[8,128]{1,0:T(8,128)S(1)}, u32[]{:S(2)}, u32[]{:S(2)}) collective-permute-start(f32[8,128]{1,0:T(8,128)S(1)} %row_squares.1.refs_0_), channel_id=1, source_target_pairs={{0,2},{1,3},{2,0},{3,1},{4,6},{5,7},{6,4},{7,5},{8,10},{9,11},{10,... | collective-permute-start | bytes 12296 | tf_op jit(solution)/shard_map/ppermute | solution.py:327
  73.2 1.0 %collective-permute-start.3 = (f32[8,128]{1,0:T(8,128)S(1)}, f32[8,128]{1,0:T(8,128)S(1)}, u32[]{:S(2)}, u32[]{:S(2)}) collective-permute-start(f32[8,128]{1,0:T(8,128)S(1)} %row_squares.1.refs_0_), channel_id=1, source_target_pairs={{0,3},{1,0},{2,1},{3,2},{4,7},{5,4},{6,5},{7,6},{8,11},{9,8},{10,9... | collective-permute-start | bytes 12296 | tf_op jit(solution)/shard_map/ppermute | solution.py:327
  74.2 0.0 collective-permute-done.1.refs_1_
  74.2 0.6 collective-permute-done.2.refs_2_
  74.8 2.0 %collective-permute-done.3.refs_3_ = f32[8,128]{1,0:T(8,128)S(1)} collective-permute-done((f32[8,128]{1,0:T(8,128)S(1)}, f32[8,128]{1,0:T(8,128)S(1)}, u32[]{:S(2)}, u32[]{:S(2)}) %collective-permute-start.3) | collective-permute-done | bytes 4128 | tf_op jit(solution)/shard_map/ppermute | solution.py:327
  76.8 0.0 all-to-all-done.1.got_ref
  76.8 0.0 copy-start.2
  76.8 1.4 %copy-done.2 = bf16[768,1024]{1,0:T(8,128)(2,1)S(1)} copy-done((bf16[768,1024]{1,0:T(8,128)(2,1)S(1)}, bf16[768,1024]{1,0:T(8,128)(2,1)}, u32[]{:S(2)}) %copy-start.2) | copy-done | bytes 1572888
  78.2 0.0 copy-start
  78.2 5.5 %cross_attention.1 = (bf16[1024,1024]{1,0:T(8,128)(2,1)S(1)}, f32[8,128]{1,0:T(8,128)S(1)}) custom-call(bf16[256,1024]{1,0:T(8,128)(2,1)S(1)} %collective-permute-done.rows_ref.came_ref, bf16[768,1024]{1,0:T(8,128)(2,1)S(1)} %copy-done.2, bf16[32,256,128]{2,1,0:T(8,128)(2,1)S(1)} %all-to-all-done.1.got_ref, f32[8,128]{1,0:T(8,128)S(1)} %row_squares.1.refs_0_, ...), custom_call_target="tpu_custom_call" | custom-call | flops 8000000000 | bytes 6291456 | tf_op jit(solution)/shard_map/cross_attention/pallas_call | solution.py:266
  83.7 0.1 collective-permute-start.4
  83.8 3.7 %collective-permute-start.5 = (f32[8,128]{1,0:T(8,128)S(1)}, f32[8,128]{1,0:T(8,128)S(1)}, u32[]{:S(2)}, u32[]{:S(2)}) collective-permute-start(f32[8,128]{1,0:T(8,128)S(1)} %get-tuple-element.22.refs_0_), channel_id=1, source_target_pairs={{0,2},{1,3},{2,0},{3,1},{4,6},{5,7},{6,4},{7,5},{8,10},{9,11},{10,... | collective-permute-start | bytes 12296 | tf_op jit(solution)/shard_map/ppermute | solution.py:327
  87.4 0.5 collective-permute-start.6
  87.9 0.7 collective-permute-done.4.refs_1_
  88.6 0.5 collective-permute-done.5.refs_2_
  89.1 2.0 %collective-permute-done.6.refs_3_ = f32[8,128]{1,0:T(8,128)S(1)} collective-permute-done((f32[8,128]{1,0:T(8,128)S(1)}, f32[8,128]{1,0:T(8,128)S(1)}, u32[]{:S(2)}, u32[]{:S(2)}) %collective-permute-start.6) | collective-permute-done | bytes 4128 | tf_op jit(solution)/shard_map/ppermute | solution.py:327
  91.1 0.0 copy-done
  91.1 3.2 %decode.1 = bf16[256,1024]{1,0:T(8,128)(2,1)} custom-call(s32[1]{0:T(128)} %bitcast.place_ref, bf16[256,1024]{1,0:T(8,128)(2,1)S(1)} %copy-done, bf16[1024,1024]{1,0:T(8,128)(2,1)S(1)} %get-tuple-element.21.prior_ref, f32[8,128]{1,0:T(8,128)S(1)} %get-tuple-element.22.refs_0_, f32[8,128]{1,0:T(8,128)S(1)} %collective-permute-done.4.refs_1_, ...), custom_call_target="tpu_custom_call" | custom-call | flops 4000000000 | bytes 3145728 | tf_op jit(solution)/shard_map/decode/pallas_call | solution.py:307
  (1 shorter events, 0.0 us)
Async XLA Ops:
  2.9 23.1 %all-to-all-start = ((bf16[32,136,128]{2,1,0:T(8,128)(2,1)}), bf16[32,136,128]{2,1,0:T(8,128)(2,1)S(1)}, u32[]{:S(2)}, u32[]{:S(2)}) async-start(bf16[32,136,128]{2,1,0:T(8,128)(2,1)} %pack_stripes.1), calls=%async_computation | async-start | bytes 2228224 | tf_op jit(solution)/shard_map/all_to_all | solution.py:338
  16.4 1.2 %copy-start.1 = (bf16[768,1024]{1,0:T(8,128)(2,1)}, bf16[768,1024]{1,0:T(8,128)(2,1)S(1)}, u32[]{:S(2)}) copy-start(bf16[768,1024]{1,0:T(8,128)(2,1)S(1)} %get-tuple-element.16.rest_ref) | copy-start | bytes 4718596
  29.1 47.7 %all-to-all-start.1 = ((bf16[32,256,128]{2,1,0:T(8,128)(2,1)}), bf16[32,256,128]{2,1,0:T(8,128)(2,1)S(1)}, u32[]{:S(2)}, u32[]{:S(2)}) async-start(bf16[32,256,128]{2,1,0:T(8,128)(2,1)} %pick_stripes.1), calls=%async_computation.1 | async-start | bytes 4194304 | tf_op jit(solution)/shard_map/all_to_all | solution.py:338
  38.5 29.0 %collective-permute-start = (bf16[256,1024]{1,0:T(8,128)(2,1)}, bf16[256,1024]{1,0:T(8,128)(2,1)S(1)}, u32[]{:S(2)}, u32[]{:S(2)}) collective-permute-start(bf16[256,1024]{1,0:T(8,128)(2,1)} %get-tuple-element.15), channel_id=1, source_target_pairs={{0,4},{4,8},{8,12},{12,16},{16,20},{20,24},{24,28},{28,32},{32,36}... | collective-permute-start | bytes 1572872 | tf_op jit(solution)/shard_map/ppermute | solution.py:334
  67.6 6.6 %collective-permute-start.1 = (f32[8,128]{1,0:T(8,128)S(1)}, f32[8,128]{1,0:T(8,128)S(1)}, u32[]{:S(2)}, u32[]{:S(2)}) collective-permute-start(f32[8,128]{1,0:T(8,128)S(1)} %row_squares.1.refs_0_), channel_id=1, source_target_pairs={{0,1},{1,2},{2,3},{3,0},{4,5},{5,6},{6,7},{7,4},{8,9},{9,10},{10,1... | collective-permute-start | bytes 12296 | tf_op jit(solution)/shard_map/ppermute | solution.py:327
  69.6 5.2 %collective-permute-start.2 = (f32[8,128]{1,0:T(8,128)S(1)}, f32[8,128]{1,0:T(8,128)S(1)}, u32[]{:S(2)}, u32[]{:S(2)}) collective-permute-start(f32[8,128]{1,0:T(8,128)S(1)} %row_squares.1.refs_0_), channel_id=1, source_target_pairs={{0,2},{1,3},{2,0},{3,1},{4,6},{5,7},{6,4},{7,5},{8,10},{9,11},{10,... | collective-permute-start | bytes 12296 | tf_op jit(solution)/shard_map/ppermute | solution.py:327
  73.2 3.6 %collective-permute-start.3 = (f32[8,128]{1,0:T(8,128)S(1)}, f32[8,128]{1,0:T(8,128)S(1)}, u32[]{:S(2)}, u32[]{:S(2)}) collective-permute-start(f32[8,128]{1,0:T(8,128)S(1)} %row_squares.1.refs_0_), channel_id=1, source_target_pairs={{0,3},{1,0},{2,1},{3,2},{4,7},{5,4},{6,5},{7,6},{8,11},{9,8},{10,9... | collective-permute-start | bytes 12296 | tf_op jit(solution)/shard_map/ppermute | solution.py:327
  76.8 1.4 %copy-start.2 = (bf16[768,1024]{1,0:T(8,128)(2,1)S(1)}, bf16[768,1024]{1,0:T(8,128)(2,1)}, u32[]{:S(2)}) copy-start(bf16[768,1024]{1,0:T(8,128)(2,1)} %copy-done.1) | copy-start | bytes 4718596
  78.2 12.8 %copy-start = (bf16[256,1024]{1,0:T(8,128)(2,1)S(1)}, bf16[256,1024]{1,0:T(8,128)(2,1)}, u32[]{:S(2)}) copy-start(bf16[256,1024]{1,0:T(8,128)(2,1)} %query_ref.5) | copy-start | bytes 1572868
  83.7 4.9 %collective-permute-start.4 = (f32[8,128]{1,0:T(8,128)S(1)}, f32[8,128]{1,0:T(8,128)S(1)}, u32[]{:S(2)}, u32[]{:S(2)}) collective-permute-start(f32[8,128]{1,0:T(8,128)S(1)} %get-tuple-element.22.refs_0_), channel_id=1, source_target_pairs={{0,1},{1,2},{2,3},{3,0},{4,5},{5,6},{6,7},{7,4},{8,9},{9,10},{10,1... | collective-permute-start | bytes 12296 | tf_op jit(solution)/shard_map/ppermute | solution.py:327
  83.8 5.3 %collective-permute-start.5 = (f32[8,128]{1,0:T(8,128)S(1)}, f32[8,128]{1,0:T(8,128)S(1)}, u32[]{:S(2)}, u32[]{:S(2)}) collective-permute-start(f32[8,128]{1,0:T(8,128)S(1)} %get-tuple-element.22.refs_0_), channel_id=1, source_target_pairs={{0,2},{1,3},{2,0},{3,1},{4,6},{5,7},{6,4},{7,5},{8,10},{9,11},{10,... | collective-permute-start | bytes 12296 | tf_op jit(solution)/shard_map/ppermute | solution.py:327
  87.4 3.6 %collective-permute-start.6 = (f32[8,128]{1,0:T(8,128)S(1)}, f32[8,128]{1,0:T(8,128)S(1)}, u32[]{:S(2)}, u32[]{:S(2)}) collective-permute-start(f32[8,128]{1,0:T(8,128)S(1)} %get-tuple-element.22.refs_0_), channel_id=1, source_target_pairs={{0,3},{1,0},{2,1},{3,2},{4,7},{5,4},{6,5},{7,6},{8,11},{9,8},{10,9... | collective-permute-start | bytes 12296 | tf_op jit(solution)/shard_map/ppermute | solution.py:327

commit v5 on v4

--- a/solution.py
+++ b/solution.py
@@ -102,44 +102,49 @@
     )(sources.T, segment_key, segment_value)
 
 
-def pick_kernel(named_ref, table_ref, out_ref):
-    here = out_ref.shape[0]
+def pick_kernel(named_ref, table_ref, out_ref, picked_ref, sems):
     devices = table_ref.shape[0]
-    first = pl.program_id(0) * here
+    groups = sems.shape[0]
+    here = devices // groups
     count = SEG_DEV * NEIGHBOURS
 
-    def one(step, carry):
-        device = first + step
-        behind = lax.rem(device + devices - 1, devices)
-        for i in range(count):
-            if i < NEIGHBOURS:
-                named = named_ref[behind, count - NEIGHBOURS + i]
-            else:
-                named = named_ref[device, i - NEIGHBOURS]
-            owner = lax.shift_right_logical(named, 2)
-            within = lax.bitwise_and(named, SEG_DEV - 1)
-            start = pl.multiple_of(within * HALF, HALF)
-            out_ref[step, i * HALF:(i + 1) * HALF, :] = table_ref[owner, pl.ds(start, HALF), :]
+    def out_of(group):
+        at = pl.ds(group * here, here)
+        return pltpu.make_async_copy(picked_ref.at[at], out_ref.at[at], sems.at[group])
+
+    def one(group, carry):
+        for step in range(here):
+            device = group * here + step
+            behind = lax.rem(device + devices - 1, devices)
+            for i in range(count):
+                if i < NEIGHBOURS:
+                    named = named_ref[behind, count - NEIGHBOURS + i]
+                else:
+                    named = named_ref[device, i - NEIGHBOURS]
+                owner = lax.shift_right_logical(named, 2)
+                within = lax.bitwise_and(named, SEG_DEV - 1)
+                start = pl.multiple_of(within * HALF, HALF)
+                picked_ref[device, i * HALF:(i + 1) * HALF, :] = table_ref[owner, pl.ds(start, HALF), :]
+        out_of(group).start()
         return carry
 
-    lax.fori_loop(0, here, one, 0, unroll=2)
+    lax.fori_loop(0, groups, one, 0)
+    for group in range(groups):
+        out_of(group).wait()
 
 
 def pick(named, table):
     devices = table.shape[0]
-    count = SEG_DEV * NEIGHBOURS
-    steps = 4
+    shape = (devices, SEG_DEV * NEIGHBOURS * HALF, HEAD_DIM)
+    groups = 8
     return pl.pallas_call(
         pick_kernel,
-        grid=(steps,),
-        out_shape=jax.ShapeDtypeStruct((devices, count * HALF, HEAD_DIM), BF16),
-        in_specs=[
-            pl.BlockSpec(memory_space=pltpu.SMEM),
-            pl.BlockSpec(table.shape, lambda i: (0, 0, 0)),
-        ],
-        out_specs=pl.BlockSpec((devices // steps, count * HALF, HEAD_DIM), lambda i: (i, 0, 0)),
+        out_shape=jax.ShapeDtypeStruct(shape, BF16),
+        in_specs=[pl.BlockSpec(memory_space=pltpu.SMEM), pl.BlockSpec(memory_space=pltpu.VMEM)],
+        out_specs=pl.BlockSpec(memory_space=pl.ANY),
+        scratch_shapes=[pltpu.VMEM(shape, BF16), pltpu.SemaphoreType.DMA((groups,))],
         compiler_params=params(PICK_MIB),
-        cost_estimate=cost(1000000, 2 * table.size + 2 * devices * count * HALF * HEAD_DIM),
+        cost_estimate=cost(1000000, 2 * table.size + 2 * devices * shape[1] * HEAD_DIM),
         name="pick_stripes",
     )(named, table)
 
@@ -162,8 +167,9 @@
     return (weights * (1.0 / jnp.sum(weights, axis=1, keepdims=True))).astype(BF16)
 
 
-def self_kernel(query_ref, key_ref, value_ref, out_ref, squares_ref):
+def self_kernel(query_ref, key_ref, value_ref, rest_ref, panel_ref, squares_ref, held_ref):
     n = pl.program_id(0)
+    last = pl.num_programs(0) - NEIGHBOURS
     heads = range(query_ref.shape[1] // HEAD_DIM)
     at = [columns_of(head) for head in heads]
     scores = [dot(key_ref[:, at[h]], query_ref[:, at[h]], (1, 1)) for h in heads]
@@ -172,30 +178,42 @@
     total = jnp.zeros((NBR_LEN, HEAD_DIM), F32)
     for h in heads:
         rows = sums[h].astype(BF16)
-        out_ref[:, at[h]] = rows
+        held_ref[:, at[h]] = rows
         wide = rows.astype(F32)
         total = total + wide * wide
-    squares_ref[pl.ds(n, 1), :] = lanes_of(total)
-
-
-def self_attention(query, key, value, first, count, held=jax.ShapeDtypeStruct):
+
+    @pl.when(n < last)
+    def _():
+        rest_ref[...] = held_ref[...]
+        squares_ref[pl.ds(n, 1), :] = lanes_of(total)
+
+    @pl.when(n >= last)
+    def _():
+        panel_ref[...] = held_ref[...]
+
+
+def self_attention(query, key, value):
     columns = query.shape[1]
-    rows = count * NBR_LEN
-    block = pl.BlockSpec((NBR_LEN, columns), lambda n: (first + n, 0))
+    count = query.shape[0] // NBR_LEN
+    last = count - NEIGHBOURS
+    block = pl.BlockSpec((NBR_LEN, columns), lambda n: (n, 0))
     return pl.pallas_call(
         self_kernel,
         grid=(count,),
         out_shape=(
-            held((rows, columns), BF16),
-            jax.ShapeDtypeStruct((count, NBR_LEN), F32),
+            pltpu.HBM((last * NBR_LEN, columns), BF16),
+            pltpu.HBM((NEIGHBOURS * NBR_LEN, columns), BF16),
+            jax.ShapeDtypeStruct((last, NBR_LEN), F32),
         ),
         in_specs=[block, block, block],
         out_specs=(
-            pl.BlockSpec((NBR_LEN, columns), lambda n: (n, 0)),
-            pl.BlockSpec((count, NBR_LEN), lambda n: (0, 0)),
+            pl.BlockSpec((NBR_LEN, columns), lambda n: (jnp.minimum(n, last - 1), 0)),
+            pl.BlockSpec((NBR_LEN, columns), lambda n: (jnp.maximum(n - last, 0), 0)),
+            pl.BlockSpec((last, NBR_LEN), lambda n: (0, 0)),
         ),
+        scratch_shapes=[pltpu.VMEM((NBR_LEN, columns), BF16)],
         compiler_params=params(SELF_MIB),
-        cost_estimate=cost(1000000000 * count, 8 * rows * columns, rows * columns),
+        cost_estimate=cost(1000000000 * count, 8 * query.size, query.size),
         name="self_attention",
     )(in_hbm(query), in_hbm(key), in_hbm(value))
 
@@ -229,55 +247,70 @@
 
 def cross_kernel(full_width, came_ref, rest_ref, got_ref, *refs):
     parts, (out_ref, squares_ref, self_ref) = refs[:-3], refs[-3:]
-    n = pl.program_id(0)
-
-    @pl.when(n < NEIGHBOURS)
+    step = pl.program_id(0)
+
+    came_steps = NEIGHBOURS * NBR_LEN // self_ref.shape[0]
+
+    @pl.when(step < came_steps)
     def _():
         self_ref[...] = came_ref[...]
 
-    @pl.when(n >= NEIGHBOURS)
+    @pl.when(step >= came_steps)
     def _():
         self_ref[...] = rest_ref[...]
 
-    count = self_ref.shape[1] // HEAD_DIM
-    heads = range(count)
-    at = [columns_of(head) for head in heads]
-    scale = lax.rsqrt(summed(parts, pl.ds(n, 1)) / full_width + EPSILON) * SCALE2
-    keys = [jnp.concatenate([got_ref[h], got_ref[count + h]], axis=0) for h in heads]
-    scores = [dot(keys[h], self_ref[:, at[h]], (1, 1)) for h in heads]
-    weights = [softmax_down(scores[h], scale) for h in heads]
-    values = [jnp.concatenate([got_ref[2 * count + h], got_ref[3 * count + h]], axis=0) for h in heads]
-    sums = [dot(weights[h], values[h], (0, 0)) for h in heads]
-    total = jnp.zeros((NBR_LEN, HEAD_DIM), F32)
-    for h in heads:
-        crossed = sums[h].astype(BF16)
-        rows = (self_ref[:, at[h]].astype(F32) + crossed.astype(F32)).astype(BF16)
-        out_ref[:, at[h]] = rows
+    here = self_ref.shape[0] // NBR_LEN
+    heads = self_ref.shape[1] // HEAD_DIM
+    each = [(i, h) for i in range(here) for h in range(heads)]
+    rows_of = [slice(i * NBR_LEN, (i + 1) * NBR_LEN) for i in range(here)]
+    at = [columns_of(head) for head in range(heads)]
+    scales = [
+        lax.rsqrt(summed(parts, pl.ds(step * here + i, 1)) / full_width + EPSILON) * SCALE2
+        for i in range(here)
+    ]
+
+    def whole(kv, i, h):
+        slot = slice(i * HALF, (i + 1) * HALF)
+        return jnp.concatenate(
+            [got_ref[(2 * kv + half) * heads + h, slot, :] for half in range(2)], axis=0
+        )
+
+    scores = [dot(whole(0, i, h), self_ref[rows_of[i], at[h]], (1, 1)) for i, h in each]
+    weights = [softmax_down(score, scales[i]) for score, (i, h) in zip(scores, each)]
+    sums = [dot(weight, whole(1, i, h), (0, 0)) for weight, (i, h) in zip(weights, each)]
+    totals = [jnp.zeros((NBR_LEN, HEAD_DIM), F32) for _ in range(here)]
+    for crossed, (i, h) in zip(sums, each):
+        own = self_ref[rows_of[i], at[h]].astype(F32)
+        rows = (own + crossed.astype(BF16).astype(F32)).astype(BF16)
+        out_ref[rows_of[i], at[h]] = rows
         wide = rows.astype(F32)
-        total = total + wide * wide
-    squares_ref[pl.ds(n, 1), :] = lanes_of(total)
-
-
-def cross_attention(came, rest, got, parts, full_width):
+        totals[i] = totals[i] + wide * wide
+    for i in range(here):
+        squares_ref[pl.ds(step * here + i, 1), :] = lanes_of(totals[i])
+
+
+def cross_attention(came, rest, got, parts, full_width, here=NEIGHBOURS):
     columns = came.shape[1]
     count = SEG_DEV * NEIGHBOURS
     rows = count * NBR_LEN
+    first = NEIGHBOURS // here
+    block = (here * NBR_LEN, columns)
     sums = pl.BlockSpec((count, NBR_LEN), lambda n: (0, 0))
     return pl.pallas_call(
         functools.partial(cross_kernel, full_width),
-        grid=(count,),
+        grid=(count // here,),
         out_shape=(
             jax.ShapeDtypeStruct((rows, columns), BF16),
             jax.ShapeDtypeStruct((count, NBR_LEN), F32),
         ),
         in_specs=[
-            pl.BlockSpec((NBR_LEN, columns), lambda n: (jnp.minimum(n, NEIGHBOURS - 1), 0)),
-            pl.BlockSpec((NBR_LEN, columns), lambda n: (jnp.maximum(n - NEIGHBOURS, 0), 0)),
-            pl.BlockSpec((got.shape[0], HALF, HEAD_DIM), lambda n: (0, n, 0)),
+            pl.BlockSpec(block, lambda n: (jnp.minimum(n, first - 1), 0)),
+            pl.BlockSpec(block, lambda n: (jnp.maximum(n - first, 0), 0)),
+            pl.BlockSpec((got.shape[0], here * HALF, HEAD_DIM), lambda n: (0, n, 0)),
         ]
         + [sums] * len(parts),
-        out_specs=(pl.BlockSpec((NBR_LEN, columns), lambda n: (n, 0)), sums),
-        scratch_shapes=[pltpu.VMEM((NBR_LEN, columns), BF16)],
+        out_specs=(pl.BlockSpec(block, lambda n: (n, 0)), sums),
+        scratch_shapes=[pltpu.VMEM(block, BF16)],
         compiler_params=params(SMALL_MIB),
         cost_estimate=cost(1000000000 * count, 6 * rows * columns, rows * columns // 2),
         name="cross_attention",
@@ -286,32 +319,42 @@
 
 def decode_kernel(full_width, place_ref, query_ref, prior_ref, *refs):
     parts, out_ref = refs[:-1], refs[-1]
-    u = pl.program_id(0)
-    empty = (u == 0) & (place_ref[0] == 0)
-    heads = range(query_ref.shape[1] // HEAD_DIM)
-    at = [columns_of(head) for head in heads]
-    totals = [summed(parts, pl.ds(u * NEIGHBOURS + n, 1)) for n in range(NEIGHBOURS)]
-    scale = lax.rsqrt(jnp.concatenate(totals, axis=1) / full_width + EPSILON) * SCALE2
-    scores = [dot(query_ref[:, at[h]], prior_ref[:, at[h]], (1, 1)) for h in heads]
-    weights = [softmax_across(scores[h] * scale) for h in heads]
-    for h in heads:
-        rows = dot(weights[h], prior_ref[:, at[h]], (1, 0))
-        out_ref[:, at[h]] = jnp.where(empty, 0.0, rows).astype(BF16)
-
-
-def decode(place, query, prior, parts, full_width):
+    step = pl.program_id(0)
+    panel = NEIGHBOURS * NBR_LEN
+    here = query_ref.shape[0] // SEG_LEN
+    each = [(i, h) for i in range(here) for h in range(query_ref.shape[1] // HEAD_DIM)]
+    asks = [slice(i * SEG_LEN, (i + 1) * SEG_LEN) for i in range(here)]
+    reads = [slice(i * panel, (i + 1) * panel) for i in range(here)]
+
+    def scale_of(i):
+        first = (step * here + i) * NEIGHBOURS
+        totals = [summed(parts, pl.ds(first + n, 1)) for n in range(NEIGHBOURS)]
+        return lax.rsqrt(jnp.concatenate(totals, axis=1) / full_width + EPSILON) * SCALE2
+
+    scales = [scale_of(i) for i in range(here)]
+    empty = (step == 0) & (place_ref[0] == 0)
+    scores = [dot(query_ref[asks[i], columns_of(h)], prior_ref[reads[i], columns_of(h)], (1, 1)) for i, h in each]
+    weights = [softmax_across(score * scales[i]) for score, (i, h) in zip(scores, each)]
+    for weight, (i, h) in zip(weights, each):
+        rows = dot(weight, prior_ref[reads[i], columns_of(h)], (1, 0))
+        if i == 0:
+            rows = jnp.where(empty, 0.0, rows)
+        out_ref[asks[i], columns_of(h)] = rows.astype(BF16)
+
+
+def decode(place, query, prior, parts, full_width, here=2):
     columns = query.shape[1]
     panel = NEIGHBOURS * NBR_LEN
-    query_block = pl.BlockSpec((SEG_LEN, columns), lambda u: (u, 0))
+    query_block = pl.BlockSpec((here * SEG_LEN, columns), lambda u: (u, 0))
     sums = pl.BlockSpec(parts[0].shape, lambda u: (0, 0))
     return pl.pallas_call(
         functools.partial(decode_kernel, full_width),
-        grid=(SEG_DEV,),
+        grid=(SEG_DEV // here,),
         out_shape=jax.ShapeDtypeStruct(query.shape, BF16),
         in_specs=[
             pl.BlockSpec(memory_space=pltpu.SMEM),
             query_block,
-            pl.BlockSpec((panel, columns), lambda u: (u, 0)),
+            pl.BlockSpec((here * panel, columns), lambda u: (u, 0)),
         ]
         + [sums] * len(parts),
         out_specs=query_block,
@@ -350,19 +393,16 @@
     columns = neighbour_query.shape[1]
     full_width = columns * lax.axis_size("head")
     per_device = SEG_DEV * NEIGHBOURS
-    last = per_device - NEIGHBOURS
     place = lax.axis_index("span").astype(jnp.int32).reshape(1)
     sources, place = lax.optimization_barrier((sources, place))
-    triple = (neighbour_query, neighbour_key, neighbour_value)
     table = exchange(pack(sources, segment_key, segment_value))
-    panel, _ = self_attention(*triple, last, NEIGHBOURS, pltpu.HBM)
+    rest, panel, rest_squares = self_attention(neighbour_query, neighbour_key, neighbour_value)
     came = from_behind(panel)
-    rest, rest_squares = self_attention(*triple, 0, last)
     table, rest_squares = lax.optimization_barrier((table, rest_squares))
     named = table[:, SEG_DEV * HALF, :per_device].astype(jnp.int32)
     got = exchange(pick(named, table))
     parts = over_heads(squares_above(came, rest_squares))
-    encoded, squares = cross_attention(came, rest, got, parts, full_width)
+    encoded, squares = cross_attention(came, in_hbm(rest), got, parts, full_width)
     return decode(place, decoder_query, encoded, over_heads(squares), full_width)
 
 

time: 94.7 us -> 91.6 us (0.967)
  local copies, waits for them, and re-layouts: 2.56 us -> 0.01 us
  Pallas kernels: 24.1 us -> 21.9 us
  waiting for transfers between devices: 41.1 us -> 42.5 us
    ppermute x1, waiting for transfers between devices: 27 us -> 30.1 us  [from_behind(): return lax.ppermute(part, 'span', [(i, i + 1) for i in range(devices - 1)])]
    unnamed x6 -> x4, local copies, waits for them, and re-layouts: 2.56 us -> 0.01 us
    all_to_all x2, waiting for transfers between devices: 8.36 us -> 6.67 us  [exchange(): return lax.all_to_all(x, 'span', split_axis=0, concat_axis=0, tiled=True)]
    pallas_call x4 -> x3, Pallas kernels: 17.9 us -> 16.4 us  [the longest x1 9.04 us: self_attention(): pl.pallas_call(self_kernel, grid=(count,), out_shape=(pltpu.HBM((last * N...]
where the time goes in v5:
time: 91.6 us; the launch traced here: 91 us
  waiting for transfers between devices  42.5 us (46%)
  starting transfers between devices  26.5 us (29%)
  Pallas kernels  21.9 us (24%)
    ppermute x1, waiting for transfers between devices, from_behind(): return lax.ppermute(part, 'span', [(i, i + 1) for i in range(devices - 1)])  30.1 us
    all_to_all x2, starting transfers between devices, exchange(): return lax.all_to_all(x, 'span', split_axis=0, concat_axis=0, tiled=True)  13.7 us
    ppermute x6, starting transfers between devices, over_heads(): lax.ppermute(part, 'head', [(i, (i + step) % heads) for i in range(heads)])  10.8 us
    pallas_call x1, Pallas kernels, self_attention(): pl.pallas_call(self_kernel, grid=(count,), out_shape=(pltpu.HBM((last * N...  9.04 us
    all_to_all x2, waiting for transfers between devices, exchange(): return lax.all_to_all(x, 'span', split_axis=0, concat_axis=0, tiled=True)  6.67 us
    ppermute x6, waiting for transfers between devices, over_heads(): lax.ppermute(part, 'head', [(i, (i + step) % heads) for i in range(heads)])  5.73 us
    pallas_call x1, Pallas kernels, cross_attention(): pl.pallas_call(functools.partial(cross_kernel, full_width), grid=(count /...  4.97 us
    pallas_call x1, Pallas kernels, pack(): pl.pallas_call(pack_kernel, out_shape=jax.ShapeDtypeStruct(shape, BF16),...  2.88 us
  transfers between devices with their start and end apart: 9, of which 7 were waited for; matrix products, arithmetic and copies ran while one was open for 0% of the time, Pallas kernels for 10%

profile of v5, /device:TPU:24, one launch (start us, length us, event | category | flops | bytes accessed | tf_op | source)
XLA Modules:
  0.0 91.0 jit_solution(6908647024139204805)
XLA Ops:
  0.0 2.9 %pack_stripes.1 = bf16[32,136,128]{2,1,0:T(8,128)(2,1)} custom-call(s32[2,4]{1,0:T(2,128)} %bitcast.4, bf16[256,1024]{1,0:T(8,128)(2,1)} %key_ref.3, bf16[256,1024]{1,0:T(8,128)(2,1)} %value_ref.3), custom_call_target="tpu_custom_call" | custom-call | flops 1000000 | bytes 2097152 | tf_op jit(solution)/shard_map/pack_stripes/pallas_call | solution.py:88
  2.9 7.4 %all-to-all-start = ((bf16[32,136,128]{2,1,0:T(8,128)(2,1)}), bf16[32,136,128]{2,1,0:T(8,128)(2,1)S(1)}, u32[]{:S(2)}, u32[]{:S(2)}) async-start(bf16[32,136,128]{2,1,0:T(8,128)(2,1)} %pack_stripes.1), calls=%async_computation | async-start | bytes 2228224 | tf_op jit(solution)/shard_map/all_to_all | solution.py:381
  10.3 9.0 %self_attention.1 = (bf16[768,1024]{1,0:T(8,128)(2,1)}, bf16[256,1024]{1,0:T(8,128)(2,1)}, f32[6,128]{1,0:T(8,128)S(1)}) custom-call(bf16[1024,1024]{1,0:T(8,128)(2,1)} %query_ref.2, bf16[1024,1024]{1,0:T(8,128)(2,1)} %key_ref.2, bf16[1024,1024]{1,0:T(8,128)(2,1)} %value_ref.2), custom_call_target="tpu_custom_call" | custom-call | flops 8000000000 | bytes 8388608 | tf_op jit(solution)/shard_map/self_attention/pallas_call | solution.py:200
  19.3 6.7 %all-to-all-done.table_ref = bf16[32,136,128]{2,1,0:T(8,128)(2,1)S(1)} async-done(((bf16[32,136,128]{2,1,0:T(8,128)(2,1)}), bf16[32,136,128]{2,1,0:T(8,128)(2,1)S(1)}, u32[]{:S(2)}, u32[]{:S(2)}) %all-to-all-start) | async-done | bytes 1114144 | tf_op jit(solution)/shard_map/all_to_all | solution.py:381
  26.0 2.4 %pick_stripes.1 = bf16[32,256,128]{2,1,0:T(8,128)(2,1)} custom-call(s32[32,8]{1,0:T(8,128)S(1)} %bitcast.3, bf16[32,136,128]{2,1,0:T(8,128)(2,1)S(1)} %all-to-all-done.table_ref), custom_call_target="tpu_custom_call" | custom-call | flops 1000000 | bytes 3211264 | tf_op jit(solution)/shard_map/pick_stripes/pallas_call | solution.py:140
  28.4 0.0 copy-start.1
  28.4 6.4 %all-to-all-start.1 = ((bf16[32,256,128]{2,1,0:T(8,128)(2,1)}), bf16[32,256,128]{2,1,0:T(8,128)(2,1)S(1)}, u32[]{:S(2)}, u32[]{:S(2)}) async-start(bf16[32,256,128]{2,1,0:T(8,128)(2,1)} %pick_stripes.1), calls=%async_computation.1 | async-start | bytes 4194304 | tf_op jit(solution)/shard_map/all_to_all | solution.py:381
  34.8 0.0 copy-done.1
  34.8 2.0 %collective-permute-start = (bf16[256,1024]{1,0:T(8,128)(2,1)S(1)}, bf16[256,1024]{1,0:T(8,128)(2,1)S(1)}, u32[]{:S(2)}, u32[]{:S(2)}) collective-permute-start(bf16[256,1024]{1,0:T(8,128)(2,1)S(1)} %copy-done.1), channel_id=1, source_target_pairs={{0,4},{4,8},{8,12},{12,16},{16,20},{20,24},{24,28},{28,32},{32,36}... | collective-permute-start | bytes 1572872 | tf_op jit(solution)/shard_map/ppermute | solution.py:377
  36.8 30.1 %collective-permute-done.rows_ref.came_ref = bf16[256,1024]{1,0:T(8,128)(2,1)S(1)} collective-permute-done((bf16[256,1024]{1,0:T(8,128)(2,1)S(1)}, bf16[256,1024]{1,0:T(8,128)(2,1)S(1)}, u32[]{:S(2)}, u32[]{:S(2)}) %collective-permute-start) | collective-permute-done | bytes 524320 | tf_op jit(solution)/shard_map/ppermute | solution.py:377
  66.9 0.2 row_squares.1.refs_0_
  67.0 2.0 %collective-permute-start.1 = (f32[8,128]{1,0:T(8,128)S(1)}, f32[8,128]{1,0:T(8,128)S(1)}, u32[]{:S(2)}, u32[]{:S(2)}) collective-permute-start(f32[8,128]{1,0:T(8,128)S(1)} %row_squares.1.refs_0_), channel_id=1, source_target_pairs={{0,1},{1,2},{2,3},{3,0},{4,5},{5,6},{6,7},{7,4},{8,9},{9,10},{10,1... | collective-permute-start | bytes 12296 | tf_op jit(solution)/shard_map/ppermute | solution.py:370
  69.0 3.6 %collective-permute-start.2 = (f32[8,128]{1,0:T(8,128)S(1)}, f32[8,128]{1,0:T(8,128)S(1)}, u32[]{:S(2)}, u32[]{:S(2)}) collective-permute-start(f32[8,128]{1,0:T(8,128)S(1)} %row_squares.1.refs_0_), channel_id=1, source_target_pairs={{0,2},{1,3},{2,0},{3,1},{4,6},{5,7},{6,4},{7,5},{8,10},{9,11},{10,... | collective-permute-start | bytes 12296 | tf_op jit(solution)/shard_map/ppermute | solution.py:370
  72.6 1.0 %collective-permute-start.3 = (f32[8,128]{1,0:T(8,128)S(1)}, f32[8,128]{1,0:T(8,128)S(1)}, u32[]{:S(2)}, u32[]{:S(2)}) collective-permute-start(f32[8,128]{1,0:T(8,128)S(1)} %row_squares.1.refs_0_), channel_id=1, source_target_pairs={{0,3},{1,0},{2,1},{3,2},{4,7},{5,4},{6,5},{7,6},{8,11},{9,8},{10,9... | collective-permute-start | bytes 12296 | tf_op jit(solution)/shard_map/ppermute | solution.py:370
  73.6 0.0 collective-permute-done.1.refs_1_
  73.6 0.6 collective-permute-done.2.refs_2_
  74.2 2.0 %collective-permute-done.3.refs_3_ = f32[8,128]{1,0:T(8,128)S(1)} collective-permute-done((f32[8,128]{1,0:T(8,128)S(1)}, f32[8,128]{1,0:T(8,128)S(1)}, u32[]{:S(2)}, u32[]{:S(2)}) %collective-permute-start.3) | collective-permute-done | bytes 4128 | tf_op jit(solution)/shard_map/ppermute | solution.py:370
  76.2 0.0 all-to-all-done.1.got_ref
  76.2 0.0 copy-start
  76.2 5.0 %cross_attention.1 = (bf16[1024,1024]{1,0:T(8,128)(2,1)S(1)}, f32[8,128]{1,0:T(8,128)S(1)}) custom-call(bf16[256,1024]{1,0:T(8,128)(2,1)S(1)} %collective-permute-done.rows_ref.came_ref, bf16[768,1024]{1,0:T(8,128)(2,1)} %get-tuple-element.16.rest_ref, bf16[32,256,128]{2,1,0:T(8,128)(2,1)S(1)} %all-to-all-done.1.got_ref, f32[8,128]{1,0:T(8,128)S(1)} %row_squares.1.refs_0_, ...), custom_call_target="tpu_custom_call" | custom-call | flops 8000000000 | bytes 6291456 | tf_op jit(solution)/shard_map/cross_attention/pallas_call | solution.py:299
  81.2 0.1 collective-permute-start.4
  81.3 3.7 %collective-permute-start.5 = (f32[8,128]{1,0:T(8,128)S(1)}, f32[8,128]{1,0:T(8,128)S(1)}, u32[]{:S(2)}, u32[]{:S(2)}) collective-permute-start(f32[8,128]{1,0:T(8,128)S(1)} %get-tuple-element.22.refs_0_), channel_id=1, source_target_pairs={{0,2},{1,3},{2,0},{3,1},{4,6},{5,7},{6,4},{7,5},{8,10},{9,11},{10,... | collective-permute-start | bytes 12296 | tf_op jit(solution)/shard_map/ppermute | solution.py:370
  85.0 0.5 collective-permute-start.6
  85.4 0.7 collective-permute-done.4.refs_1_
  86.1 0.5 collective-permute-done.5.refs_2_
  86.6 2.0 %collective-permute-done.6.refs_3_ = f32[8,128]{1,0:T(8,128)S(1)} collective-permute-done((f32[8,128]{1,0:T(8,128)S(1)}, f32[8,128]{1,0:T(8,128)S(1)}, u32[]{:S(2)}, u32[]{:S(2)}) %collective-permute-start.6) | collective-permute-done | bytes 4128 | tf_op jit(solution)/shard_map/ppermute | solution.py:370
  88.6 0.0 copy-done
  88.6 2.5 %decode.1 = bf16[256,1024]{1,0:T(8,128)(2,1)} custom-call(s32[1]{0:T(128)} %bitcast.place_ref, bf16[256,1024]{1,0:T(8,128)(2,1)S(1)} %copy-done, bf16[1024,1024]{1,0:T(8,128)(2,1)S(1)} %get-tuple-element.21.prior_ref, f32[8,128]{1,0:T(8,128)S(1)} %get-tuple-element.22.refs_0_, f32[8,128]{1,0:T(8,128)S(1)} %collective-permute-done.4.refs_1_, ...), custom_call_target="tpu_custom_call" | custom-call | flops 4000000000 | bytes 3145728 | tf_op jit(solution)/shard_map/decode/pallas_call | solution.py:350
  (1 shorter events, 0.0 us)
Async XLA Ops:
  2.9 23.1 %all-to-all-start = ((bf16[32,136,128]{2,1,0:T(8,128)(2,1)}), bf16[32,136,128]{2,1,0:T(8,128)(2,1)S(1)}, u32[]{:S(2)}, u32[]{:S(2)}) async-start(bf16[32,136,128]{2,1,0:T(8,128)(2,1)} %pack_stripes.1), calls=%async_computation | async-start | bytes 2228224 | tf_op jit(solution)/shard_map/all_to_all | solution.py:381
  28.4 6.4 %copy-start.1 = (bf16[256,1024]{1,0:T(8,128)(2,1)S(1)}, bf16[256,1024]{1,0:T(8,128)(2,1)}, u32[]{:S(2)}) copy-start(bf16[256,1024]{1,0:T(8,128)(2,1)} %get-tuple-element.15) | copy-start | bytes 1572868
  28.4 47.8 %all-to-all-start.1 = ((bf16[32,256,128]{2,1,0:T(8,128)(2,1)}), bf16[32,256,128]{2,1,0:T(8,128)(2,1)S(1)}, u32[]{:S(2)}, u32[]{:S(2)}) async-start(bf16[32,256,128]{2,1,0:T(8,128)(2,1)} %pick_stripes.1), calls=%async_computation.1 | async-start | bytes 4194304 | tf_op jit(solution)/shard_map/all_to_all | solution.py:381
  34.8 32.1 %collective-permute-start = (bf16[256,1024]{1,0:T(8,128)(2,1)S(1)}, bf16[256,1024]{1,0:T(8,128)(2,1)S(1)}, u32[]{:S(2)}, u32[]{:S(2)}) collective-permute-start(bf16[256,1024]{1,0:T(8,128)(2,1)S(1)} %copy-done.1), channel_id=1, source_target_pairs={{0,4},{4,8},{8,12},{12,16},{16,20},{20,24},{24,28},{28,32},{32,36}... | collective-permute-start | bytes 1572872 | tf_op jit(solution)/shard_map/ppermute | solution.py:377
  67.0 6.6 %collective-permute-start.1 = (f32[8,128]{1,0:T(8,128)S(1)}, f32[8,128]{1,0:T(8,128)S(1)}, u32[]{:S(2)}, u32[]{:S(2)}) collective-permute-start(f32[8,128]{1,0:T(8,128)S(1)} %row_squares.1.refs_0_), channel_id=1, source_target_pairs={{0,1},{1,2},{2,3},{3,0},{4,5},{5,6},{6,7},{7,4},{8,9},{9,10},{10,1... | collective-permute-start | bytes 12296 | tf_op jit(solution)/shard_map/ppermute | solution.py:370
  69.0 5.2 %collective-permute-start.2 = (f32[8,128]{1,0:T(8,128)S(1)}, f32[8,128]{1,0:T(8,128)S(1)}, u32[]{:S(2)}, u32[]{:S(2)}) collective-permute-start(f32[8,128]{1,0:T(8,128)S(1)} %row_squares.1.refs_0_), channel_id=1, source_target_pairs={{0,2},{1,3},{2,0},{3,1},{4,6},{5,7},{6,4},{7,5},{8,10},{9,11},{10,... | collective-permute-start | bytes 12296 | tf_op jit(solution)/shard_map/ppermute | solution.py:370
  72.6 3.6 %collective-permute-start.3 = (f32[8,128]{1,0:T(8,128)S(1)}, f32[8,128]{1,0:T(8,128)S(1)}, u32[]{:S(2)}, u32[]{:S(2)}) collective-permute-start(f32[8,128]{1,0:T(8,128)S(1)} %row_squares.1.refs_0_), channel_id=1, source_target_pairs={{0,3},{1,0},{2,1},{3,2},{4,7},{5,4},{6,5},{7,6},{8,11},{9,8},{10,9... | collective-permute-start | bytes 12296 | tf_op jit(solution)/shard_map/ppermute | solution.py:370
  76.2 12.3 %copy-start = (bf16[256,1024]{1,0:T(8,128)(2,1)S(1)}, bf16[256,1024]{1,0:T(8,128)(2,1)}, u32[]{:S(2)}) copy-start(bf16[256,1024]{1,0:T(8,128)(2,1)} %query_ref.3) | copy-start | bytes 1572868
  81.2 4.9 %collective-permute-start.4 = (f32[8,128]{1,0:T(8,128)S(1)}, f32[8,128]{1,0:T(8,128)S(1)}, u32[]{:S(2)}, u32[]{:S(2)}) collective-permute-start(f32[8,128]{1,0:T(8,128)S(1)} %get-tuple-element.22.refs_0_), channel_id=1, source_target_pairs={{0,1},{1,2},{2,3},{3,0},{4,5},{5,6},{6,7},{7,4},{8,9},{9,10},{10,1... | collective-permute-start | bytes 12296 | tf_op jit(solution)/shard_map/ppermute | solution.py:370
  81.3 5.3 %collective-permute-start.5 = (f32[8,128]{1,0:T(8,128)S(1)}, f32[8,128]{1,0:T(8,128)S(1)}, u32[]{:S(2)}, u32[]{:S(2)}) collective-permute-start(f32[8,128]{1,0:T(8,128)S(1)} %get-tuple-element.22.refs_0_), channel_id=1, source_target_pairs={{0,2},{1,3},{2,0},{3,1},{4,6},{5,7},{6,4},{7,5},{8,10},{9,11},{10,... | collective-permute-start | bytes 12296 | tf_op jit(solution)/shard_map/ppermute | solution.py:370
  85.0 3.6 %collective-permute-start.6 = (f32[8,128]{1,0:T(8,128)S(1)}, f32[8,128]{1,0:T(8,128)S(1)}, u32[]{:S(2)}, u32[]{:S(2)}) collective-permute-start(f32[8,128]{1,0:T(8,128)S(1)} %get-tuple-element.22.refs_0_), channel_id=1, source_target_pairs={{0,3},{1,0},{2,1},{3,2},{4,7},{5,4},{6,5},{7,6},{8,11},{9,8},{10,9... | collective-permute-start | bytes 12296 | tf_op jit(solution)/shard_map/ppermute | solution.py:370

commit v6 on v5

--- a/solution.py
+++ b/solution.py
@@ -19,6 +19,7 @@
 SCALE2 = HEAD_DIM ** (-0.5) * LOG2E
 HALF = SEG_LEN // 2
 TAIL = 8
+AT_ONCE = 2
 PACK_MIB = 60
 SELF_MIB = 24
 PICK_MIB = 24
@@ -246,118 +247,120 @@
 
 
 def cross_kernel(full_width, came_ref, rest_ref, got_ref, *refs):
-    parts, (out_ref, squares_ref, self_ref) = refs[:-3], refs[-3:]
-    step = pl.program_id(0)
-
-    came_steps = NEIGHBOURS * NBR_LEN // self_ref.shape[0]
-
-    @pl.when(step < came_steps)
-    def _():
-        self_ref[...] = came_ref[...]
-
-    @pl.when(step >= came_steps)
-    def _():
-        self_ref[...] = rest_ref[...]
-
-    here = self_ref.shape[0] // NBR_LEN
-    heads = self_ref.shape[1] // HEAD_DIM
-    each = [(i, h) for i in range(here) for h in range(heads)]
-    rows_of = [slice(i * NBR_LEN, (i + 1) * NBR_LEN) for i in range(here)]
-    at = [columns_of(head) for head in range(heads)]
-    scales = [
-        lax.rsqrt(summed(parts, pl.ds(step * here + i, 1)) / full_width + EPSILON) * SCALE2
-        for i in range(here)
-    ]
-
-    def whole(kv, i, h):
-        slot = slice(i * HALF, (i + 1) * HALF)
-        return jnp.concatenate(
-            [got_ref[(2 * kv + half) * heads + h, slot, :] for half in range(2)], axis=0
-        )
-
-    scores = [dot(whole(0, i, h), self_ref[rows_of[i], at[h]], (1, 1)) for i, h in each]
-    weights = [softmax_down(score, scales[i]) for score, (i, h) in zip(scores, each)]
-    sums = [dot(weight, whole(1, i, h), (0, 0)) for weight, (i, h) in zip(weights, each)]
-    totals = [jnp.zeros((NBR_LEN, HEAD_DIM), F32) for _ in range(here)]
-    for crossed, (i, h) in zip(sums, each):
-        own = self_ref[rows_of[i], at[h]].astype(F32)
-        rows = (own + crossed.astype(BF16).astype(F32)).astype(BF16)
-        out_ref[rows_of[i], at[h]] = rows
-        wide = rows.astype(F32)
-        totals[i] = totals[i] + wide * wide
-    for i in range(here):
-        squares_ref[pl.ds(step * here + i, 1), :] = lanes_of(totals[i])
-
-
-def cross_attention(came, rest, got, parts, full_width, here=NEIGHBOURS):
+    parts, (out_ref, squares_ref, rest_rows, sems) = refs[:-4], refs[-4:]
+    panel = NEIGHBOURS * NBR_LEN
+    heads = came_ref.shape[1] // HEAD_DIM
+
+    def into(seg):
+        at = pl.ds((seg - 1) * panel, panel)
+        return pltpu.make_async_copy(rest_ref.at[at, :], rest_rows.at[at, :], sems.at[seg - 1])
+
+    for seg in range(1, SEG_DEV):
+        into(seg).start()
+    for seg in range(SEG_DEV):
+        if seg > 0:
+            into(seg).wait()
+        each = [(seg * NEIGHBOURS + i, h) for i in range(NEIGHBOURS) for h in range(heads)]
+
+        def own(n, h):
+            first = n * NBR_LEN - (panel if seg > 0 else 0)
+            ref = rest_rows if seg > 0 else came_ref
+            return ref[first:first + NBR_LEN, columns_of(h)]
+
+        def whole(kv, n, h):
+            slot = slice(n * HALF, (n + 1) * HALF)
+            return jnp.concatenate(
+                [got_ref[(2 * kv + half) * heads + h, slot, :] for half in range(2)], axis=0
+            )
+
+        total = summed(parts, slice(seg * NEIGHBOURS, (seg + 1) * NEIGHBOURS))
+        scale = lax.rsqrt(total / full_width + EPSILON) * SCALE2
+        scores = [dot(whole(0, n, h), own(n, h), (1, 1)) for n, h in each]
+        weights = [
+            softmax_down(score, scale[n % NEIGHBOURS:n % NEIGHBOURS + 1, :])
+            for score, (n, h) in zip(scores, each)
+        ]
+        sums = [dot(weight, whole(1, n, h), (0, 0)) for weight, (n, h) in zip(weights, each)]
+        squares = {n: jnp.zeros((NBR_LEN, HEAD_DIM), F32) for n, _ in each}
+        for crossed, (n, h) in zip(sums, each):
+            rows = (own(n, h).astype(F32) + crossed.astype(BF16).astype(F32)).astype(BF16)
+            out_ref[n * NBR_LEN:(n + 1) * NBR_LEN, columns_of(h)] = rows
+            wide = rows.astype(F32)
+            squares[n] = squares[n] + wide * wide
+        for n in squares:
+            squares_ref[n:n + 1, :] = lanes_of(squares[n])
+
+
+def cross_attention(came, rest, got, parts, full_width):
     columns = came.shape[1]
     count = SEG_DEV * NEIGHBOURS
     rows = count * NBR_LEN
-    first = NEIGHBOURS // here
-    block = (here * NBR_LEN, columns)
-    sums = pl.BlockSpec((count, NBR_LEN), lambda n: (0, 0))
+    vmem = pl.BlockSpec(memory_space=pltpu.VMEM)
     return pl.pallas_call(
         functools.partial(cross_kernel, full_width),
-        grid=(count // here,),
         out_shape=(
             jax.ShapeDtypeStruct((rows, columns), BF16),
             jax.ShapeDtypeStruct((count, NBR_LEN), F32),
         ),
-        in_specs=[
-            pl.BlockSpec(block, lambda n: (jnp.minimum(n, first - 1), 0)),
-            pl.BlockSpec(block, lambda n: (jnp.maximum(n - first, 0), 0)),
-            pl.BlockSpec((got.shape[0], here * HALF, HEAD_DIM), lambda n: (0, n, 0)),
-        ]
-        + [sums] * len(parts),
-        out_specs=(pl.BlockSpec(block, lambda n: (n, 0)), sums),
-        scratch_shapes=[pltpu.VMEM(block, BF16)],
+        in_specs=[vmem, pl.BlockSpec(memory_space=pl.ANY), vmem] + [vmem] * len(parts),
+        out_specs=(vmem, vmem),
+        scratch_shapes=[pltpu.VMEM(rest.shape, BF16), pltpu.SemaphoreType.DMA((SEG_DEV - 1,))],
         compiler_params=params(SMALL_MIB),
         cost_estimate=cost(1000000000 * count, 6 * rows * columns, rows * columns // 2),
         name="cross_attention",
-    )(came, rest, got, *parts)
+    )(came, in_hbm(rest), got, *parts)
 
 
 def decode_kernel(full_width, place_ref, query_ref, prior_ref, *refs):
-    parts, out_ref = refs[:-1], refs[-1]
-    step = pl.program_id(0)
+    parts, (out_ref, out_rows, sems) = refs[:-3], refs[-3:]
     panel = NEIGHBOURS * NBR_LEN
-    here = query_ref.shape[0] // SEG_LEN
-    each = [(i, h) for i in range(here) for h in range(query_ref.shape[1] // HEAD_DIM)]
-    asks = [slice(i * SEG_LEN, (i + 1) * SEG_LEN) for i in range(here)]
-    reads = [slice(i * panel, (i + 1) * panel) for i in range(here)]
-
-    def scale_of(i):
-        first = (step * here + i) * NEIGHBOURS
-        totals = [summed(parts, pl.ds(first + n, 1)) for n in range(NEIGHBOURS)]
-        return lax.rsqrt(jnp.concatenate(totals, axis=1) / full_width + EPSILON) * SCALE2
-
-    scales = [scale_of(i) for i in range(here)]
-    empty = (step == 0) & (place_ref[0] == 0)
-    scores = [dot(query_ref[asks[i], columns_of(h)], prior_ref[reads[i], columns_of(h)], (1, 1)) for i, h in each]
-    weights = [softmax_across(score * scales[i]) for score, (i, h) in zip(scores, each)]
-    for weight, (i, h) in zip(weights, each):
-        rows = dot(weight, prior_ref[reads[i], columns_of(h)], (1, 0))
-        if i == 0:
-            rows = jnp.where(empty, 0.0, rows)
-        out_ref[asks[i], columns_of(h)] = rows.astype(BF16)
-
-
-def decode(place, query, prior, parts, full_width, here=2):
-    columns = query.shape[1]
-    panel = NEIGHBOURS * NBR_LEN
-    query_block = pl.BlockSpec((here * SEG_LEN, columns), lambda u: (u, 0))
-    sums = pl.BlockSpec(parts[0].shape, lambda u: (0, 0))
+    heads = query_ref.shape[1] // HEAD_DIM
+    empty = place_ref[0] == 0
+
+    def out_of(group):
+        at = pl.ds(group * AT_ONCE * SEG_LEN, AT_ONCE * SEG_LEN)
+        return pltpu.make_async_copy(out_rows.at[at, :], out_ref.at[at, :], sems.at[group])
+
+    totals = summed(parts, slice(None))
+    scales = lax.rsqrt(totals / full_width + EPSILON) * SCALE2
+    for group in range(SEG_DEV // AT_ONCE):
+        each = [(group * AT_ONCE + i, h) for i in range(AT_ONCE) for h in range(heads)]
+        scale = {
+            u: jnp.concatenate(
+                [scales[n:n + 1, :] for n in range(u * NEIGHBOURS, (u + 1) * NEIGHBOURS)], axis=1
+            )
+            for u, _ in each
+        }
+
+        def prior(u, h):
+            return prior_ref[u * panel:(u + 1) * panel, columns_of(h)]
+
+        scores = [
+            dot(query_ref[u * SEG_LEN:(u + 1) * SEG_LEN, columns_of(h)], prior(u, h), (1, 1))
+            for u, h in each
+        ]
+        weights = [softmax_across(score * scale[u]) for score, (u, h) in zip(scores, each)]
+        for weight, (u, h) in zip(weights, each):
+            rows = dot(weight, prior(u, h), (1, 0))
+            if u == 0:
+                rows = jnp.where(empty, 0.0, rows)
+            out_rows[u * SEG_LEN:(u + 1) * SEG_LEN, columns_of(h)] = rows.astype(BF16)
+        out_of(group).start()
+    for group in range(SEG_DEV // AT_ONCE):
+        out_of(group).wait()
+
+
+def decode(place, query, prior, parts, full_width):
+    vmem = pl.BlockSpec(memory_space=pltpu.VMEM)
     return pl.pallas_call(
         functools.partial(decode_kernel, full_width),
-        grid=(SEG_DEV // here,),
         out_shape=jax.ShapeDtypeStruct(query.shape, BF16),
-        in_specs=[
-            pl.BlockSpec(memory_space=pltpu.SMEM),
-            query_block,
-            pl.BlockSpec((here * panel, columns), lambda u: (u, 0)),
-        ]
-        + [sums] * len(parts),
-        out_specs=query_block,
+        in_specs=[pl.BlockSpec(memory_space=pltpu.SMEM), vmem, vmem] + [vmem] * len(parts),
+        out_specs=pl.BlockSpec(memory_space=pl.ANY),
+        scratch_shapes=[
+            pltpu.VMEM(query.shape, BF16),
+            pltpu.SemaphoreType.DMA((SEG_DEV // AT_ONCE,)),
+        ],
         compiler_params=params(SMALL_MIB),
         cost_estimate=cost(4000000000, 4 * query.size + 2 * prior.size, query.size * 2),
         name="decode",
@@ -402,7 +405,7 @@
     named = table[:, SEG_DEV * HALF, :per_device].astype(jnp.int32)
     got = exchange(pick(named, table))
     parts = over_heads(squares_above(came, rest_squares))
-    encoded, squares = cross_attention(came, in_hbm(rest), got, parts, full_width)
+    encoded, squares = cross_attention(came, rest, got, parts, full_width)
     return decode(place, decoder_query, encoded, over_heads(squares), full_width)
 
 

time: 91.6 us -> 90.2 us (0.985)
  Pallas kernels: 21.9 us -> 20.6 us
    pallas_call x2, Pallas kernels: 7.44 us -> 6.1 us  [the longest x1 3.75 us: cross_attention(): pl.pallas_call(functools.partial(cross_kernel, full_width), out_shape=(ja...]
where the time goes in v6:
time: 90.2 us; the launch traced here: 89.7 us
  waiting for transfers between devices  42.5 us (47%)
  starting transfers between devices  26.5 us (29%)
  Pallas kernels  20.6 us (23%)
    ppermute x1, waiting for transfers between devices, from_behind(): return lax.ppermute(part, 'span', [(i, i + 1) for i in range(devices - 1)])  30.1 us
    all_to_all x2, starting transfers between devices, exchange(): return lax.all_to_all(x, 'span', split_axis=0, concat_axis=0, tiled=True)  13.7 us
    ppermute x6, starting transfers between devices, over_heads(): lax.ppermute(part, 'head', [(i, (i + step) % heads) for i in range(heads)])  10.8 us
    pallas_call x1, Pallas kernels, self_attention(): pl.pallas_call(self_kernel, grid=(count,), out_shape=(pltpu.HBM((last * N...  9.04 us
    all_to_all x2, waiting for transfers between devices, exchange(): return lax.all_to_all(x, 'span', split_axis=0, concat_axis=0, tiled=True)  6.67 us
    ppermute x6, waiting for transfers between devices, over_heads(): lax.ppermute(part, 'head', [(i, (i + step) % heads) for i in range(heads)])  5.74 us
    pallas_call x1, Pallas kernels, cross_attention(): pl.pallas_call(functools.partial(cross_kernel, full_width), out_shape=(ja...  3.75 us
    pallas_call x1, Pallas kernels, pack(): pl.pallas_call(pack_kernel, out_shape=jax.ShapeDtypeStruct(shape, BF16),...  2.88 us
  transfers between devices with their start and end apart: 9, of which 7 were waited for; matrix products, arithmetic and copies ran while one was open for 0% of the time, Pallas kernels for 10%

profile of v6, /device:TPU:24, one launch (start us, length us, event | category | flops | bytes accessed | tf_op | source)
XLA Modules:
  0.0 89.7 jit_solution(6988387144777365272)
XLA Ops:
  0.0 2.9 %pack_stripes.1 = bf16[32,136,128]{2,1,0:T(8,128)(2,1)} custom-call(s32[2,4]{1,0:T(2,128)} %bitcast.4, bf16[256,1024]{1,0:T(8,128)(2,1)} %key_ref.3, bf16[256,1024]{1,0:T(8,128)(2,1)} %value_ref.3), custom_call_target="tpu_custom_call" | custom-call | flops 1000000 | bytes 2097152 | tf_op jit(solution)/shard_map/pack_stripes/pallas_call | solution.py:89
  2.9 7.4 %all-to-all-start = ((bf16[32,136,128]{2,1,0:T(8,128)(2,1)}), bf16[32,136,128]{2,1,0:T(8,128)(2,1)S(1)}, u32[]{:S(2)}, u32[]{:S(2)}) async-start(bf16[32,136,128]{2,1,0:T(8,128)(2,1)} %pack_stripes.1), calls=%async_computation | async-start | bytes 2228224 | tf_op jit(solution)/shard_map/all_to_all | solution.py:384
  10.3 9.0 %self_attention.1 = (bf16[768,1024]{1,0:T(8,128)(2,1)}, bf16[256,1024]{1,0:T(8,128)(2,1)}, f32[6,128]{1,0:T(8,128)S(1)}) custom-call(bf16[1024,1024]{1,0:T(8,128)(2,1)} %query_ref.2, bf16[1024,1024]{1,0:T(8,128)(2,1)} %key_ref.2, bf16[1024,1024]{1,0:T(8,128)(2,1)} %value_ref.2), custom_call_target="tpu_custom_call" | custom-call | flops 8000000000 | bytes 8388608 | tf_op jit(solution)/shard_map/self_attention/pallas_call | solution.py:201
  19.3 6.7 %all-to-all-done.table_ref = bf16[32,136,128]{2,1,0:T(8,128)(2,1)S(1)} async-done(((bf16[32,136,128]{2,1,0:T(8,128)(2,1)}), bf16[32,136,128]{2,1,0:T(8,128)(2,1)S(1)}, u32[]{:S(2)}, u32[]{:S(2)}) %all-to-all-start) | async-done | bytes 1114144 | tf_op jit(solution)/shard_map/all_to_all | solution.py:384
  26.0 2.4 %pick_stripes.1 = bf16[32,256,128]{2,1,0:T(8,128)(2,1)} custom-call(s32[32,8]{1,0:T(8,128)S(1)} %bitcast.3, bf16[32,136,128]{2,1,0:T(8,128)(2,1)S(1)} %all-to-all-done.table_ref), custom_call_target="tpu_custom_call" | custom-call | flops 1000000 | bytes 3211264 | tf_op jit(solution)/shard_map/pick_stripes/pallas_call | solution.py:141
  28.4 0.0 copy-start.1
  28.4 6.4 %all-to-all-start.1 = ((bf16[32,256,128]{2,1,0:T(8,128)(2,1)}), bf16[32,256,128]{2,1,0:T(8,128)(2,1)S(1)}, u32[]{:S(2)}, u32[]{:S(2)}) async-start(bf16[32,256,128]{2,1,0:T(8,128)(2,1)} %pick_stripes.1), calls=%async_computation.1 | async-start | bytes 4194304 | tf_op jit(solution)/shard_map/all_to_all | solution.py:384
  34.8 0.0 copy-done.1
  34.8 2.0 %collective-permute-start = (bf16[256,1024]{1,0:T(8,128)(2,1)S(1)}, bf16[256,1024]{1,0:T(8,128)(2,1)S(1)}, u32[]{:S(2)}, u32[]{:S(2)}) collective-permute-start(bf16[256,1024]{1,0:T(8,128)(2,1)S(1)} %copy-done.1), channel_id=1, source_target_pairs={{0,4},{4,8},{8,12},{12,16},{16,20},{20,24},{24,28},{28,32},{32,36}... | collective-permute-start | bytes 1572872 | tf_op jit(solution)/shard_map/ppermute | solution.py:380
  36.8 30.1 %collective-permute-done.rows_ref.came_ref = bf16[256,1024]{1,0:T(8,128)(2,1)S(1)} collective-permute-done((bf16[256,1024]{1,0:T(8,128)(2,1)S(1)}, bf16[256,1024]{1,0:T(8,128)(2,1)S(1)}, u32[]{:S(2)}, u32[]{:S(2)}) %collective-permute-start) | collective-permute-done | bytes 524320 | tf_op jit(solution)/shard_map/ppermute | solution.py:380
  66.9 0.2 row_squares.1.refs_0_
  67.0 2.0 %collective-permute-start.1 = (f32[8,128]{1,0:T(8,128)S(1)}, f32[8,128]{1,0:T(8,128)S(1)}, u32[]{:S(2)}, u32[]{:S(2)}) collective-permute-start(f32[8,128]{1,0:T(8,128)S(1)} %row_squares.1.refs_0_), channel_id=1, source_target_pairs={{0,1},{1,2},{2,3},{3,0},{4,5},{5,6},{6,7},{7,4},{8,9},{9,10},{10,1... | collective-permute-start | bytes 12296 | tf_op jit(solution)/shard_map/ppermute | solution.py:373
  69.0 3.6 %collective-permute-start.2 = (f32[8,128]{1,0:T(8,128)S(1)}, f32[8,128]{1,0:T(8,128)S(1)}, u32[]{:S(2)}, u32[]{:S(2)}) collective-permute-start(f32[8,128]{1,0:T(8,128)S(1)} %row_squares.1.refs_0_), channel_id=1, source_target_pairs={{0,2},{1,3},{2,0},{3,1},{4,6},{5,7},{6,4},{7,5},{8,10},{9,11},{10,... | collective-permute-start | bytes 12296 | tf_op jit(solution)/shard_map/ppermute | solution.py:373
  72.6 1.0 %collective-permute-start.3 = (f32[8,128]{1,0:T(8,128)S(1)}, f32[8,128]{1,0:T(8,128)S(1)}, u32[]{:S(2)}, u32[]{:S(2)}) collective-permute-start(f32[8,128]{1,0:T(8,128)S(1)} %row_squares.1.refs_0_), channel_id=1, source_target_pairs={{0,3},{1,0},{2,1},{3,2},{4,7},{5,4},{6,5},{7,6},{8,11},{9,8},{10,9... | collective-permute-start | bytes 12296 | tf_op jit(solution)/shard_map/ppermute | solution.py:373
  73.6 0.0 collective-permute-done.1.refs_1_
  73.6 0.6 collective-permute-done.2.refs_2_
  74.2 2.0 %collective-permute-done.3.refs_3_ = f32[8,128]{1,0:T(8,128)S(1)} collective-permute-done((f32[8,128]{1,0:T(8,128)S(1)}, f32[8,128]{1,0:T(8,128)S(1)}, u32[]{:S(2)}, u32[]{:S(2)}) %collective-permute-start.3) | collective-permute-done | bytes 4128 | tf_op jit(solution)/shard_map/ppermute | solution.py:373
  76.2 0.0 all-to-all-done.1.got_ref
  76.2 0.0 copy-start
  76.2 3.8 %cross_attention.1 = (bf16[1024,1024]{1,0:T(8,128)(2,1)S(1)}, f32[8,128]{1,0:T(8,128)S(1)}) custom-call(bf16[256,1024]{1,0:T(8,128)(2,1)S(1)} %collective-permute-done.rows_ref.came_ref, bf16[768,1024]{1,0:T(8,128)(2,1)} %get-tuple-element.16.rest_ref, bf16[32,256,128]{2,1,0:T(8,128)(2,1)S(1)} %all-to-all-done.1.got_ref, f32[8,128]{1,0:T(8,128)S(1)} %row_squares.1.refs_0_, ...), custom_call_target="tpu_custom_call" | custom-call | flops 8000000000 | bytes 6291456 | tf_op jit(solution)/shard_map/cross_attention/pallas_call | solution.py:299
  80.0 0.1 collective-permute-start.4
  80.1 3.7 %collective-permute-start.5 = (f32[8,128]{1,0:T(8,128)S(1)}, f32[8,128]{1,0:T(8,128)S(1)}, u32[]{:S(2)}, u32[]{:S(2)}) collective-permute-start(f32[8,128]{1,0:T(8,128)S(1)} %get-tuple-element.22.refs_0_), channel_id=1, source_target_pairs={{0,2},{1,3},{2,0},{3,1},{4,6},{5,7},{6,4},{7,5},{8,10},{9,11},{10,... | collective-permute-start | bytes 12296 | tf_op jit(solution)/shard_map/ppermute | solution.py:373
  83.7 0.5 collective-permute-start.6
  84.2 0.7 collective-permute-done.4.refs_1_
  84.9 0.5 collective-permute-done.5.refs_2_
  85.4 2.0 %collective-permute-done.6.refs_3_ = f32[8,128]{1,0:T(8,128)S(1)} collective-permute-done((f32[8,128]{1,0:T(8,128)S(1)}, f32[8,128]{1,0:T(8,128)S(1)}, u32[]{:S(2)}, u32[]{:S(2)}) %collective-permute-start.6) | collective-permute-done | bytes 4128 | tf_op jit(solution)/shard_map/ppermute | solution.py:373
  87.3 0.0 copy-done
  87.3 2.3 %decode.1 = bf16[256,1024]{1,0:T(8,128)(2,1)} custom-call(s32[1]{0:T(128)} %bitcast.place_ref, bf16[256,1024]{1,0:T(8,128)(2,1)S(1)} %copy-done, bf16[1024,1024]{1,0:T(8,128)(2,1)S(1)} %get-tuple-element.21.prior_ref, f32[8,128]{1,0:T(8,128)S(1)} %get-tuple-element.22.refs_0_, f32[8,128]{1,0:T(8,128)S(1)} %collective-permute-done.4.refs_1_, ...), custom_call_target="tpu_custom_call" | custom-call | flops 4000000000 | bytes 3145728 | tf_op jit(solution)/shard_map/decode/pallas_call | solution.py:355
  (1 shorter events, 0.0 us)
Async XLA Ops:
  2.9 23.1 %all-to-all-start = ((bf16[32,136,128]{2,1,0:T(8,128)(2,1)}), bf16[32,136,128]{2,1,0:T(8,128)(2,1)S(1)}, u32[]{:S(2)}, u32[]{:S(2)}) async-start(bf16[32,136,128]{2,1,0:T(8,128)(2,1)} %pack_stripes.1), calls=%async_computation | async-start | bytes 2228224 | tf_op jit(solution)/shard_map/all_to_all | solution.py:384
  28.4 6.4 %copy-start.1 = (bf16[256,1024]{1,0:T(8,128)(2,1)S(1)}, bf16[256,1024]{1,0:T(8,128)(2,1)}, u32[]{:S(2)}) copy-start(bf16[256,1024]{1,0:T(8,128)(2,1)} %get-tuple-element.15) | copy-start | bytes 1572868
  28.4 47.8 %all-to-all-start.1 = ((bf16[32,256,128]{2,1,0:T(8,128)(2,1)}), bf16[32,256,128]{2,1,0:T(8,128)(2,1)S(1)}, u32[]{:S(2)}, u32[]{:S(2)}) async-start(bf16[32,256,128]{2,1,0:T(8,128)(2,1)} %pick_stripes.1), calls=%async_computation.1 | async-start | bytes 4194304 | tf_op jit(solution)/shard_map/all_to_all | solution.py:384
  34.8 32.1 %collective-permute-start = (bf16[256,1024]{1,0:T(8,128)(2,1)S(1)}, bf16[256,1024]{1,0:T(8,128)(2,1)S(1)}, u32[]{:S(2)}, u32[]{:S(2)}) collective-permute-start(bf16[256,1024]{1,0:T(8,128)(2,1)S(1)} %copy-done.1), channel_id=1, source_target_pairs={{0,4},{4,8},{8,12},{12,16},{16,20},{20,24},{24,28},{28,32},{32,36}... | collective-permute-start | bytes 1572872 | tf_op jit(solution)/shard_map/ppermute | solution.py:380
  67.0 6.6 %collective-permute-start.1 = (f32[8,128]{1,0:T(8,128)S(1)}, f32[8,128]{1,0:T(8,128)S(1)}, u32[]{:S(2)}, u32[]{:S(2)}) collective-permute-start(f32[8,128]{1,0:T(8,128)S(1)} %row_squares.1.refs_0_), channel_id=1, source_target_pairs={{0,1},{1,2},{2,3},{3,0},{4,5},{5,6},{6,7},{7,4},{8,9},{9,10},{10,1... | collective-permute-start | bytes 12296 | tf_op jit(solution)/shard_map/ppermute | solution.py:373
  69.0 5.2 %collective-permute-start.2 = (f32[8,128]{1,0:T(8,128)S(1)}, f32[8,128]{1,0:T(8,128)S(1)}, u32[]{:S(2)}, u32[]{:S(2)}) collective-permute-start(f32[8,128]{1,0:T(8,128)S(1)} %row_squares.1.refs_0_), channel_id=1, source_target_pairs={{0,2},{1,3},{2,0},{3,1},{4,6},{5,7},{6,4},{7,5},{8,10},{9,11},{10,... | collective-permute-start | bytes 12296 | tf_op jit(solution)/shard_map/ppermute | solution.py:373
  72.6 3.6 %collective-permute-start.3 = (f32[8,128]{1,0:T(8,128)S(1)}, f32[8,128]{1,0:T(8,128)S(1)}, u32[]{:S(2)}, u32[]{:S(2)}) collective-permute-start(f32[8,128]{1,0:T(8,128)S(1)} %row_squares.1.refs_0_), channel_id=1, source_target_pairs={{0,3},{1,0},{2,1},{3,2},{4,7},{5,4},{6,5},{7,6},{8,11},{9,8},{10,9... | collective-permute-start | bytes 12296 | tf_op jit(solution)/shard_map/ppermute | solution.py:373
  76.2 11.1 %copy-start = (bf16[256,1024]{1,0:T(8,128)(2,1)S(1)}, bf16[256,1024]{1,0:T(8,128)(2,1)}, u32[]{:S(2)}) copy-start(bf16[256,1024]{1,0:T(8,128)(2,1)} %query_ref.3) | copy-start | bytes 1572868
  80.0 4.9 %collective-permute-start.4 = (f32[8,128]{1,0:T(8,128)S(1)}, f32[8,128]{1,0:T(8,128)S(1)}, u32[]{:S(2)}, u32[]{:S(2)}) collective-permute-start(f32[8,128]{1,0:T(8,128)S(1)} %get-tuple-element.22.refs_0_), channel_id=1, source_target_pairs={{0,1},{1,2},{2,3},{3,0},{4,5},{5,6},{6,7},{7,4},{8,9},{9,10},{10,1... | collective-permute-start | bytes 12296 | tf_op jit(solution)/shard_map/ppermute | solution.py:373
  80.1 5.3 %collective-permute-start.5 = (f32[8,128]{1,0:T(8,128)S(1)}, f32[8,128]{1,0:T(8,128)S(1)}, u32[]{:S(2)}, u32[]{:S(2)}) collective-permute-start(f32[8,128]{1,0:T(8,128)S(1)} %get-tuple-element.22.refs_0_), channel_id=1, source_target_pairs={{0,2},{1,3},{2,0},{3,1},{4,6},{5,7},{6,4},{7,5},{8,10},{9,11},{10,... | collective-permute-start | bytes 12296 | tf_op jit(solution)/shard_map/ppermute | solution.py:373
  83.7 3.6 %collective-permute-start.6 = (f32[8,128]{1,0:T(8,128)S(1)}, f32[8,128]{1,0:T(8,128)S(1)}, u32[]{:S(2)}, u32[]{:S(2)}) collective-permute-start(f32[8,128]{1,0:T(8,128)S(1)} %get-tuple-element.22.refs_0_), channel_id=1, source_target_pairs={{0,3},{1,0},{2,1},{3,2},{4,7},{5,4},{6,5},{7,6},{8,11},{9,8},{10,9... | collective-permute-start | bytes 12296 | tf_op jit(solution)/shard_map/ppermute | solution.py:373

commit v7 on v6

--- a/solution.py
+++ b/solution.py
@@ -45,7 +45,7 @@
     return pltpu.with_memory_space_constraint(x, pltpu.HBM)
 
 
-def pack_kernel(sources_ref, key_ref, value_ref, out_ref, rows_ref, packed_ref, in_sems, out_sems):
+def pack_kernel(sources_ref, key_ref, value_ref, out_ref, rows_ref, packed_ref, listed_ref, in_sems, out_sems, listed_sem):
     heads = key_ref.shape[1] // HEAD_DIM
 
     def into(kv, seg):
@@ -57,13 +57,16 @@
         at = pl.ds(seg * HALF, HALF + TAIL if seg == SEG_DEV - 1 else HALF)
         return pltpu.make_async_copy(packed_ref.at[:, at, :], out_ref.at[:, at, :], out_sems.at[seg])
 
+    listing = pltpu.make_async_copy(sources_ref, listed_ref, listed_sem)
+    listing.start()
     for seg in range(SEG_DEV):
         for kv in range(2):
             into(kv, seg).start()
+    listing.wait()
     lane = lax.broadcasted_iota(jnp.int32, (TAIL, HEAD_DIM), 1)
     tail = jnp.zeros((TAIL, HEAD_DIM), F32)
     for i in range(SEG_DEV * NEIGHBOURS):
-        named = sources_ref[i % NEIGHBOURS, i // NEIGHBOURS].astype(F32)
+        named = listed_ref[i % NEIGHBOURS, i // NEIGHBOURS].astype(F32)
         tail = jnp.where(lane == i, named, tail)
     tail = tail.astype(BF16)
     for stripe in range(4 * heads):
@@ -89,13 +92,15 @@
     return pl.pallas_call(
         pack_kernel,
         out_shape=jax.ShapeDtypeStruct(shape, BF16),
-        in_specs=[pl.BlockSpec(memory_space=pltpu.SMEM), hbm, hbm],
+        in_specs=[hbm, hbm, hbm],
         out_specs=hbm,
         scratch_shapes=[
             pltpu.VMEM((2, rows, columns), BF16),
             pltpu.VMEM(shape, BF16),
+            pltpu.SMEM((NEIGHBOURS, SEG_DEV), jnp.int32),
             pltpu.SemaphoreType.DMA((2, SEG_DEV)),
             pltpu.SemaphoreType.DMA((SEG_DEV,)),
+            pltpu.SemaphoreType.DMA,
         ],
         compiler_params=params(PACK_MIB),
         cost_estimate=cost(1000000, 2 * 2 * segment_key.size * 2),
@@ -104,7 +109,8 @@
 
 
 def pick_kernel(named_ref, table_ref, out_ref, picked_ref, sems):
-    devices = table_ref.shape[0]
+    devices, long, _ = table_ref.shape
+    rows_ref = table_ref.reshape(devices * long, HEAD_DIM)
     groups = sems.shape[0]
     here = devices // groups
     count = SEG_DEV * NEIGHBOURS
@@ -122,10 +128,8 @@
                     named = named_ref[behind, count - NEIGHBOURS + i]
                 else:
                     named = named_ref[device, i - NEIGHBOURS]
-                owner = lax.shift_right_logical(named, 2)
-                within = lax.bitwise_and(named, SEG_DEV - 1)
-                start = pl.multiple_of(within * HALF, HALF)
-                picked_ref[device, i * HALF:(i + 1) * HALF, :] = table_ref[owner, pl.ds(start, HALF), :]
+                start = pl.multiple_of(named * HALF + lax.shift_right_logical(named, 2) * TAIL, TAIL)
+                picked_ref[device, i * HALF:(i + 1) * HALF, :] = rows_ref[pl.ds(start, HALF), :]
         out_of(group).start()
         return carry
 
@@ -258,8 +262,9 @@
     for seg in range(1, SEG_DEV):
         into(seg).start()
     for seg in range(SEG_DEV):
-        if seg > 0:
-            into(seg).wait()
+        if seg == 1:
+            for behind in range(1, SEG_DEV):
+                into(behind).wait()
         each = [(seg * NEIGHBOURS + i, h) for i in range(NEIGHBOURS) for h in range(heads)]
 
         def own(n, h):
@@ -311,11 +316,11 @@
     )(came, in_hbm(rest), got, *parts)
 
 
-def decode_kernel(full_width, place_ref, query_ref, prior_ref, *refs):
+def decode_kernel(full_width, query_ref, prior_ref, *refs):
     parts, (out_ref, out_rows, sems) = refs[:-3], refs[-3:]
     panel = NEIGHBOURS * NBR_LEN
     heads = query_ref.shape[1] // HEAD_DIM
-    empty = place_ref[0] == 0
+    empty = lax.axis_index("span") == 0
 
     def out_of(group):
         at = pl.ds(group * AT_ONCE * SEG_LEN, AT_ONCE * SEG_LEN)
@@ -350,12 +355,12 @@
         out_of(group).wait()
 
 
-def decode(place, query, prior, parts, full_width):
+def decode(query, prior, parts, full_width):
     vmem = pl.BlockSpec(memory_space=pltpu.VMEM)
     return pl.pallas_call(
         functools.partial(decode_kernel, full_width),
         out_shape=jax.ShapeDtypeStruct(query.shape, BF16),
-        in_specs=[pl.BlockSpec(memory_space=pltpu.SMEM), vmem, vmem] + [vmem] * len(parts),
+        in_specs=[vmem, vmem] + [vmem] * len(parts),
         out_specs=pl.BlockSpec(memory_space=pl.ANY),
         scratch_shapes=[
             pltpu.VMEM(query.shape, BF16),
@@ -364,14 +369,14 @@
         compiler_params=params(SMALL_MIB),
         cost_estimate=cost(4000000000, 4 * query.size + 2 * prior.size, query.size * 2),
         name="decode",
-    )(place, query, prior, *parts)
+    )(query, prior, *parts)
 
 
 def over_heads(part):
     heads = lax.axis_size("head")
     return [part] + [
         lax.ppermute(part, "head", [(i, (i + step) % heads) for i in range(heads)])
-        for step in range(1, heads)
+        for step in (1, 3, 2)
     ]
 
 
@@ -396,8 +401,6 @@
     columns = neighbour_query.shape[1]
     full_width = columns * lax.axis_size("head")
     per_device = SEG_DEV * NEIGHBOURS
-    place = lax.axis_index("span").astype(jnp.int32).reshape(1)
-    sources, place = lax.optimization_barrier((sources, place))
     table = exchange(pack(sources, segment_key, segment_value))
     rest, panel, rest_squares = self_attention(neighbour_query, neighbour_key, neighbour_value)
     came = from_behind(panel)
@@ -406,7 +409,7 @@
     got = exchange(pick(named, table))
     parts = over_heads(squares_above(came, rest_squares))
     encoded, squares = cross_attention(came, rest, got, parts, full_width)
-    return decode(place, decoder_query, encoded, over_heads(squares), full_width)
+    return decode(decoder_query, encoded, over_heads(squares), full_width)
 
 
 def solution(mesh):

time: 90.2 us -> 91 us (level)
  waiting for transfers between devices: 42.5 us -> 44.6 us
    ppermute x6, waiting for transfers between devices: 5.74 us -> 7.86 us  [over_heads(): lax.ppermute(part, 'head', [(i, (i + step) % heads) for i in range(heads)])]
    ppermute x6, starting transfers between devices: 10.8 us -> 9.85 us  [over_heads(): lax.ppermute(part, 'head', [(i, (i + step) % heads) for i in range(heads)])]
  transfers between devices with their start and end apart: 9 -> 9, of which waited for: 7 -> 5; matrix products, arithmetic and copies ran while one was open for 0% -> 0% of each run, Pallas kernels for 10% -> 10%
where the time goes in v7:
time: 91 us; the launch traced here: 90.5 us
  waiting for transfers between devices  44.6 us (49%)
  starting transfers between devices  25.6 us (28%)
  Pallas kernels  20.2 us (22%)
    ppermute x1, waiting for transfers between devices, from_behind(): return lax.ppermute(part, 'span', [(i, i + 1) for i in range(devices - 1)])  30.1 us
    all_to_all x2, starting transfers between devices, exchange(): return lax.all_to_all(x, 'span', split_axis=0, concat_axis=0, tiled=True)  13.7 us
    ppermute x6, starting transfers between devices, over_heads(): lax.ppermute(part, 'head', [(i, (i + step) % heads) for i in range(heads)])  9.85 us
    pallas_call x1, Pallas kernels, self_attention(): pl.pallas_call(self_kernel, grid=(count,), out_shape=(pltpu.HBM((last * N...  9.04 us
    ppermute x6, waiting for transfers between devices, over_heads(): lax.ppermute(part, 'head', [(i, (i + step) % heads) for i in range(heads)])  7.86 us
    all_to_all x2, waiting for transfers between devices, exchange(): return lax.all_to_all(x, 'span', split_axis=0, concat_axis=0, tiled=True)  6.67 us
    pallas_call x1, Pallas kernels, cross_attention(): pl.pallas_call(functools.partial(cross_kernel, full_width), out_shape=(ja...  4.07 us
    pallas_call x1, Pallas kernels, decode(): pl.pallas_call(functools.partial(decode_kernel, full_width), out_shape=ja...  2.35 us
  transfers between devices with their start and end apart: 9, of which 5 were waited for; matrix products, arithmetic and copies ran while one was open for 0% of the time, Pallas kernels for 10%

profile of v7, /device:TPU:24, one launch (start us, length us, event | category | flops | bytes accessed | tf_op | source)
XLA Modules:
  0.0 90.5 jit_solution(2646277344930284041)
XLA Ops:
  0.0 2.2 %pack_stripes.1 = bf16[32,136,128]{2,1,0:T(8,128)(2,1)} custom-call(s32[2,4]{1,0:T(2,128)} %bitcast.3, bf16[256,1024]{1,0:T(8,128)(2,1)} %key_ref.3, bf16[256,1024]{1,0:T(8,128)(2,1)} %value_ref.3), custom_call_target="tpu_custom_call" | custom-call | flops 1000000 | bytes 2097152 | tf_op jit(solution)/shard_map/pack_stripes/pallas_call | solution.py:92
  2.2 7.4 %all-to-all-start = ((bf16[32,136,128]{2,1,0:T(8,128)(2,1)}), bf16[32,136,128]{2,1,0:T(8,128)(2,1)S(1)}, u32[]{:S(2)}, u32[]{:S(2)}) async-start(bf16[32,136,128]{2,1,0:T(8,128)(2,1)} %pack_stripes.1), calls=%async_computation | async-start | bytes 2228224 | tf_op jit(solution)/shard_map/all_to_all | solution.py:389
  9.6 9.0 %self_attention.1 = (bf16[768,1024]{1,0:T(8,128)(2,1)}, bf16[256,1024]{1,0:T(8,128)(2,1)}, f32[6,128]{1,0:T(8,128)S(1)}) custom-call(bf16[1024,1024]{1,0:T(8,128)(2,1)} %query_ref.2, bf16[1024,1024]{1,0:T(8,128)(2,1)} %key_ref.2, bf16[1024,1024]{1,0:T(8,128)(2,1)} %value_ref.2), custom_call_target="tpu_custom_call" | custom-call | flops 8000000000 | bytes 8388608 | tf_op jit(solution)/shard_map/self_attention/pallas_call | solution.py:205
  18.6 6.7 %all-to-all-done.table_ref = bf16[32,136,128]{2,1,0:T(8,128)(2,1)S(1)} async-done(((bf16[32,136,128]{2,1,0:T(8,128)(2,1)}), bf16[32,136,128]{2,1,0:T(8,128)(2,1)S(1)}, u32[]{:S(2)}, u32[]{:S(2)}) %all-to-all-start) | async-done | bytes 1114144 | tf_op jit(solution)/shard_map/all_to_all | solution.py:389
  25.3 2.3 %pick_stripes.1 = bf16[32,256,128]{2,1,0:T(8,128)(2,1)} custom-call(s32[32,8]{1,0:T(8,128)S(1)} %bitcast.2, bf16[32,136,128]{2,1,0:T(8,128)(2,1)S(1)} %all-to-all-done.table_ref), custom_call_target="tpu_custom_call" | custom-call | flops 1000000 | bytes 3211264 | tf_op jit(solution)/shard_map/pick_stripes/pallas_call | solution.py:145
  27.6 0.0 copy-start.1
  27.6 6.4 %all-to-all-start.1 = ((bf16[32,256,128]{2,1,0:T(8,128)(2,1)}), bf16[32,256,128]{2,1,0:T(8,128)(2,1)S(1)}, u32[]{:S(2)}, u32[]{:S(2)}) async-start(bf16[32,256,128]{2,1,0:T(8,128)(2,1)} %pick_stripes.1), calls=%async_computation.1 | async-start | bytes 4194304 | tf_op jit(solution)/shard_map/all_to_all | solution.py:389
  34.0 0.0 copy-done.1
  34.0 2.0 %collective-permute-start = (bf16[256,1024]{1,0:T(8,128)(2,1)S(1)}, bf16[256,1024]{1,0:T(8,128)(2,1)S(1)}, u32[]{:S(2)}, u32[]{:S(2)}) collective-permute-start(bf16[256,1024]{1,0:T(8,128)(2,1)S(1)} %copy-done.1), channel_id=1, source_target_pairs={{0,4},{4,8},{8,12},{12,16},{16,20},{20,24},{24,28},{28,32},{32,36}... | collective-permute-start | bytes 1572872 | tf_op jit(solution)/shard_map/ppermute | solution.py:385
  36.1 30.1 %collective-permute-done.rows_ref.came_ref = bf16[256,1024]{1,0:T(8,128)(2,1)S(1)} collective-permute-done((bf16[256,1024]{1,0:T(8,128)(2,1)S(1)}, bf16[256,1024]{1,0:T(8,128)(2,1)S(1)}, u32[]{:S(2)}, u32[]{:S(2)}) %collective-permute-start) | collective-permute-done | bytes 524320 | tf_op jit(solution)/shard_map/ppermute | solution.py:385
  66.1 0.2 row_squares.1.refs_0_
  66.3 2.0 %collective-permute-start.1 = (f32[8,128]{1,0:T(8,128)S(1)}, f32[8,128]{1,0:T(8,128)S(1)}, u32[]{:S(2)}, u32[]{:S(2)}) collective-permute-start(f32[8,128]{1,0:T(8,128)S(1)} %row_squares.1.refs_0_), channel_id=1, source_target_pairs={{0,1},{1,2},{2,3},{3,0},{4,5},{5,6},{6,7},{7,4},{8,9},{9,10},{10,1... | collective-permute-start | bytes 12296 | tf_op jit(solution)/shard_map/ppermute | solution.py:378
  68.3 2.2 %collective-permute-start.2 = (f32[8,128]{1,0:T(8,128)S(1)}, f32[8,128]{1,0:T(8,128)S(1)}, u32[]{:S(2)}, u32[]{:S(2)}) collective-permute-start(f32[8,128]{1,0:T(8,128)S(1)} %row_squares.1.refs_0_), channel_id=1, source_target_pairs={{0,3},{1,0},{2,1},{3,2},{4,7},{5,4},{6,5},{7,6},{8,11},{9,8},{10,9... | collective-permute-start | bytes 12296 | tf_op jit(solution)/shard_map/ppermute | solution.py:378
  70.5 1.8 %collective-permute-start.3 = (f32[8,128]{1,0:T(8,128)S(1)}, f32[8,128]{1,0:T(8,128)S(1)}, u32[]{:S(2)}, u32[]{:S(2)}) collective-permute-start(f32[8,128]{1,0:T(8,128)S(1)} %row_squares.1.refs_0_), channel_id=1, source_target_pairs={{0,2},{1,3},{2,0},{3,1},{4,6},{5,7},{6,4},{7,5},{8,10},{9,11},{10,... | collective-permute-start | bytes 12296 | tf_op jit(solution)/shard_map/ppermute | solution.py:378
  72.3 0.0 collective-permute-done.1.refs_1_
  72.3 0.0 collective-permute-done.2.refs_2_
  72.3 3.3 %collective-permute-done.3.refs_3_ = f32[8,128]{1,0:T(8,128)S(1)} collective-permute-done((f32[8,128]{1,0:T(8,128)S(1)}, f32[8,128]{1,0:T(8,128)S(1)}, u32[]{:S(2)}, u32[]{:S(2)}) %collective-permute-start.3) | collective-permute-done | bytes 4128 | tf_op jit(solution)/shard_map/ppermute | solution.py:378
  75.6 0.0 all-to-all-done.1.got_ref
  75.6 0.0 copy-start
  75.6 4.1 %cross_attention.1 = (bf16[1024,1024]{1,0:T(8,128)(2,1)S(1)}, f32[8,128]{1,0:T(8,128)S(1)}) custom-call(bf16[256,1024]{1,0:T(8,128)(2,1)S(1)} %collective-permute-done.rows_ref.came_ref, bf16[768,1024]{1,0:T(8,128)(2,1)} %get-tuple-element.13.rest_ref, bf16[32,256,128]{2,1,0:T(8,128)(2,1)S(1)} %all-to-all-done.1.got_ref, f32[8,128]{1,0:T(8,128)S(1)} %row_squares.1.refs_0_, ...), custom_call_target="tpu_custom_call" | custom-call | flops 8000000000 | bytes 6291456 | tf_op jit(solution)/shard_map/cross_attention/pallas_call | solution.py:304
  79.7 0.1 collective-permute-start.4
  79.8 3.2 %collective-permute-start.5 = (f32[8,128]{1,0:T(8,128)S(1)}, f32[8,128]{1,0:T(8,128)S(1)}, u32[]{:S(2)}, u32[]{:S(2)}) collective-permute-start(f32[8,128]{1,0:T(8,128)S(1)} %get-tuple-element.18.refs_0_), channel_id=1, source_target_pairs={{0,3},{1,0},{2,1},{3,2},{4,7},{5,4},{6,5},{7,6},{8,11},{9,8},{10,9... | collective-permute-start | bytes 12296 | tf_op jit(solution)/shard_map/ppermute | solution.py:378
  83.0 0.6 collective-permute-start.6
  83.6 1.0 %collective-permute-done.4.refs_1_ = f32[8,128]{1,0:T(8,128)S(1)} collective-permute-done((f32[8,128]{1,0:T(8,128)S(1)}, f32[8,128]{1,0:T(8,128)S(1)}, u32[]{:S(2)}, u32[]{:S(2)}) %collective-permute-start.4) | collective-permute-done | bytes 4128 | tf_op jit(solution)/shard_map/ppermute | solution.py:378
  84.6 0.0 collective-permute-done.5.refs_2_
  84.6 3.5 %collective-permute-done.6.refs_3_ = f32[8,128]{1,0:T(8,128)S(1)} collective-permute-done((f32[8,128]{1,0:T(8,128)S(1)}, f32[8,128]{1,0:T(8,128)S(1)}, u32[]{:S(2)}, u32[]{:S(2)}) %collective-permute-start.6) | collective-permute-done | bytes 4128 | tf_op jit(solution)/shard_map/ppermute | solution.py:378
  88.1 0.0 copy-done
  88.1 2.3 %decode.1 = bf16[256,1024]{1,0:T(8,128)(2,1)} custom-call(bf16[256,1024]{1,0:T(8,128)(2,1)S(1)} %copy-done, bf16[1024,1024]{1,0:T(8,128)(2,1)S(1)} %get-tuple-element.17.prior_ref, f32[8,128]{1,0:T(8,128)S(1)} %get-tuple-element.18.refs_0_, f32[8,128]{1,0:T(8,128)S(1)} %collective-permute-done.4.refs_1_, f32[8,128]{1,0:T(8,128)S(1)} %collective-permute-done.5.refs_2_, ...), custom_call_target="tpu_custom_call" | custom-call | flops 4000000000 | bytes 3145728 | tf_op jit(solution)/shard_map/decode/pallas_call | solution.py:360
  (1 shorter events, 0.0 us)
Async XLA Ops:
  2.2 23.1 %all-to-all-start = ((bf16[32,136,128]{2,1,0:T(8,128)(2,1)}), bf16[32,136,128]{2,1,0:T(8,128)(2,1)S(1)}, u32[]{:S(2)}, u32[]{:S(2)}) async-start(bf16[32,136,128]{2,1,0:T(8,128)(2,1)} %pack_stripes.1), calls=%async_computation | async-start | bytes 2228224 | tf_op jit(solution)/shard_map/all_to_all | solution.py:389
  27.6 6.4 %copy-start.1 = (bf16[256,1024]{1,0:T(8,128)(2,1)S(1)}, bf16[256,1024]{1,0:T(8,128)(2,1)}, u32[]{:S(2)}) copy-start(bf16[256,1024]{1,0:T(8,128)(2,1)} %get-tuple-element.12) | copy-start | bytes 1572868
  27.6 48.0 %all-to-all-start.1 = ((bf16[32,256,128]{2,1,0:T(8,128)(2,1)}), bf16[32,256,128]{2,1,0:T(8,128)(2,1)S(1)}, u32[]{:S(2)}, u32[]{:S(2)}) async-start(bf16[32,256,128]{2,1,0:T(8,128)(2,1)} %pick_stripes.1), calls=%async_computation.1 | async-start | bytes 4194304 | tf_op jit(solution)/shard_map/all_to_all | solution.py:389
  34.0 32.1 %collective-permute-start = (bf16[256,1024]{1,0:T(8,128)(2,1)S(1)}, bf16[256,1024]{1,0:T(8,128)(2,1)S(1)}, u32[]{:S(2)}, u32[]{:S(2)}) collective-permute-start(bf16[256,1024]{1,0:T(8,128)(2,1)S(1)} %copy-done.1), channel_id=1, source_target_pairs={{0,4},{4,8},{8,12},{12,16},{16,20},{20,24},{24,28},{28,32},{32,36}... | collective-permute-start | bytes 1572872 | tf_op jit(solution)/shard_map/ppermute | solution.py:385
  66.3 6.0 %collective-permute-start.1 = (f32[8,128]{1,0:T(8,128)S(1)}, f32[8,128]{1,0:T(8,128)S(1)}, u32[]{:S(2)}, u32[]{:S(2)}) collective-permute-start(f32[8,128]{1,0:T(8,128)S(1)} %row_squares.1.refs_0_), channel_id=1, source_target_pairs={{0,1},{1,2},{2,3},{3,0},{4,5},{5,6},{6,7},{7,4},{8,9},{9,10},{10,1... | collective-permute-start | bytes 12296 | tf_op jit(solution)/shard_map/ppermute | solution.py:378
  68.3 4.0 %collective-permute-start.2 = (f32[8,128]{1,0:T(8,128)S(1)}, f32[8,128]{1,0:T(8,128)S(1)}, u32[]{:S(2)}, u32[]{:S(2)}) collective-permute-start(f32[8,128]{1,0:T(8,128)S(1)} %row_squares.1.refs_0_), channel_id=1, source_target_pairs={{0,3},{1,0},{2,1},{3,2},{4,7},{5,4},{6,5},{7,6},{8,11},{9,8},{10,9... | collective-permute-start | bytes 12296 | tf_op jit(solution)/shard_map/ppermute | solution.py:378
  70.5 5.1 %collective-permute-start.3 = (f32[8,128]{1,0:T(8,128)S(1)}, f32[8,128]{1,0:T(8,128)S(1)}, u32[]{:S(2)}, u32[]{:S(2)}) collective-permute-start(f32[8,128]{1,0:T(8,128)S(1)} %row_squares.1.refs_0_), channel_id=1, source_target_pairs={{0,2},{1,3},{2,0},{3,1},{4,6},{5,7},{6,4},{7,5},{8,10},{9,11},{10,... | collective-permute-start | bytes 12296 | tf_op jit(solution)/shard_map/ppermute | solution.py:378
  75.6 12.5 %copy-start = (bf16[256,1024]{1,0:T(8,128)(2,1)S(1)}, bf16[256,1024]{1,0:T(8,128)(2,1)}, u32[]{:S(2)}) copy-start(bf16[256,1024]{1,0:T(8,128)(2,1)} %query_ref.3) | copy-start | bytes 1572868
  79.7 4.9 %collective-permute-start.4 = (f32[8,128]{1,0:T(8,128)S(1)}, f32[8,128]{1,0:T(8,128)S(1)}, u32[]{:S(2)}, u32[]{:S(2)}) collective-permute-start(f32[8,128]{1,0:T(8,128)S(1)} %get-tuple-element.18.refs_0_), channel_id=1, source_target_pairs={{0,1},{1,2},{2,3},{3,0},{4,5},{5,6},{6,7},{7,4},{8,9},{9,10},{10,1... | collective-permute-start | bytes 12296 | tf_op jit(solution)/shard_map/ppermute | solution.py:378
  79.8 4.8 %collective-permute-start.5 = (f32[8,128]{1,0:T(8,128)S(1)}, f32[8,128]{1,0:T(8,128)S(1)}, u32[]{:S(2)}, u32[]{:S(2)}) collective-permute-start(f32[8,128]{1,0:T(8,128)S(1)} %get-tuple-element.18.refs_0_), channel_id=1, source_target_pairs={{0,3},{1,0},{2,1},{3,2},{4,7},{5,4},{6,5},{7,6},{8,11},{9,8},{10,9... | collective-permute-start | bytes 12296 | tf_op jit(solution)/shard_map/ppermute | solution.py:378
  83.0 5.1 %collective-permute-start.6 = (f32[8,128]{1,0:T(8,128)S(1)}, f32[8,128]{1,0:T(8,128)S(1)}, u32[]{:S(2)}, u32[]{:S(2)}) collective-permute-start(f32[8,128]{1,0:T(8,128)S(1)} %get-tuple-element.18.refs_0_), channel_id=1, source_target_pairs={{0,2},{1,3},{2,0},{3,1},{4,6},{5,7},{6,4},{7,5},{8,10},{9,11},{10,... | collective-permute-start | bytes 12296 | tf_op jit(solution)/shard_map/ppermute | solution.py:378
